TPU v7x, 16 devices: a whole 2x2x2 slice. The times are simulated.
16 devices in a mesh: fsdp: 16 (over z, y, x, core).
Axes of the slice: x: 2, y: 2, z: 2, core: 2. Of those that a mesh axis runs over, the one named last changes fastest.
Arguments:
- x: bfloat16 [32, 1024, 1024], P('fsdp')
- lengths: int32 [32], P('fsdp')
- d_y: bfloat16 [32, 1024, 1024], P('fsdp')
- w_attn: bfloat16 [2, 4, 1024, 1024], P(None, None, 'fsdp')
- b_attn: bfloat16 [2, 4, 1024], P(None, None, 'fsdp')
- ln_par: bfloat16 [2, 4, 1024], P(None, None, 'fsdp')
- w_up: bfloat16 [2, 1024, 4096], P(None, 'fsdp')
- b_up: bfloat16 [2, 4096], P(None, 'fsdp')
- w_down: bfloat16 [2, 4096, 1024], P(None, 'fsdp')
- b_down: bfloat16 [2, 1024], P(None, 'fsdp')
Outputs:
- output 1: bfloat16 [32, 1024, 1024], P('fsdp')
- output 2: float32 [2, 4, 1024, 1024], P(None, None, 'fsdp')
- output 3: float32 [2, 4, 1024], P(None, None, 'fsdp')
- output 4: float32 [2, 4, 1024], P(None, None, 'fsdp')
- output 5: float32 [2, 1024, 4096], P(None, 'fsdp')
- output 6: float32 [2, 4096], P(None, 'fsdp')
- output 7: float32 [2, 4096, 1024], P(None, 'fsdp')
- output 8: float32 [2, 1024], P(None, 'fsdp')
All inputs are finite; a program needn't handle non-finite values.
Results may differ from a plain program's by a relative error of at most 0.013046.
Values are sent between devices in bfloat16 or wider.
A program may use at most 1 GiB of HBM per device.

v0:
```python
import math
import functools
import jax
import jax.numpy as jnp
from jax import lax
from jax.sharding import PartitionSpec as P

HEAD_DIM = 64
EPS = 1e-5
THETA = 10000.0
NEG_BIG = -1e30


def rotary_tables(seq_len):
    half_dim = HEAD_DIM // 2
    inv_freq = 1.0 / (THETA ** (jnp.arange(half_dim, dtype=jnp.float32) * (2.0 / HEAD_DIM)))
    angles = jnp.arange(seq_len, dtype=jnp.float32)[:, None] * inv_freq[None, :]
    return jnp.cos(angles)[:, None, :], jnp.sin(angles)[:, None, :]


def rotate(tensor, cos_tab, sin_tab):
    half_dim = HEAD_DIM // 2
    first_half = tensor[..., :half_dim]
    second_half = tensor[..., half_dim:]
    return jnp.concatenate([first_half * cos_tab - second_half * sin_tab, second_half * cos_tab + first_half * sin_tab], axis=-1)


def rotate_back(tensor, cos_tab, sin_tab):
    half_dim = HEAD_DIM // 2
    first_half = tensor[..., :half_dim]
    second_half = tensor[..., half_dim:]
    return jnp.concatenate([first_half * cos_tab + second_half * sin_tab, second_half * cos_tab - first_half * sin_tab], axis=-1)


def norm_fwd(x_in, gain, shift):
    row_mean = jnp.mean(x_in, axis=-1, keepdims=True)
    centered = x_in - row_mean
    variance = jnp.mean(centered * centered, axis=-1, keepdims=True)
    return centered * lax.rsqrt(variance + EPS) * gain + shift


def gelu_slope(pre_act):
    normal_cdf = 0.5 * (1.0 + lax.erf(pre_act * (1.0 / math.sqrt(2.0))))
    density = jnp.exp(-0.5 * pre_act * pre_act) * (1.0 / math.sqrt(2.0 * math.pi))
    return normal_cdf + pre_act * density


def layer_forward(x, weights, lengths, tables):
    w_attn, b_attn, ln_par, w_up, b_up, w_down, b_down = weights
    cos_tab, sin_tab = tables
    num_seq, seq_len, model_dim = x.shape
    num_heads = model_dim // HEAD_DIM
    x_f32 = x.astype(jnp.float32)
    h_one = norm_fwd(x_f32, ln_par[0].astype(jnp.float32), ln_par[1].astype(jnp.float32)).astype(jnp.bfloat16)
    projected = jnp.einsum('bld,kde->kble', h_one, w_attn[:3], preferred_element_type=jnp.float32)
    projected = (projected + b_attn[:3, None, None, :].astype(jnp.float32)).reshape(3, num_seq, seq_len, num_heads, HEAD_DIM)
    query_rot = rotate(projected[0] * (HEAD_DIM ** -0.5), cos_tab, sin_tab).astype(jnp.bfloat16)
    key_rot = rotate(projected[1], cos_tab, sin_tab).astype(jnp.bfloat16)
    values = projected[2].astype(jnp.bfloat16)
    scores = jnp.einsum('bqhd,bkhd->bhqk', query_rot, key_rot, preferred_element_type=jnp.float32)
    key_valid = jnp.arange(seq_len)[None, None, None, :] < lengths[:, None, None, None]
    probs_bf = jax.nn.softmax(jnp.where(key_valid, scores, NEG_BIG), axis=-1).astype(jnp.bfloat16)
    context = jnp.einsum('bhqk,bkhd->bqhd', probs_bf, values, preferred_element_type=jnp.float32)
    context = context.astype(jnp.bfloat16).reshape(num_seq, seq_len, model_dim)
    attn_out = jnp.einsum('bld,de->ble', context, w_attn[3], preferred_element_type=jnp.float32)
    x_mid = (x_f32 + attn_out + b_attn[3].astype(jnp.float32)).astype(jnp.bfloat16)
    mid_f32 = x_mid.astype(jnp.float32)
    h_two = norm_fwd(mid_f32, ln_par[2].astype(jnp.float32), ln_par[3].astype(jnp.float32)).astype(jnp.bfloat16)
    pre_act = jnp.einsum('bld,df->blf', h_two, w_up, preferred_element_type=jnp.float32) + b_up.astype(jnp.float32)
    act_bf = jax.nn.gelu(pre_act, approximate=False).astype(jnp.bfloat16)
    mlp_out = jnp.einsum('blf,fd->bld', act_bf, w_down, preferred_element_type=jnp.float32)
    y_out = (mid_f32 + mlp_out + b_down.astype(jnp.float32)).astype(jnp.bfloat16)
    saved_acts = (x, h_one, query_rot, key_rot, values, probs_bf, context, x_mid, h_two, pre_act, act_bf)
    return y_out, saved_acts


def layer_backward(d_out, saved_acts, weights, tables):
    w_attn, ln_par, w_up, w_down = weights[0], weights[2], weights[3], weights[5]
    cos_tab, sin_tab = tables
    x, h_one, query_rot, key_rot, values, probs_bf, context, x_mid, h_two, pre_act, act_bf = saved_acts
    num_seq, seq_len, model_dim = x.shape
    num_heads = model_dim // HEAD_DIM
    gb_down = jnp.sum(d_out, axis=(0, 1), dtype=jnp.float32)
    gw_down = jnp.einsum('blf,bld->fd', act_bf, d_out, preferred_element_type=jnp.float32)
    d_act = jnp.einsum('bld,fd->blf', d_out, w_down, preferred_element_type=jnp.float32)
    d_pre = d_act * gelu_slope(pre_act)
    gb_up = jnp.sum(d_pre, axis=(0, 1))
    d_pre_bf = d_pre.astype(jnp.bfloat16)
    gw_up = jnp.einsum('bld,blf->df', h_two, d_pre_bf, preferred_element_type=jnp.float32)
    d_h_two = jnp.einsum('blf,df->bld', d_pre_bf, w_up, preferred_element_type=jnp.float32)
    _, norm_pull_two = jax.vjp(norm_fwd, x_mid.astype(jnp.float32), ln_par[2].astype(jnp.float32), ln_par[3].astype(jnp.float32))
    d_mid_norm, g_gain_two, g_shift_two = norm_pull_two(d_h_two)
    d_mid = (d_out.astype(jnp.float32) + d_mid_norm).astype(jnp.bfloat16)
    gb_out = jnp.sum(d_mid, axis=(0, 1), dtype=jnp.float32)
    gw_out = jnp.einsum('bld,ble->de', context, d_mid, preferred_element_type=jnp.float32)
    d_context = jnp.einsum('ble,de->bld', d_mid, w_attn[3], preferred_element_type=jnp.float32)
    d_context = d_context.astype(jnp.bfloat16).reshape(num_seq, seq_len, num_heads, HEAD_DIM)
    d_probs = jnp.einsum('bqhd,bkhd->bhqk', d_context, values, preferred_element_type=jnp.float32)
    d_values = jnp.einsum('bhqk,bqhd->bkhd', probs_bf, d_context, preferred_element_type=jnp.float32)
    probs_f32 = probs_bf.astype(jnp.float32)
    d_scores = (probs_f32 * (d_probs - jnp.sum(d_probs * probs_f32, axis=-1, keepdims=True))).astype(jnp.bfloat16)
    d_query = jnp.einsum('bhqk,bkhd->bqhd', d_scores, key_rot, preferred_element_type=jnp.float32)
    d_key = jnp.einsum('bhqk,bqhd->bkhd', d_scores, query_rot, preferred_element_type=jnp.float32)
    d_proj = jnp.stack([
        (rotate_back(d_query, cos_tab, sin_tab) * (HEAD_DIM ** -0.5)).astype(jnp.bfloat16),
        rotate_back(d_key, cos_tab, sin_tab).astype(jnp.bfloat16),
        d_values.astype(jnp.bfloat16)]).reshape(3, num_seq, seq_len, model_dim)
    gb_qkv = jnp.sum(d_proj, axis=(1, 2), dtype=jnp.float32)
    gw_qkv = jnp.einsum('bld,kble->kde', h_one, d_proj, preferred_element_type=jnp.float32)
    d_h_one = jnp.einsum('kble,kde->bld', d_proj, w_attn[:3], preferred_element_type=jnp.float32)
    _, norm_pull_one = jax.vjp(norm_fwd, x.astype(jnp.float32), ln_par[0].astype(jnp.float32), ln_par[1].astype(jnp.float32))
    d_x_norm, g_gain_one, g_shift_one = norm_pull_one(d_h_one)
    d_x = (d_mid.astype(jnp.float32) + d_x_norm).astype(jnp.bfloat16)
    gb_attn = jnp.concatenate([gb_qkv, gb_out[None]], axis=0)
    g_ln = jnp.stack([g_gain_one, g_shift_one, g_gain_two, g_shift_two])
    return d_x, (gw_qkv, gw_out, gb_attn, g_ln, gw_up, gb_up, gw_down, gb_down)


def gather_layer(layer_shards, axis_name):
    w_attn, b_attn, ln_par, w_up, b_up, w_down, b_down = layer_shards
    return (lax.all_gather(w_attn, axis_name, axis=1, tiled=True),
            lax.all_gather(b_attn, axis_name, axis=1, tiled=True),
            lax.all_gather(ln_par, axis_name, axis=1, tiled=True),
            lax.all_gather(w_up, axis_name, axis=0, tiled=True),
            lax.all_gather(b_up, axis_name, axis=0, tiled=True),
            lax.all_gather(w_down, axis_name, axis=0, tiled=True),
            lax.all_gather(b_down, axis_name, axis=0, tiled=True))


def scatter_grads(layer_grads, axis_name):
    gw_qkv, gw_out, gb_attn, g_ln, gw_up, gb_up, gw_down, gb_down = layer_grads
    reduce_rows = functools.partial(lax.psum_scatter, axis_name=axis_name, tiled=True)
    attn_part = jnp.concatenate([reduce_rows(gw_qkv, scatter_dimension=1), reduce_rows(gw_out, scatter_dimension=0)[None]], axis=0)
    return (attn_part,
            reduce_rows(gb_attn, scatter_dimension=1),
            reduce_rows(g_ln, scatter_dimension=1),
            reduce_rows(gw_up, scatter_dimension=0),
            reduce_rows(gb_up, scatter_dimension=0),
            reduce_rows(gw_down, scatter_dimension=0),
            reduce_rows(gb_down, scatter_dimension=0))


def solution(mesh):
    axis_name = mesh.axis_names[0]
    batch_spec = P(axis_name)
    weight_specs = (P(None, None, axis_name, None), P(None, None, axis_name), P(None, None, axis_name),
                    P(None, axis_name, None), P(None, axis_name), P(None, axis_name, None), P(None, axis_name))

    def device_step(x, lengths, d_y, w_attn, b_attn, ln_par, w_up, b_up, w_down, b_down):
        shards = (w_attn, b_attn, ln_par, w_up, b_up, w_down, b_down)
        num_layers = w_attn.shape[0]
        tables = rotary_tables(x.shape[1])
        hidden = x
        saved_list = []
        for layer_idx in range(num_layers):
            full_wts = gather_layer(tuple(shard[layer_idx] for shard in shards), axis_name)
            hidden, saved_acts = layer_forward(hidden, full_wts, lengths, tables)
            saved_list.append(saved_acts)
        grad_x = d_y
        grads_list = [None] * num_layers
        for layer_idx in reversed(range(num_layers)):
            layer_shards, grad_x = lax.optimization_barrier((tuple(shard[layer_idx] for shard in shards), grad_x))
            full_wts = gather_layer(layer_shards, axis_name)
            grad_x, layer_grads = layer_backward(grad_x, saved_list[layer_idx], full_wts, tables)
            grads_list[layer_idx] = scatter_grads(layer_grads, axis_name)
        stacked = tuple(jnp.stack([grads_list[layer_pos][field_pos] for layer_pos in range(num_layers)]) for field_pos in range(7))
        return (grad_x,) + stacked

    return jax.shard_map(device_step, mesh=mesh,
                         in_specs=(batch_spec, batch_spec, batch_spec) + weight_specs,
                         out_specs=(batch_spec,) + weight_specs,
                         check_vma=False)
```

profile of v0, /device:TPU:0, one launch (start us, length us, event | category | flops | bytes accessed | tf_op | source)
XLA Modules:
  0.0 3114.8 jit_solution(15758606635681820729)
XLA Ops:
  60.5 32.4 %all-reduce = bf16[1024]{0:T(1024)(128)(2,1)S(1)} all-reduce(bf16[1024]{0:T(1024)(128)(2,1)S(1)} %dynamic-update-slice), channel_id=8, replica_groups=mesh['fsdp'=16] {'fsdp'}, use_global_device_ids=true, to_apply=%add | all-reduce | flops 1024 | bytes 4096
  318.6 53.7 %fusion.231 = (f32[2,16,1024]{2,1,0:T(8,128)S(1)}, f32[2,16,1024,1024]{2,3,1,0:T(8,128)}) fusion(pred[2,1024]{1,0:T(4,128)(4,1)S(1)} %iota_compare_fusion, bf16[2,1024,16,32]{1,3,2,0:T(8,128)(2,1)S(1)} %get-tuple-element.130, bf16[2,1024,16,32]{1,3,2,0:T(8,128)(2,1)} %get-tuple-element.131, bf16[2,1024,16,32]{1,3,2,0:T(8,128)(2,1)} %get-tuple-element.107, ...), kind=kOutput, calls=%fused_computation.381 | convolution fusion | flops 4412408832 | bytes 142739456 | tf_op jit(solution)/shard_map/sub | solution.py:62
  372.3 64.3 %divide_convert_fusion.1 = bf16[2,16,1024,1024]{2,3,1,0:T(8,128)(2,1)} fusion(f32[2,16,1024,1024]{2,3,1,0:T(8,128)} %get-tuple-element.147, f32[2,16,1024]{2,1,0:T(8,128)S(1)} %get-tuple-element.146), kind=kLoop, calls=%fused_computation.12 | loop fusion | flops 67108864 | bytes 201457664 | tf_op jit(solution)/shard_map/convert_element_type | solution.py:62
  474.8 43.1 %fusion.127 = (u8[1024,4096]{1,0:T(8,128)(4,1)}, u8[1024,4096]{1,0:T(8,128)(4,1)}, f32[2,1024,4096]{2,1,0:T(8,128)}) fusion(f32[4096]{0:T(1024)S(1)} %bitcast.348, bf16[1,1024,4096]{2,1,0:T(8,128)(2,1)} %all-gather.40.cloned.1.call-done, bf16[2,1024,1024]{1,2,0:T(8,128)(2,1)} %copy-done.6, f32[1024]{0:T(1024)S(1)} %copy-done.85, f32[1024]{0:T(1024)S(1)} %copy-done.83, ...), kind=kOutput, calls=%fused_computation.193 | convolution fusion | flops 17301504000 | bytes 54566912 | tf_op jit(solution)/shard_map/bld,df->blf/dot_general | solution.py:69
  518.0 80.5 %fusion.18 = bf16[2,1024,4096]{2,1,0:T(8,128)(2,1)} fusion(f32[2,1024,4096]{2,1,0:T(8,128)} %get-tuple-element.150, f32[4096]{0:T(1024)S(1)} %bitcast.349, u8[1024,4096]{1,0:T(8,128)(4,1)} %get-tuple-element.63, u8[1024,4096]{1,0:T(8,128)(4,1)} %get-tuple-element.62), kind=kLoop, calls=%fused_computation.28 | loop fusion | flops 595591168 | bytes 58736640 | tf_op jit(solution)/shard_map/convert_element_type | solution.py:70
  692.2 53.6 %fusion.232 = (f32[2,16,1024]{2,1,0:T(8,128)S(1)}, f32[2,16,1024,1024]{2,3,1,0:T(8,128)}) fusion(pred[2,1024]{1,0:T(4,128)(4,1)S(1)} %copy-done.102, bf16[2,1024,16,32]{1,3,2,0:T(8,128)(2,1)S(1)} %get-tuple-element.128, bf16[2,1024,16,32]{1,3,2,0:T(8,128)(2,1)} %get-tuple-element.129, bf16[2,1024,16,32]{1,3,2,0:T(8,128)(2,1)} %get-tuple-element.103, ...), kind=kOutput, calls=%fused_computation.382 | convolution fusion | flops 4412408832 | bytes 142739456 | tf_op jit(solution)/shard_map/sub | solution.py:62
  745.8 64.3 %divide_convert_fusion = bf16[2,16,1024,1024]{2,3,1,0:T(8,128)(2,1)} fusion(f32[2,16,1024,1024]{2,3,1,0:T(8,128)} %get-tuple-element.154, f32[2,16,1024]{2,1,0:T(8,128)S(1)} %get-tuple-element.153), kind=kLoop, calls=%fused_computation.10 | loop fusion | flops 67108864 | bytes 201457664 | tf_op jit(solution)/shard_map/convert_element_type | solution.py:62
  848.7 42.8 %fusion.128 = (u8[1024,4096]{1,0:T(8,128)(4,1)}, u8[1024,4096]{1,0:T(8,128)(4,1)}, f32[2,1024,4096]{2,1,0:T(8,128)}) fusion(f32[4096]{0:T(1024)S(1)} %bitcast.361, bf16[1,1024,4096]{2,1,0:T(8,128)(2,1)} %all-gather.46.cloned.1.call-done, bf16[2,1024,1024]{1,2,0:T(8,128)(2,1)} %copy-done.8, f32[1024]{0:T(1024)S(1)} %copy-done.89, f32[1024]{0:T(1024)S(1)} %copy-done.87, ...), kind=kOutput, calls=%fused_computation.194 | convolution fusion | flops 17301504000 | bytes 54566912 | tf_op jit(solution)/shard_map/bld,df->blf/dot_general | solution.py:69
  891.5 37.9 %fusion.237 = (f32[4096]{0:T(1024)}, bf16[2,1024,4096]{2,1,0:T(8,128)(2,1)}) fusion(f32[2,1024,4096]{2,1,0:T(8,128)} %get-tuple-element.173, f32[4096]{0:T(1024)S(1)} %bitcast.362, bf16[2,1024,1024]{2,1,0:T(8,128)(2,1)} %param.12, bf16[4096,1024]{1,0:T(8,128)(2,1)} %all-gather.26.cloned.1.call-done), kind=kOutput, calls=%fused_computation.387 | convolution fusion | flops 17280528384 | bytes 62947328 | tf_op jit(solution)/shard_map/bld,fd->blf/dot_general | solution.py:85
  1034.5 71.6 %fusion.2 = (f32[2,16,1024]{2,1,0:T(8,128)S(1)}, f32[2,16,1024,1024]{2,3,1,0:T(8,128)}) fusion(bf16[2,16,1024,1024]{2,3,1,0:T(8,128)(2,1)} %divide_convert_fusion, bf16[2,1024,16,64]{1,3,2,0:T(8,128)(2,1)} %bitcast.304, bf16[2,1024,16,64]{1,3,2,0:T(8,128)(2,1)} %bitcast.298), kind=kOutput, calls=%fused_computation.6 | convolution fusion | flops 4395597824 | bytes 209846272 | tf_op jit(solution)/shard_map/bqhd,bkhd->bhqk/dot_general | solution.py:98
  1106.1 104.1 %fusion.3 = bf16[2,16,1024,1024]{2,3,1,0:T(8,128)(2,1)} fusion(f32[2,16,1024,1024]{2,3,1,0:T(8,128)} %get-tuple-element.158, f32[2,16,1024]{2,1,0:T(8,128)S(1)} %get-tuple-element.157, f32[2,16,1024,1024]{2,3,1,0:T(8,128)} %get-tuple-element.154, f32[2,16,1024]{2,1,0:T(8,128)S(1)} %copy-done.32), kind=kLoop, calls=%fused_computation.7 | loop fusion | flops 201326592 | bytes 335806464 | tf_op jit(solution)/shard_map/convert_element_type | solution.py:101
  1210.2 32.7 %convolution_bitcast_fusion.7 = f32[2,1024,16,64]{1,3,2,0:T(8,128)} fusion(bf16[2,16,1024,1024]{2,3,1,0:T(8,128)(2,1)} %fusion.3, bf16[2,1024,16,32]{1,3,2,0:T(8,128)(2,1)} %get-tuple-element.103, bf16[2,1024,16,32]{1,3,2,0:T(8,128)(2,1)} %get-tuple-element.102), kind=kOutput, calls=%fused_computation.233 | convolution fusion | flops 4303355904 | bytes 79691776 | tf_op jit(solution)/shard_map/bhqk,bqhd->bkhd/dot_general | solution.py:103
  1415.9 38.0 %fusion.238 = (f32[4096]{0:T(1024)}, bf16[2,1024,4096]{2,1,0:T(8,128)(2,1)}) fusion(f32[2,1024,4096]{2,1,0:T(8,128)} %get-tuple-element.150, f32[4096]{0:T(1024)S(1)} %bitcast.350, bf16[2,1024,1024]{1,2,0:T(8,128)(2,1)} %fusion.92, bf16[4096,1024]{0,1:T(8,128)(2,1)} %all-gather.32.cloned.1.call-done), kind=kOutput, calls=%fused_computation.388 | convolution fusion | flops 17280528384 | bytes 62947328 | tf_op jit(solution)/shard_map/bld,fd->blf/dot_general | solution.py:85
  1540.2 32.1 %convolution_convert_fusion = bf16[2,16,64,1024]{3,2,1,0:T(8,128)(2,1)} fusion(bf16[2,1024,16,64]{1,3,2,0:T(8,128)(2,1)} %bitcast.305, bf16[2,16,1024,1024]{2,3,1,0:T(8,128)(2,1)} %divide_convert_fusion.1), kind=kOutput, calls=%fused_computation.235 | convolution fusion | flops 4297064448 | bytes 75497472 | tf_op jit(solution)/shard_map/bhqk,bqhd->bkhd/dot_general | solution.py:99
  1572.3 71.6 %fusion.4 = (f32[2,16,1024]{2,1,0:T(8,128)S(1)}, f32[2,16,1024,1024]{2,3,1,0:T(8,128)}) fusion(bf16[2,16,1024,1024]{2,3,1,0:T(8,128)(2,1)} %divide_convert_fusion.1, bf16[2,1024,16,64]{1,3,2,0:T(8,128)(2,1)} %bitcast.306, bf16[2,1024,16,64]{1,3,2,0:T(8,128)(2,1)} %bitcast.296), kind=kOutput, calls=%fused_computation.8 | convolution fusion | flops 4395597824 | bytes 209846272 | tf_op jit(solution)/shard_map/bqhd,bkhd->bhqk/dot_general | solution.py:98
  1644.0 104.2 %fusion.5 = bf16[2,16,1024,1024]{2,3,1,0:T(8,128)(2,1)} fusion(f32[2,16,1024,1024]{2,3,1,0:T(8,128)} %get-tuple-element.160, f32[2,16,1024]{2,1,0:T(8,128)S(1)} %get-tuple-element.159, f32[2,16,1024,1024]{2,3,1,0:T(8,128)} %get-tuple-element.147, f32[2,16,1024]{2,1,0:T(8,128)S(1)} %copy-done.30), kind=kLoop, calls=%fused_computation.9 | loop fusion | flops 201326592 | bytes 335806464 | tf_op jit(solution)/shard_map/convert_element_type | solution.py:101
  1748.1 32.7 %convolution_bitcast_fusion.5 = f32[2,1024,16,64]{1,3,2,0:T(8,128)} fusion(bf16[2,16,1024,1024]{2,3,1,0:T(8,128)(2,1)} %fusion.5, bf16[2,1024,16,32]{1,3,2,0:T(8,128)(2,1)} %get-tuple-element.107, bf16[2,1024,16,32]{1,3,2,0:T(8,128)(2,1)} %get-tuple-element.106), kind=kOutput, calls=%fused_computation.231 | convolution fusion | flops 4303355904 | bytes 79691776 | tf_op jit(solution)/shard_map/bhqk,bqhd->bkhd/dot_general | solution.py:103
  1986.2 94.8 %fusion.74 = f32[4096,1024]{1,0:T(8,128)} fusion(bf16[2,1024,1024]{2,1,0:T(8,128)(2,1)} %param.12, f32[2,1024,4096]{2,1,0:T(8,128)} %get-tuple-element.173, f32[4096]{0:T(1024)S(1)} %bitcast.363, u8[1024,4096]{1,0:T(8,128)(4,1)} %get-tuple-element.61, u8[1024,4096]{1,0:T(8,128)(4,1)} %get-tuple-element.60), kind=kOutput, calls=%fused_computation.133 | convolution fusion | flops 17775460352 | bytes 62930944 | tf_op jit(solution)/shard_map/blf,bld->fd/dot_general | solution.py:84
  2157.1 33.0 %all-reduce.7 = (f32[4096]{0:T(1024)S(1)}, f32[4096]{0:T(1024)S(1)}, f32[1024]{0:T(1024)S(1)}, f32[1024]{0:T(1024)S(1)}) all-reduce(f32[4096]{0:T(1024)S(1)} %copy-done.77, f32[4096]{0:T(1024)S(1)} %copy-done.78, f32[1024]{0:T(1024)S(1)} %copy-done.79, f32[1024]{0:T(1024)S(1)} %copy-done.80), channel_id=25, replica_groups=mesh['fsdp'=16] {'fsdp'}, use_global_device_ids=true, to_apply=%region_47.48.clone | all-reduce | flops 10240 | bytes 81920
  2210.3 181.4 %all-reduce.11.cloned.1.call-done = (f32[3,1024,1024]{2,0,1:T(4,128)}, f32[3,1024,1024]{2,0,1:T(4,128)}) async-done(((f32[3,1024,1024]{2,0,1:T(4,128)}, f32[3,1024,1024]{2,0,1:T(4,128)}), (f32[3,1024,1024]{2,0,1:T(4,128)}, f32[3,1024,1024]{2,0,1:T(4,128)})) %all-reduce.11.cloned.1.call-update) | async-done | bytes 25165840
  2397.7 173.6 %reduce-scatter.29.cloned.1.call-done = f32[256,1024]{1,0:T(8,128)} async-done(((f32[4096,1024]{1,0:T(8,128)}), f32[256,1024]{1,0:T(8,128)}) %reduce-scatter.29.cloned.1.call-update) | async-done | bytes 1048592 | tf_op jit(solution)/shard_map/reduce_scatter | solution.py:139
  2571.2 177.6 %reduce-scatter.27.cloned.1.call-done = f32[256,1024]{1,0:T(8,128)} async-done(((f32[4096,1024]{1,0:T(8,128)}), f32[256,1024]{1,0:T(8,128)}) %reduce-scatter.27.cloned.1.call-update) | async-done | bytes 1048592 | tf_op jit(solution)/shard_map/reduce_scatter | solution.py:139
  2752.0 174.7 %reduce-scatter.25.cloned.1.call-done = f32[64,4096]{1,0:T(8,128)} async-done(((f32[1024,4096]{1,0:T(8,128)}), f32[64,4096]{1,0:T(8,128)}) %reduce-scatter.25.cloned.1.call-update) | async-done | bytes 1048592 | tf_op jit(solution)/shard_map/reduce_scatter | solution.py:137
  2926.7 177.8 %reduce-scatter.23.cloned.1.call-done = f32[64,4096]{1,0:T(8,128)} async-done(((f32[1024,4096]{1,0:T(8,128)}), f32[64,4096]{1,0:T(8,128)}) %reduce-scatter.23.cloned.1.call-update) | async-done | bytes 1048592 | tf_op jit(solution)/shard_map/reduce_scatter | solution.py:137
  (451 shorter events, 1126.1 us)
Async XLA Ops:
  7.2 216.2 %all-gather.38.cloned.1.call-start = ((), (), s32[]{:S(2)}) async-start(), calls=%async_computation.20 | async-start | bytes 8912896 | tf_op jit(solution)/shard_map/all_gather | solution.py:121
  9.9 286.5 %all-gather.44.cloned.1.call-start = ((), (), s32[]{:S(2)}) async-start(), calls=%async_computation.23 | async-start | bytes 8912896 | tf_op jit(solution)/shard_map/all_gather | solution.py:121
  11.2 463.6 %all-gather.40.cloned.1.call-start = ((), (), s32[]{:S(2)}) async-start(), calls=%async_computation.21 | async-start | bytes 8912896 | tf_op jit(solution)/shard_map/all_gather | solution.py:124
  13.9 584.6 %all-gather.42.cloned.1.call-start = ((), (), s32[]{:S(2)}) async-start(), calls=%async_computation.22 | async-start | bytes 8912896 | tf_op jit(solution)/shard_map/all_gather | solution.py:126
  15.9 832.7 %all-gather.46.cloned.1.call-start = ((), (), s32[]{:S(2)}) async-start(), calls=%async_computation.24 | async-start | bytes 8912896 | tf_op jit(solution)/shard_map/all_gather | solution.py:124
  16.5 874.9 %all-gather.26.cloned.1.call-start = ((), (), s32[]{:S(2)}) async-start(), calls=%async_computation.10 | async-start | bytes 8912896 | tf_op jit(solution)/shard_map/all_gather | solution.py:126
  17.2 912.2 %all-gather.28.cloned.1.call-start = ((), (), s32[]{:S(2)}) async-start(), calls=%async_computation.11 | async-start | bytes 8912896 | tf_op jit(solution)/shard_map/all_gather | solution.py:124
  17.9 964.8 %all-gather.30.cloned.1.call-start = ((), (), s32[]{:S(2)}) async-start(), calls=%async_computation.12 | async-start | bytes 8912896 | tf_op jit(solution)/shard_map/all_gather | solution.py:121
  18.7 1397.3 %all-gather.32.cloned.1.call-start = ((), (), s32[]{:S(2)}) async-start(), calls=%async_computation.13 | async-start | bytes 8912896 | tf_op jit(solution)/shard_map/all_gather | solution.py:126
  93.5 225.1 %copy-start.101 = (pred[2,1024]{1,0:T(4,128)(4,1)}, pred[2,1024]{1,0:T(4,128)(4,1)S(1)}, u32[]{:S(2)}) copy-start(pred[2,1024]{1,0:T(4,128)(4,1)S(1)} %iota_compare_fusion) | copy-start | bytes 6148
  119.7 189.9 %copy-start.20 = (f32[1024,32]{0,1:T(8,128)}, f32[1024,32]{0,1:T(8,128)S(1)}, u32[]{:S(2)}) copy-start(f32[1024,32]{0,1:T(8,128)S(1)} %get-tuple-element.144) | copy-start | bytes 393220
  1353.0 113.7 %all-gather.34.cloned.1.call-start = ((), (), s32[]{:S(2)}) async-start(), calls=%async_computation.14 | async-start | bytes 8912896 | tf_op jit(solution)/shard_map/all_gather | solution.py:124
  1353.6 166.6 %all-gather.36.cloned.1.call-start = ((), (), s32[]{:S(2)}) async-start(), calls=%async_computation.15 | async-start | bytes 8912896 | tf_op jit(solution)/shard_map/all_gather | solution.py:121
  1354.3 799.7 %reduce-scatter.37.cloned.1.call-start = ((), (), s32[]{:S(2)}) async-start(), calls=%async_computation.28 | async-start | bytes 557056
  1372.2 782.7 %reduce-scatter.41.cloned.1.call-start = ((), (), s32[]{:S(2)}) async-start(), calls=%async_computation.30 | async-start | bytes 557056
  1385.2 770.5 %reduce-scatter.33.cloned.1.call-start = ((), (), s32[]{:S(2)}) async-start(), calls=%async_computation.26 | async-start | bytes 4456448
  1385.9 820.7 %reduce-scatter.35.cloned.1.call-start = ((), (), s32[]{:S(2)}) async-start(), calls=%async_computation.27 | async-start | bytes 557056
  1893.9 313.6 %reduce-scatter.39.cloned.1.call-start = ((), (), s32[]{:S(2)}) async-start(), calls=%async_computation.29 | async-start | bytes 557056
  1895.3 313.6 %reduce-scatter.31.cloned.1.call-start = ((), (), s32[]{:S(2)}) async-start(), calls=%async_computation.25 | async-start | bytes 4456448
  1905.3 486.4 %all-reduce.11.cloned.1.call-start = ((), (), s32[]{:S(2)}) async-start(), calls=%async_computation.31 | async-start | bytes 67108864
  1985.5 585.7 %reduce-scatter.29.cloned.1.call-start = ((), (), s32[]{:S(2)}) async-start(), calls=%async_computation.19 | async-start | bytes 17825792 | tf_op jit(solution)/shard_map/reduce_scatter | solution.py:139
  2081.0 667.9 %reduce-scatter.27.cloned.1.call-start = ((), (), s32[]{:S(2)}) async-start(), calls=%async_computation.18 | async-start | bytes 17825792 | tf_op jit(solution)/shard_map/reduce_scatter | solution.py:139
  2105.0 821.7 %reduce-scatter.25.cloned.1.call-start = ((), (), s32[]{:S(2)}) async-start(), calls=%async_computation.17 | async-start | bytes 17825792 | tf_op jit(solution)/shard_map/reduce_scatter | solution.py:137
  2129.3 975.2 %reduce-scatter.23.cloned.1.call-start = ((), (), s32[]{:S(2)}) async-start(), calls=%async_computation.16 | async-start | bytes 17825792 | tf_op jit(solution)/shard_map/reduce_scatter | solution.py:137
  (110 other events, 2511.4 us)
Sparse Core Ops, SparseCore 0:
  10.3 53.9 all-gather.37
  66.5 49.5 all-gather.43
  118.3 50.9 all-gather.39
  171.4 63.5 all-gather.41
  237.0 48.6 all-gather.45
  287.8 48.6 all-gather.25
  338.7 48.6 all-gather.27
  389.7 48.6 all-gather.29
  1353.1 62.7 all-gather.31
  1418.0 48.6 all-gather.33
  1469.0 48.6 all-gather.35
  1519.7 54.5 reduce-scatter.36
  1576.5 52.7 reduce-scatter.40
  1631.4 61.9 reduce-scatter.32
  1894.0 54.5 reduce-scatter.34
  1951.2 52.6 reduce-scatter.38
  2006.0 62.0 reduce-scatter.30
  2074.0 317.5 all-reduce.10
  2393.9 177.2 reduce-scatter.28
  2573.4 175.4 reduce-scatter.26
  2751.2 175.4 reduce-scatter.24
  2928.9 175.4 reduce-scatter.22
where the time goes:
time: 3130 us; the launch traced here: 3110 us
  matrix products  1080 us (35%)
  waiting for transfers between devices  931 us (30%)
  other arithmetic  649 us (21%)
  local copies, waits for them, and re-layouts  271 us (9%)
  blocking collectives  172 us (5%)
    reduce_scatter x2, waiting for transfers between devices, scatter_grads(): reduce_rows(gw_up, scatter_dimension=0)  353 us
    reduce_scatter x2, waiting for transfers between devices, scatter_grads(): reduce_rows(gw_down, scatter_dimension=0)  351 us
    convert_element_type x2, other arithmetic, layer_backward(): (probs_f32 * (d_probs - jnp.sum(d_probs * probs_f32, axis=-1, keepdims=Tr...  208 us
    unnamed x29, waiting for transfers between devices  185 us
    dot_general x2, matrix products, layer_backward(): jnp.einsum('bqhd,bkhd->bhqk', d_context, values, preferred_element_type=j...  143 us
    convert_element_type x2, other arithmetic, layer_forward(): jax.nn.softmax(jnp.where(key_valid, scores, NEG_BIG), axis=-1)  129 us
    dot_general x2, matrix products, layer_backward(): jnp.einsum('blf,bld->fd', act_bf, d_out, preferred_element_type=jnp.float32)  119 us
    sub x2, matrix products, layer_forward(): jax.nn.softmax(jnp.where(key_valid, scores, NEG_BIG), axis=-1)  107 us
  transfers between devices with their start and end apart: 22, of which 7 were waited for; matrix products, arithmetic and copies ran while one was open for 51% of the time, Pallas kernels for 0%

commit v1 on v0

--- a/solution.py
+++ b/solution.py
@@ -116,28 +116,103 @@
     return d_x, (gw_qkv, gw_out, gb_attn, g_ln, gw_up, gb_up, gw_down, gb_down)
 
 
-def gather_layer(layer_shards, axis_name):
+BITS = {'c': 1, 'x': 2, 'y': 4, 'z': 8}
+
+
+def swap(value, axis_name, dim):
+    num = 16
+    return lax.ppermute(value, axis_name, [(i, i ^ BITS[dim]) for i in range(num)])
+
+
+def bit_of(axis_name, dim):
+    return (lax.axis_index(axis_name) // BITS[dim]) % 2
+
+
+def gather_rows(shard, axis_name, order):
+    me = lax.axis_index(axis_name)
+    held = shard[None]
+    masks = [0]
+    for dim in order:
+        got = swap(held, axis_name, dim)
+        held = jnp.concatenate([held, got], axis=0)
+        masks = masks + [m ^ BITS[dim] for m in masks]
+    rows = shard.shape[0]
+    out = jnp.zeros((16,) + shard.shape, shard.dtype)
+    pos = [masks.index(m) for m in range(16)]
+    ordered = jnp.stack([held[p] for p in pos])
+    ordered = ordered.reshape((2, 2, 2, 2) + shard.shape)
+    for ax, dim in enumerate(('z', 'y', 'x', 'c')):
+        flip = bit_of(axis_name, dim)
+        ordered = jnp.where(flip == 1, jnp.flip(ordered, ax), ordered)
+    return ordered.reshape((16 * rows,) + shard.shape[1:])
+
+
+def scatter_rows(full, axis_name, order):
+    rows = full.shape[0] // 16
+    cur = full.reshape((2, 2, 2, 2, rows) + full.shape[1:])
+    dims = ['z', 'y', 'x', 'c']
+    for dim in order:
+        ax = dims.index(dim)
+        mine = bit_of(axis_name, dim)
+        give = lax.dynamic_index_in_dim(cur, 1 - mine, ax, keepdims=False).astype(jnp.bfloat16)
+        keep = lax.dynamic_index_in_dim(cur, mine, ax, keepdims=False)
+        cur = keep + swap(give, axis_name, dim).astype(jnp.float32)
+        dims.remove(dim)
+    return cur
+
+
+ORDERS = (('x', 'y', 'z', 'c'), ('y', 'z', 'x', 'c'), ('z', 'x', 'y', 'c'))
+SORDERS = (('c', 'x', 'y', 'z'), ('c', 'y', 'z', 'x'), ('c', 'z', 'x', 'y'))
+
+
+def gather_small(layer_shards, axis_name):
     w_attn, b_attn, ln_par, w_up, b_up, w_down, b_down = layer_shards
-    return (lax.all_gather(w_attn, axis_name, axis=1, tiled=True),
-            lax.all_gather(b_attn, axis_name, axis=1, tiled=True),
-            lax.all_gather(ln_par, axis_name, axis=1, tiled=True),
-            lax.all_gather(w_up, axis_name, axis=0, tiled=True),
-            lax.all_gather(b_up, axis_name, axis=0, tiled=True),
-            lax.all_gather(w_down, axis_name, axis=0, tiled=True),
-            lax.all_gather(b_down, axis_name, axis=0, tiled=True))
-
-
-def scatter_grads(layer_grads, axis_name):
+    packed = jnp.concatenate([b_attn.reshape(-1), ln_par.reshape(-1), b_up, b_down])
+    full = lax.all_gather(packed, axis_name)
+    n = b_attn.shape[1]
+    nu = b_up.shape[0]
+    ba = full[:, :4 * n].reshape(16, 4, n).transpose(1, 0, 2).reshape(4, 16 * n)
+    lp = full[:, 4 * n:8 * n].reshape(16, 4, n).transpose(1, 0, 2).reshape(4, 16 * n)
+    bu = full[:, 8 * n:8 * n + nu].reshape(-1)
+    bd = full[:, 8 * n + nu:].reshape(-1)
+    return ba, lp, bu, bd
+
+
+def gather_layer(layer_idx, layer_shards, axis_name):
+    w_attn, b_attn, ln_par, w_up, b_up, w_down, b_down = layer_shards
+    ba, lp, bu, bd = gather_small(layer_shards, axis_name)
+    if layer_idx == 0:
+        parts = [gather_rows(w_attn[i], axis_name, ORDERS[i % 3]) for i in range(4)]
+        wa = jnp.stack(parts)
+        wu = gather_rows(w_up, axis_name, ORDERS[1])
+        wd = gather_rows(w_down, axis_name, ORDERS[2])
+    else:
+        wa = lax.all_gather(w_attn, axis_name, axis=1, tiled=True)
+        wu = lax.all_gather(w_up, axis_name, axis=0, tiled=True)
+        wd = lax.all_gather(w_down, axis_name, axis=0, tiled=True)
+    return (wa, ba, lp, wu, bu, wd, bd)
+
+
+def scatter_grads(layer_idx, layer_grads, axis_name):
     gw_qkv, gw_out, gb_attn, g_ln, gw_up, gb_up, gw_down, gb_down = layer_grads
     reduce_rows = functools.partial(lax.psum_scatter, axis_name=axis_name, tiled=True)
-    attn_part = jnp.concatenate([reduce_rows(gw_qkv, scatter_dimension=1), reduce_rows(gw_out, scatter_dimension=0)[None]], axis=0)
-    return (attn_part,
-            reduce_rows(gb_attn, scatter_dimension=1),
-            reduce_rows(g_ln, scatter_dimension=1),
-            reduce_rows(gw_up, scatter_dimension=0),
-            reduce_rows(gb_up, scatter_dimension=0),
-            reduce_rows(gw_down, scatter_dimension=0),
-            reduce_rows(gb_down, scatter_dimension=0))
+    if layer_idx == 0:
+        attn_part = jnp.stack([scatter_rows(gw_qkv[i], axis_name, SORDERS[i]) for i in range(3)] + [scatter_rows(gw_out, axis_name, SORDERS[0])])
+        up_part = scatter_rows(gw_up, axis_name, SORDERS[1])
+        down_part = scatter_rows(gw_down, axis_name, SORDERS[2])
+    else:
+        half = lambda g: g.astype(jnp.bfloat16)
+        attn_part = jnp.concatenate([reduce_rows(half(gw_qkv), scatter_dimension=1), reduce_rows(half(gw_out), scatter_dimension=0)[None]], axis=0).astype(jnp.float32)
+        up_part = reduce_rows(half(gw_up), scatter_dimension=0).astype(jnp.float32)
+        down_part = reduce_rows(half(gw_down), scatter_dimension=0).astype(jnp.float32)
+    n = gb_attn.shape[1] // 16
+    nu = gb_up.shape[0] // 16
+    packed = jnp.concatenate([gb_attn.reshape(4, 16, n).transpose(1, 0, 2).reshape(16, 4 * n),
+                              g_ln.reshape(4, 16, n).transpose(1, 0, 2).reshape(16, 4 * n),
+                              gb_up.reshape(16, nu), gb_down.reshape(16, n)], axis=1)
+    small = lax.psum_scatter(packed, axis_name, scatter_dimension=0, tiled=True)[0]
+    return (attn_part, small[:4 * n].reshape(4, n), small[4 * n:8 * n].reshape(4, n), up_part,
+            small[8 * n:8 * n + nu], down_part, small[8 * n + nu:])
 
 
 def solution(mesh):
@@ -152,17 +227,18 @@
         tables = rotary_tables(x.shape[1])
         hidden = x
         saved_list = []
+        full_list = []
         for layer_idx in range(num_layers):
-            full_wts = gather_layer(tuple(shard[layer_idx] for shard in shards), axis_name)
+            full_wts = gather_layer(layer_idx, tuple(shard[layer_idx] for shard in shards), axis_name)
+            full_list.append(full_wts)
             hidden, saved_acts = layer_forward(hidden, full_wts, lengths, tables)
             saved_list.append(saved_acts)
         grad_x = d_y
         grads_list = [None] * num_layers
         for layer_idx in reversed(range(num_layers)):
-            layer_shards, grad_x = lax.optimization_barrier((tuple(shard[layer_idx] for shard in shards), grad_x))
-            full_wts = gather_layer(layer_shards, axis_name)
+            full_wts = full_list[layer_idx]
             grad_x, layer_grads = layer_backward(grad_x, saved_list[layer_idx], full_wts, tables)
-            grads_list[layer_idx] = scatter_grads(layer_grads, axis_name)
+            grads_list[layer_idx] = scatter_grads(layer_idx, layer_grads, axis_name)
         stacked = tuple(jnp.stack([grads_list[layer_pos][field_pos] for layer_pos in range(num_layers)]) for field_pos in range(7))
         return (grad_x,) + stacked
 

time: 3130 us -> 2440 us (0.78)
  waiting for transfers between devices: 931 us -> 184 us
  blocking collectives: 172 us -> 39.1 us
  other arithmetic: 649 us -> 777 us
  starting transfers between devices: 1.11 us -> 46.4 us
  local copies, waits for them, and re-layouts: 271 us -> 311 us
    reduce_scatter x4, waiting for transfers between devices: 704 us -> 0.04 us  [the longest x1 0.02 us: scatter_grads(): reduce_rows(half(gw_out), scatter_dimension=0)[None]]
    unnamed x29 -> x9, waiting for transfers between devices: 185 us -> 0.13 us
    ppermute x0 -> x48, waiting for transfers between devices: none -> 184 us  [swap(): lax.ppermute(value, axis_name, [(i, i ^ BITS[dim]) for i in range(num)])]
    select_n x0 -> x22, other arithmetic: none -> 134 us  [gather_rows(): ordered = jnp.where(flip == 1, jnp.flip(ordered, ax), ordered)]
    all_gather x8 -> x0, blocking collectives: 106 us -> none  [the longest x4 50.9 us: gather_layer(): lax.all_gather(ln_par, axis_name, axis=1, tiled=True)]
    unnamed x256 -> x452, local copies, waits for them, and re-layouts: 95.8 us -> 145 us
    ppermute x0 -> x48, starting transfers between devices: none -> 46 us  [swap(): lax.ppermute(value, axis_name, [(i, i ^ BITS[dim]) for i in range(num)])]
    convert_element_type x2, other arithmetic: 44.1 us -> 0.2 us  [layer_forward(): ln_par[2].astype(jnp.float32)]
  transfers between devices with their start and end apart: 22 -> 56, of which waited for: 7 -> 14; matrix products, arithmetic and copies ran while one was open for 51% -> 50% of each run, Pallas kernels for 0% -> 0%
where the time goes in v1:
time: 2440 us; the launch traced here: 2420 us
  matrix products  1050 us (43%)
  other arithmetic  777 us (32%)
  local copies, waits for them, and re-layouts  311 us (13%)
  waiting for transfers between devices  184 us (8%)
  starting transfers between devices  46.4 us (2%)
  blocking collectives  39.1 us (2%)
    convert_element_type x2, other arithmetic, layer_backward(): (probs_f32 * (d_probs - jnp.sum(d_probs * probs_f32, axis=-1, keepdims=Tr...  208 us
    ppermute x48, waiting for transfers between devices, swap(): lax.ppermute(value, axis_name, [(i, i ^ BITS[dim]) for i in range(num)])  184 us
    unnamed x452, local copies, waits for them, and re-layouts  145 us
    dot_general x2, matrix products, layer_backward(): jnp.einsum('bqhd,bkhd->bhqk', d_context, values, preferred_element_type=j...  143 us
    select_n x22, other arithmetic, gather_rows(): ordered = jnp.where(flip == 1, jnp.flip(ordered, ax), ordered)  134 us
    convert_element_type x2, other arithmetic, layer_forward(): jax.nn.softmax(jnp.where(key_valid, scores, NEG_BIG), axis=-1)  129 us
    dot_general x2, matrix products, layer_backward(): jnp.einsum('blf,bld->fd', act_bf, d_out, preferred_element_type=jnp.float32)  117 us
    sub x2, matrix products, layer_forward(): jax.nn.softmax(jnp.where(key_valid, scores, NEG_BIG), axis=-1)  107 us
  transfers between devices with their start and end apart: 56, of which 14 were waited for; matrix products, arithmetic and copies ran while one was open for 50% of the time, Pallas kernels for 0%

profile of v1, /device:TPU:0, one launch (start us, length us, event | category | flops | bytes accessed | tf_op | source)
XLA Modules:
  0.0 2421.1 jit_solution(18439522975943733064)
XLA Ops:
  31.9 39.1 %all-reduce.5 = (bf16[13312]{0:T(1024)(128)(2,1)}, bf16[13312]{0:T(1024)(128)(2,1)}) all-reduce(bf16[13312]{0:T(1024)(128)(2,1)} %dynamic-update-slice, bf16[13312]{0:T(1024)(128)(2,1)} %dynamic-update-slice.1), channel_id=3, replica_groups=mesh['fsdp'=16] {'fsdp'}, use_global_device_ids=true, to_apply=%add | all-reduce | flops 26624 | bytes 106496
  164.1 42.1 %collective-permute-done.2 = bf16[4,64,1024]{2,1,0:T(8,128)(2,1)S(1)} collective-permute-done((bf16[4,64,1024]{2,1,0:T(8,128)(2,1)S(1)}, bf16[4,64,1024]{2,1,0:T(8,128)(2,1)S(1)}, u32[]{:S(2)}, u32[]{:S(2)}) %collective-permute-start.2) | collective-permute-done | bytes 524320 | tf_op jit(solution)/shard_map/ppermute | solution.py:124
  313.4 53.6 %fusion.262 = (f32[2,16,1024]{2,1,0:T(8,128)S(1)}, f32[2,16,1024,1024]{2,3,1,0:T(8,128)}) fusion(pred[2,1024]{1,0:T(4,128)(4,1)S(1)} %copy-done.167, bf16[2,1024,16,32]{1,3,2,0:T(8,128)(2,1)S(1)} %get-tuple-element.128, bf16[2,1024,16,32]{1,3,2,0:T(8,128)(2,1)} %get-tuple-element.129, bf16[2,1024,16,32]{1,3,2,0:T(8,128)(2,1)} %get-tuple-element.104, ...), kind=kOutput, calls=%fused_computation.609 | convolution fusion | flops 4412408832 | bytes 142739456 | tf_op jit(solution)/shard_map/sub | solution.py:62
  367.6 64.3 %divide_convert_fusion.1 = bf16[2,16,1024,1024]{2,3,1,0:T(8,128)(2,1)} fusion(f32[2,16,1024,1024]{2,3,1,0:T(8,128)} %get-tuple-element.147, f32[2,16,1024]{2,1,0:T(8,128)S(1)} %get-tuple-element.146), kind=kLoop, calls=%fused_computation.12 | loop fusion | flops 67108864 | bytes 201457664 | tf_op jit(solution)/shard_map/convert_element_type | solution.py:62
  636.4 43.2 %fusion.119 = (u8[1024,4096]{1,0:T(8,128)(4,1)}, u8[1024,4096]{1,0:T(8,128)(4,1)}, f32[2,1024,4096]{2,1,0:T(8,128)}) fusion(f32[4096]{0:T(1024)S(1)} %bitcast.456, bf16[1024,4096,1]{1,0,2:T(8,128)(2,1)} %bitcast.429, bf16[2,1024,1024]{1,2,0:T(8,128)(2,1)} %copy-done.8, f32[1024]{0:T(1024)S(1)} %copy-done.157, f32[1024]{0:T(1024)S(1)} %copy-done.119, ...), kind=kOutput, calls=%fused_computation.199 | convolution fusion | flops 17301504000 | bytes 54566912 | tf_op jit(solution)/shard_map/bld,df->blf/dot_general | solution.py:69
  679.6 80.7 %fusion.18 = bf16[2,1024,4096]{2,1,0:T(8,128)(2,1)} fusion(f32[2,1024,4096]{2,1,0:T(8,128)} %get-tuple-element.150, f32[4096]{0:T(1024)S(1)} %bitcast.457, u8[1024,4096]{1,0:T(8,128)(4,1)} %get-tuple-element.51, u8[1024,4096]{1,0:T(8,128)(4,1)} %get-tuple-element.50), kind=kLoop, calls=%fused_computation.28 | loop fusion | flops 595591168 | bytes 58736640 | tf_op jit(solution)/shard_map/convert_element_type | solution.py:70
  835.7 53.4 %fusion.263 = (f32[2,16,1024]{2,1,0:T(8,128)S(1)}, f32[2,16,1024,1024]{2,3,1,0:T(8,128)}) fusion(pred[2,1024]{1,0:T(4,128)(4,1)S(1)} %copy-done.168, bf16[2,1024,16,32]{1,3,2,0:T(8,128)(2,1)S(1)} %get-tuple-element.126, bf16[2,1024,16,32]{1,3,2,0:T(8,128)(2,1)} %get-tuple-element.127, bf16[2,1024,16,32]{1,3,2,0:T(8,128)(2,1)} %get-tuple-element.100, ...), kind=kOutput, calls=%fused_computation.610 | convolution fusion | flops 4412408832 | bytes 142739456 | tf_op jit(solution)/shard_map/sub | solution.py:62
  889.1 64.7 %divide_convert_fusion = bf16[2,16,1024,1024]{2,3,1,0:T(8,128)(2,1)} fusion(f32[2,16,1024,1024]{2,3,1,0:T(8,128)} %get-tuple-element.154, f32[2,16,1024]{2,1,0:T(8,128)S(1)} %get-tuple-element.153), kind=kLoop, calls=%fused_computation.10 | loop fusion | flops 67108864 | bytes 201457664 | tf_op jit(solution)/shard_map/convert_element_type | solution.py:62
  969.9 26.8 %convolution_convert_fusion.2 = bf16[2,16,64,1024]{3,2,1,0:T(8,128)(2,1)} fusion(bf16[2,1024,16,64]{1,3,2,0:T(8,128)(2,1)} %bitcast.397, bf16[2,16,1024,1024]{2,3,1,0:T(8,128)(2,1)} %divide_convert_fusion), kind=kOutput, calls=%fused_computation.274 | convolution fusion | flops 4297064448 | bytes 75497472 | tf_op jit(solution)/shard_map/bhqk,bkhd->bqhd/dot_general | solution.py:63
  1009.7 42.9 %fusion.120 = (u8[1024,4096]{1,0:T(8,128)(4,1)}, u8[1024,4096]{1,0:T(8,128)(4,1)}, f32[2,1024,4096]{2,1,0:T(8,128)}) fusion(f32[4096]{0:T(1024)S(1)} %bitcast.459, bf16[1,1024,4096]{2,1,0:T(8,128)(2,1)} %all-gather.13.cloned.1.call-done, bf16[2,1024,1024]{1,2,0:T(8,128)(2,1)} %copy-done.14, f32[1024]{0:T(1024)S(1)} %copy-done.155, ...), kind=kOutput, calls=%fused_computation.200 | convolution fusion | flops 17301504000 | bytes 54566912 | tf_op jit(solution)/shard_map/bld,df->blf/dot_general | solution.py:69
  1052.6 38.0 %fusion.264 = (f32[4096]{0:T(1024)}, bf16[2,1024,4096]{2,1,0:T(8,128)(2,1)}) fusion(f32[2,1024,4096]{2,1,0:T(8,128)} %get-tuple-element.173, f32[4096]{0:T(1024)S(1)} %bitcast.460, bf16[2,1024,1024]{2,1,0:T(8,128)(2,1)} %param.12, bf16[1,4096,1024]{2,1,0:T(8,128)(2,1)} %all-gather.9.cloned.1.call-done), kind=kOutput, calls=%fused_computation.611 | convolution fusion | flops 17280528384 | bytes 62947328 | tf_op jit(solution)/shard_map/bld,fd->blf/dot_general | solution.py:85
  1146.8 31.9 %convolution_convert_fusion.1 = bf16[2,16,64,1024]{3,2,1,0:T(8,128)(2,1)} fusion(bf16[2,1024,16,64]{1,3,2,0:T(8,128)(2,1)} %bitcast.405, bf16[2,16,1024,1024]{2,3,1,0:T(8,128)(2,1)} %divide_convert_fusion), kind=kOutput, calls=%fused_computation.273 | convolution fusion | flops 4297064448 | bytes 75497472 | tf_op jit(solution)/shard_map/bhqk,bqhd->bkhd/dot_general | solution.py:99
  1178.7 71.6 %fusion.2 = (f32[2,16,1024]{2,1,0:T(8,128)S(1)}, f32[2,16,1024,1024]{2,3,1,0:T(8,128)}) fusion(bf16[2,16,1024,1024]{2,3,1,0:T(8,128)(2,1)} %divide_convert_fusion, bf16[2,1024,16,64]{1,3,2,0:T(8,128)(2,1)} %bitcast.406, bf16[2,1024,16,64]{1,3,2,0:T(8,128)(2,1)} %bitcast.398), kind=kOutput, calls=%fused_computation.6 | convolution fusion | flops 4395597824 | bytes 209846272 | tf_op jit(solution)/shard_map/bqhd,bkhd->bhqk/dot_general | solution.py:98
  1250.3 104.1 %fusion.3 = bf16[2,16,1024,1024]{2,3,1,0:T(8,128)(2,1)} fusion(f32[2,16,1024,1024]{2,3,1,0:T(8,128)} %get-tuple-element.158, f32[2,16,1024]{2,1,0:T(8,128)S(1)} %get-tuple-element.157, f32[2,16,1024,1024]{2,3,1,0:T(8,128)} %get-tuple-element.154, f32[2,16,1024]{2,1,0:T(8,128)S(1)} %copy-done.84), kind=kLoop, calls=%fused_computation.7 | loop fusion | flops 201326592 | bytes 335806464 | tf_op jit(solution)/shard_map/convert_element_type | solution.py:101
  1354.4 32.7 %convolution_bitcast_fusion.3 = f32[2,1024,16,64]{1,3,2,0:T(8,128)} fusion(bf16[2,16,1024,1024]{2,3,1,0:T(8,128)(2,1)} %fusion.3, bf16[2,1024,16,32]{1,3,2,0:T(8,128)(2,1)} %get-tuple-element.100, bf16[2,1024,16,32]{1,3,2,0:T(8,128)(2,1)} %get-tuple-element.99), kind=kOutput, calls=%fused_computation.254 | convolution fusion | flops 4303355904 | bytes 79691776 | tf_op jit(solution)/shard_map/bhqk,bqhd->bkhd/dot_general | solution.py:103
  1387.1 27.3 %convolution_bitcast_fusion.4 = f32[2,1024,16,64]{1,3,2,0:T(8,128)} fusion(bf16[2,16,1024,1024]{2,3,1,0:T(8,128)(2,1)} %fusion.3, bf16[2,1024,16,32]{1,3,2,0:T(8,128)(2,1)S(1)} %copy-done.44, bf16[2,1024,16,32]{1,3,2,0:T(8,128)(2,1)} %get-tuple-element.127), kind=kOutput, calls=%fused_computation.255 | convolution fusion | flops 4303355904 | bytes 79691776 | tf_op jit(solution)/shard_map/bhqk,bkhd->bqhd/dot_general | solution.py:102
  1504.1 38.8 %fusion.267 = (f32[4096]{0:T(1024)}, bf16[2,1024,4096]{2,1,0:T(8,128)(2,1)}) fusion(f32[2,1024,4096]{2,1,0:T(8,128)} %get-tuple-element.150, f32[4096]{0:T(1024)S(1)} %bitcast.458, bf16[2,1024,1024]{1,2,0:T(8,128)(2,1)S(1)} %get-tuple-element.81, bf16[4096,1024,1]{1,0,2:T(8,128)(2,1)} %bitcast.434), kind=kOutput, calls=%fused_computation.614 | convolution fusion | flops 17280528384 | bytes 62947328 | tf_op jit(solution)/shard_map/bld,fd->blf/dot_general | solution.py:85
  1598.5 31.7 %convolution_convert_fusion = bf16[2,16,64,1024]{3,2,1,0:T(8,128)(2,1)} fusion(bf16[2,1024,16,64]{1,3,2,0:T(8,128)(2,1)} %bitcast.407, bf16[2,16,1024,1024]{2,3,1,0:T(8,128)(2,1)} %divide_convert_fusion.1), kind=kOutput, calls=%fused_computation.272 | convolution fusion | flops 4297064448 | bytes 75497472 | tf_op jit(solution)/shard_map/bhqk,bqhd->bkhd/dot_general | solution.py:99
  1630.2 71.5 %fusion.4 = (f32[2,16,1024]{2,1,0:T(8,128)S(1)}, f32[2,16,1024,1024]{2,3,1,0:T(8,128)}) fusion(bf16[2,16,1024,1024]{2,3,1,0:T(8,128)(2,1)} %divide_convert_fusion.1, bf16[2,1024,16,64]{1,3,2,0:T(8,128)(2,1)} %bitcast.408, bf16[2,1024,16,64]{1,3,2,0:T(8,128)(2,1)} %bitcast.396), kind=kOutput, calls=%fused_computation.8 | convolution fusion | flops 4395597824 | bytes 209846272 | tf_op jit(solution)/shard_map/bqhd,bkhd->bhqk/dot_general | solution.py:98
  1701.7 104.2 %fusion.5 = bf16[2,16,1024,1024]{2,3,1,0:T(8,128)(2,1)} fusion(f32[2,16,1024,1024]{2,3,1,0:T(8,128)} %get-tuple-element.160, f32[2,16,1024]{2,1,0:T(8,128)S(1)} %get-tuple-element.159, f32[2,16,1024,1024]{2,3,1,0:T(8,128)} %get-tuple-element.147, f32[2,16,1024]{2,1,0:T(8,128)S(1)} %copy-done.82), kind=kLoop, calls=%fused_computation.9 | loop fusion | flops 201326592 | bytes 335806464 | tf_op jit(solution)/shard_map/convert_element_type | solution.py:101
  1805.9 32.8 %convolution_bitcast_fusion.1 = f32[2,1024,16,64]{1,3,2,0:T(8,128)} fusion(bf16[2,16,1024,1024]{2,3,1,0:T(8,128)(2,1)} %fusion.5, bf16[2,1024,16,32]{1,3,2,0:T(8,128)(2,1)} %get-tuple-element.104, bf16[2,1024,16,32]{1,3,2,0:T(8,128)(2,1)} %get-tuple-element.103), kind=kOutput, calls=%fused_computation.252 | convolution fusion | flops 4303355904 | bytes 79691776 | tf_op jit(solution)/shard_map/bhqk,bqhd->bkhd/dot_general | solution.py:103
  1838.7 27.3 %convolution_bitcast_fusion.2 = f32[2,1024,16,64]{1,3,2,0:T(8,128)} fusion(bf16[2,16,1024,1024]{2,3,1,0:T(8,128)(2,1)} %fusion.5, bf16[2,1024,16,32]{1,3,2,0:T(8,128)(2,1)S(1)} %copy-done.42, bf16[2,1024,16,32]{1,3,2,0:T(8,128)(2,1)} %get-tuple-element.129), kind=kOutput, calls=%fused_computation.253 | convolution fusion | flops 4303355904 | bytes 79691776 | tf_op jit(solution)/shard_map/bhqk,bkhd->bqhd/dot_general | solution.py:102
  1982.8 94.6 %bitcast_convert_fusion = bf16[4096,1024]{1,0:T(8,128)(2,1)} fusion(bf16[2,1024,1024]{2,1,0:T(8,128)(2,1)} %param.12, f32[2,1024,4096]{2,1,0:T(8,128)} %get-tuple-element.173, f32[4096]{0:T(1024)S(1)} %bitcast.461, u8[1024,4096]{1,0:T(8,128)(4,1)} %get-tuple-element.49, u8[1024,4096]{1,0:T(8,128)(4,1)} %get-tuple-element.48), kind=kOutput, calls=%fused_computation.81 | convolution fusion | flops 17779654656 | bytes 54542336 | tf_op jit(solution)/shard_map/blf,bld->fd/dot_general | solution.py:84
  2312.7 49.9 %collective-permute-done.45 = bf16[2,2,256,1024]{3,2,0,1:T(8,128)(2,1)} collective-permute-done((bf16[2,2,256,1024]{3,2,0,1:T(8,128)(2,1)}, bf16[2,2,256,1024]{3,2,0,1:T(8,128)(2,1)}, u32[]{:S(2)}, u32[]{:S(2)}) %collective-permute-start.45) | collective-permute-done | bytes 2097184 | tf_op jit(solution)/shard_map/ppermute | solution.py:124
  (841 shorter events, 1136.5 us)
Async XLA Ops:
  7.2 781.4 %all-gather.11.cloned.1.call-start = ((), (), s32[]{:S(2)}) async-start(), calls=%async_computation.9 | async-start | bytes 8912896 | tf_op jit(solution)/shard_map/all_gather | solution.py:190
  9.7 1000.0 %all-gather.13.cloned.1.call-start = ((), (), s32[]{:S(2)}) async-start(), calls=%async_computation.10 | async-start | bytes 8912896 | tf_op jit(solution)/shard_map/all_gather | solution.py:191
  12.2 1040.4 %all-gather.9.cloned.1.call-start = ((), (), s32[]{:S(2)}) async-start(), calls=%async_computation.8 | async-start | bytes 8912896 | tf_op jit(solution)/shard_map/all_gather | solution.py:192
  14.1 101.1 %collective-permute-start.12 = (bf16[1,64,1024]{2,1,0:T(8,128)(2,1)}, bf16[1,64,1024]{2,1,0:T(8,128)(2,1)S(1)}, u32[]{:S(2)}, u32[]{:S(2)}) collective-permute-start(bf16[1,64,1024]{2,1,0:T(8,128)(2,1)} %get-tuple-element.114), channel_id=1, source_target_pairs={{0,2},{1,3},{2,0},{3,1},{4,6},{5,7},{6,4},{7,5},{8,10},{9,11},{10,... | collective-permute-start | bytes 393224 | tf_op jit(solution)/shard_map/ppermute | solution.py:124
  17.4 101.1 %collective-permute-start.8 = (bf16[1,64,1024]{2,1,0:T(8,128)(2,1)S(1)}, bf16[1,64,1024]{2,1,0:T(8,128)(2,1)S(1)}, u32[]{:S(2)}, u32[]{:S(2)}) collective-permute-start(bf16[1,64,1024]{2,1,0:T(8,128)(2,1)S(1)} %get-tuple-element.115), channel_id=1, source_target_pairs={{0,8},{1,9},{2,10},{3,11},{4,12},{5,13},{6,14},{7,15},{8,0},{9,1},... | collective-permute-start | bytes 393224 | tf_op jit(solution)/shard_map/ppermute | solution.py:124
  19.0 99.8 %collective-permute-start.4 = (bf16[1,64,1024]{2,1,0:T(8,128)(2,1)S(1)}, bf16[1,64,1024]{2,1,0:T(8,128)(2,1)S(1)}, u32[]{:S(2)}, u32[]{:S(2)}) collective-permute-start(bf16[1,64,1024]{2,1,0:T(8,128)(2,1)S(1)} %get-tuple-element.116), channel_id=1, source_target_pairs={{0,4},{1,5},{2,6},{3,7},{4,0},{5,1},{6,2},{7,3},{8,12},{9,13},{10,... | collective-permute-start | bytes 393224 | tf_op jit(solution)/shard_map/ppermute | solution.py:124
  20.5 100.3 %collective-permute-start = (bf16[1,64,1024]{2,1,0:T(8,128)(2,1)S(1)}, bf16[1,64,1024]{2,1,0:T(8,128)(2,1)S(1)}, u32[]{:S(2)}, u32[]{:S(2)}) collective-permute-start(bf16[1,64,1024]{2,1,0:T(8,128)(2,1)S(1)} %get-tuple-element.117), channel_id=1, source_target_pairs={{0,2},{1,3},{2,0},{3,1},{4,6},{5,7},{6,4},{7,5},{8,10},{9,11},{10,... | collective-permute-start | bytes 393224 | tf_op jit(solution)/shard_map/ppermute | solution.py:124
  21.0 106.1 %collective-permute-start.16 = (bf16[1,64,4096]{2,1,0:T(8,128)(2,1)S(1)}, bf16[1,64,4096]{2,1,0:T(8,128)(2,1)S(1)}, u32[]{:S(2)}, u32[]{:S(2)}) collective-permute-start(bf16[1,64,4096]{2,1,0:T(8,128)(2,1)S(1)} %get-tuple-element.113), channel_id=1, source_target_pairs={{0,4},{1,5},{2,6},{3,7},{4,0},{5,1},{6,2},{7,3},{8,12},{9,13},{10,... | collective-permute-start | bytes 1572872 | tf_op jit(solution)/shard_map/ppermute | solution.py:124
  24.0 2200.8 %all-reduce.8.cloned.1.call-start = ((), (), s32[]{:S(2)}) async-start(), calls=%async_computation.11 | async-start | bytes 229376
  128.4 79.0 %collective-permute-start.17 = (bf16[2,64,4096]{2,1,0:T(8,128)(2,1)S(1)}, bf16[2,64,4096]{2,1,0:T(8,128)(2,1)S(1)}, u32[]{:S(2)}, u32[]{:S(2)}) collective-permute-start(bf16[2,64,4096]{2,1,0:T(8,128)(2,1)S(1)} %pad_maximum_fusion.46), channel_id=1, source_target_pairs={{0,8},{1,9},{2,10},{3,11},{4,12},{5,13},{6,14},{7,15},{8,0},{9,1},... | collective-permute-start | bytes 3145736 | tf_op jit(solution)/shard_map/ppermute | solution.py:124
  209.4 226.7 %collective-permute-start.18 = (bf16[4,64,4096]{2,1,0:T(8,128)(2,1)}, bf16[4,64,4096]{2,1,0:T(8,128)(2,1)}, u32[]{:S(2)}, u32[]{:S(2)}) collective-permute-start(bf16[4,64,4096]{2,1,0:T(8,128)(2,1)} %pad_maximum_fusion.13), channel_id=1, source_target_pairs={{0,2},{1,3},{2,0},{3,1},{4,6},{5,7},{6,4},{7,5},{8,10},{9,11},{10,... | collective-permute-start | bytes 6291464 | tf_op jit(solution)/shard_map/ppermute | solution.py:124
  212.4 265.3 %collective-permute-start.22 = (bf16[4,256,1024]{2,1,0:T(8,128)(2,1)}, bf16[4,256,1024]{2,1,0:T(8,128)(2,1)}, u32[]{:S(2)}, u32[]{:S(2)}) collective-permute-start(bf16[4,256,1024]{2,1,0:T(8,128)(2,1)} %pad_maximum_fusion.14), channel_id=1, source_target_pairs={{0,4},{1,5},{2,6},{3,7},{4,0},{5,1},{6,2},{7,3},{8,12},{9,13},{10,... | collective-permute-start | bytes 6291464 | tf_op jit(solution)/shard_map/ppermute | solution.py:124
  482.3 81.4 %collective-permute-start.23 = (bf16[8,256,1024]{2,1,0:T(8,128)(2,1)}, bf16[8,256,1024]{2,1,0:T(8,128)(2,1)S(1)}, u32[]{:S(2)}, u32[]{:S(2)}) collective-permute-start(bf16[8,256,1024]{2,1,0:T(8,128)(2,1)} %pad_maximum_fusion.6), channel_id=1, source_target_pairs={{0,1},{1,0},{2,3},{3,2},{4,5},{5,4},{6,7},{7,6},{8,9},{9,8},{10,11... | collective-permute-start | bytes 12582920 | tf_op jit(solution)/shard_map/ppermute | solution.py:124
  1953.9 451.9 %reduce-scatter.7.cloned.1.call-start = ((), (), s32[]{:S(2)}) async-start(), calls=%async_computation.5 | async-start | bytes 2228224 | tf_op jit(solution)/shard_map/reduce_scatter | solution.py:205
  1963.3 442.6 %reduce-scatter.5.cloned.1.call-start = ((), (), s32[]{:S(2)}) async-start(), calls=%async_computation.4 | async-start | bytes 6684672 | tf_op jit(solution)/shard_map/reduce_scatter | solution.py:205
  1982.8 425.8 %reduce-scatter.11.cloned.1.call-start = ((), (), s32[]{:S(2)}) async-start(), calls=%async_computation.7 | async-start | bytes 8912896 | tf_op jit(solution)/shard_map/reduce_scatter | solution.py:207
  2077.4 333.8 %reduce-scatter.9.cloned.1.call-start = ((), (), s32[]{:S(2)}) async-start(), calls=%async_computation.6 | async-start | bytes 8912896 | tf_op jit(solution)/shard_map/reduce_scatter | solution.py:206
  2108.0 164.6 %collective-permute-start.44 = (bf16[2,2,2,256,1024]{4,3,1,2,0:T(8,128)(2,1)}, bf16[2,2,2,256,1024]{4,3,1,2,0:T(8,128)(2,1)}, u32[]{:S(2)}, u32[]{:S(2)}) collective-permute-start(bf16[2,2,2,256,1024]{4,3,1,2,0:T(8,128)(2,1)} %fusion.131), channel_id=1, source_target_pairs={{0,1},{1,0},{2,3},{3,2},{4,5},{5,4},{6,7},{7,6},{8,9},{9,8},{10,11... | collective-permute-start | bytes 12582920 | tf_op jit(solution)/shard_map/ppermute | solution.py:124
  2131.5 150.2 %collective-permute-start.40 = (bf16[2,2,2,64,4096]{4,3,2,0,1:T(8,128)(2,1)}, bf16[2,2,2,64,4096]{4,3,2,0,1:T(8,128)(2,1)}, u32[]{:S(2)}, u32[]{:S(2)}) collective-permute-start(bf16[2,2,2,64,4096]{4,3,2,0,1:T(8,128)(2,1)} %fusion.130), channel_id=1, source_target_pairs={{0,1},{1,0},{2,3},{3,2},{4,5},{5,4},{6,7},{7,6},{8,9},{9,8},{10,11... | collective-permute-start | bytes 12582920 | tf_op jit(solution)/shard_map/ppermute | solution.py:124
  2146.7 84.1 %collective-permute-start.36 = (bf16[2,2,2,64,1024]{4,3,2,1,0:T(8,128)(2,1)S(1)}, bf16[2,2,2,64,1024]{4,3,2,1,0:T(8,128)(2,1)}, u32[]{:S(2)}, u32[]{:S(2)}) collective-permute-start(bf16[2,2,2,64,1024]{4,3,2,1,0:T(8,128)(2,1)S(1)} %fusion.158), channel_id=1, source_target_pairs={{0,1},{1,0},{2,3},{3,2},{4,5},{5,4},{6,7},{7,6},{8,9},{9,8},{10,11... | collective-permute-start | bytes 3145736 | tf_op jit(solution)/shard_map/ppermute | solution.py:124
  2281.7 80.9 %collective-permute-start.45 = (bf16[2,2,256,1024]{3,2,0,1:T(8,128)(2,1)}, bf16[2,2,256,1024]{3,2,0,1:T(8,128)(2,1)}, u32[]{:S(2)}, u32[]{:S(2)}) collective-permute-start(bf16[2,2,256,1024]{3,2,0,1:T(8,128)(2,1)} %fusion.151), channel_id=1, source_target_pairs={{0,8},{1,9},{2,10},{3,11},{4,12},{5,13},{6,14},{7,15},{8,0},{9,1},... | collective-permute-start | bytes 6291464 | tf_op jit(solution)/shard_map/ppermute | solution.py:124
  2294.4 74.2 %collective-permute-start.41 = (bf16[2,2,64,4096]{3,2,1,0:T(8,128)(2,1)S(1)}, bf16[2,2,64,4096]{3,2,1,0:T(8,128)(2,1)S(1)}, u32[]{:S(2)}, u32[]{:S(2)}) collective-permute-start(bf16[2,2,64,4096]{3,2,1,0:T(8,128)(2,1)S(1)} %fusion.150), channel_id=1, source_target_pairs={{0,4},{1,5},{2,6},{3,7},{4,0},{5,1},{6,2},{7,3},{8,12},{9,13},{10,... | collective-permute-start | bytes 6291464 | tf_op jit(solution)/shard_map/ppermute | solution.py:124
  2296.9 76.3 %collective-permute-start.39 = (bf16[64,1024]{1,0:T(8,128)(2,1)S(1)}, bf16[64,1024]{1,0:T(8,128)(2,1)S(1)}, u32[]{:S(2)}, u32[]{:S(2)}) collective-permute-start(bf16[64,1024]{1,0:T(8,128)(2,1)S(1)} %fusion.183), channel_id=1, source_target_pairs={{0,8},{1,9},{2,10},{3,11},{4,12},{5,13},{6,14},{7,15},{8,0},{9,1},... | collective-permute-start | bytes 393224 | tf_op jit(solution)/shard_map/ppermute | solution.py:124
  2299.6 75.2 %collective-permute-start.31 = (bf16[64,1024]{1,0:T(8,128)(2,1)S(1)}, bf16[64,1024]{1,0:T(8,128)(2,1)S(1)}, u32[]{:S(2)}, u32[]{:S(2)}) collective-permute-start(bf16[64,1024]{1,0:T(8,128)(2,1)S(1)} %fusion.181), channel_id=1, source_target_pairs={{0,2},{1,3},{2,0},{3,1},{4,6},{5,7},{6,4},{7,5},{8,10},{9,11},{10,... | collective-permute-start | bytes 393224 | tf_op jit(solution)/shard_map/ppermute | solution.py:124
  (210 other events, 6095.2 us)
Sparse Core Ops, SparseCore 0:
  10.3 58.7 all-gather.10
  71.3 49.4 all-gather.12
  123.1 76.6 all-gather.8
  1954.0 64.0 all-reduce.7
  2020.8 56.1 reduce-scatter.6
  2079.2 70.6 reduce-scatter.4
  2152.2 98.3 reduce-scatter.10
  2252.9 106.7 reduce-scatter.8

commit v2 on v0

v2 whole, which is shorter than its diff:
```python
import functools, math
import jax
import jax.numpy as jnp
from jax import lax
from jax.experimental import pallas as pl
from jax.experimental.pallas import tpu as pltpu
from jax.sharding import PartitionSpec as P

HEAD_DIM = 64
SEQ = 1024
QT = 256
RB = 64
PAIR = 2 * HEAD_DIM
NEG_BIG = -1e30
NN = (((1,), (0,)), ((), ()))
NT = (((1,), (1,)), ((), ()))
TN = (((0,), (0,)), ((), ()))


def dot(a, b, dims):
    return lax.dot_general(a, b, dims, preferred_element_type=jnp.float32)


def lane_iota(rows):
    return lax.broadcasted_iota(jnp.int32, (rows, PAIR), 1)


def attn_fwd_kernel(len_ref, q_ref, k_ref, v_ref, ctx_ref, p_ref, ka_ref, qa_ref, vt_ref, e_ref, top_ref, sum_ref, ctxt_ref):
    seq_len = len_ref[pl.program_id(0)]
    lane = lane_iota(1)
    hidden_key = lax.broadcasted_iota(jnp.int32, (SEQ, PAIR), 0) >= seq_len
    for h in range(2):
        mine = (lane // HEAD_DIM) == h
        aux = lane == (1 - h) * HEAD_DIM
        own = mine.astype(jnp.float32).astype(jnp.bfloat16)
        one = aux.astype(jnp.float32).astype(jnp.bfloat16)
        bar = jnp.where(aux, NEG_BIG, 0.0).astype(jnp.bfloat16)
        ka_ref[h] = jnp.where(hidden_key, jnp.broadcast_to(bar, (SEQ, PAIR)), k_ref[...] * own)
        qa_ref[h] = q_ref[...] * own + one
    vt_ref[...] = v_ref[...].T
    def at(t):
        return pl.ds(pl.multiple_of(t * QT, QT), QT)

    def fold(x, op):
        while x.shape[0] > 8:
            half = x.shape[0] // 2
            x = op(x[:half], x[half:])
        return x

    def spread(x):
        return jnp.concatenate([x] * (RB // 8), axis=0)

    def rise(t, h):
        s = dot(ka_ref[h], qa_ref[h, at(t)], NT)
        for c in range(SEQ // RB):
            part = s[c * RB:(c + 1) * RB]
            top = fold(part, jnp.maximum)
            e = jnp.exp(part - spread(top))
            e_ref[h, c * RB:(c + 1) * RB] = e
            top_ref[h, c * 8:(c + 1) * 8] = top
            sum_ref[h, c * 8:(c + 1) * 8] = fold(e, jnp.add)

    def settle(t, h):
        tops = top_ref[h]
        weight = jnp.exp(tops - jnp.max(tops, axis=0, keepdims=True))
        scale = weight * (1.0 / jnp.sum(weight * sum_ref[h], axis=0, keepdims=True))
        for c in range(SEQ // RB):
            p_ref[h, c * RB:(c + 1) * RB, at(t)] = (e_ref[h, c * RB:(c + 1) * RB] * spread(scale[c * 8:(c + 1) * 8])).astype(jnp.bfloat16)
        rows = slice(h * HEAD_DIM, (h + 1) * HEAD_DIM)
        ctxt_ref[rows, at(t)] = dot(vt_ref[rows], p_ref[h, :, at(t)], NN)

    last = SEQ // QT - 1
    rise(0, 0)

    def turn(t, _):
        settle(t, 0)
        rise(t, 1)
        rise(jnp.minimum(t + 1, last), 0)
        settle(t, 1)
        return 0

    lax.fori_loop(0, SEQ // QT, turn, 0)
    ctx_ref[...] = ctxt_ref[...].T.astype(jnp.bfloat16)


def attn_fwd(lengths, q, k, v):
    tokens, width = q.shape
    seqs, pairs = tokens // SEQ, width // PAIR
    spec = pl.BlockSpec((SEQ, PAIR), lambda b, h, n: (b, h))
    return pl.pallas_call(
        attn_fwd_kernel,
        grid_spec=pltpu.PrefetchScalarGridSpec(
            num_scalar_prefetch=1, grid=(seqs, pairs),
            in_specs=[spec, spec, spec],
            out_specs=[spec, pl.BlockSpec((None, 2, SEQ, SEQ), lambda b, h, n: (b, h, 0, 0))],
            scratch_shapes=[pltpu.VMEM((2, SEQ, PAIR), jnp.bfloat16), pltpu.VMEM((2, SEQ, PAIR), jnp.bfloat16),
                            pltpu.VMEM((PAIR, SEQ), jnp.bfloat16), pltpu.VMEM((2, SEQ, QT), jnp.float32), pltpu.VMEM((2, SEQ // RB * 8, QT), jnp.float32), pltpu.VMEM((2, SEQ // RB * 8, QT), jnp.float32),
                            pltpu.VMEM((PAIR, SEQ), jnp.float32)]),
        out_shape=[jax.ShapeDtypeStruct((tokens, width), jnp.bfloat16),
                   jax.ShapeDtypeStruct((seqs, 2 * pairs, SEQ, SEQ), jnp.bfloat16)],
        compiler_params=pltpu.CompilerParams(dimension_semantics=("arbitrary", "arbitrary"), vmem_limit_bytes=56 << 20),
        cost_estimate=pl.CostEstimate(flops=4 * tokens * SEQ * width * 4, bytes_accessed=90 << 20, transcendentals=tokens * SEQ * 16),
        name='attn_fwd',
    )(lengths, q, k, v)


def spin(x, cos, sin, sign):
    half = HEAD_DIM // 2
    low = (lax.broadcasted_iota(jnp.int32, x.shape, 1) % HEAD_DIM) < half
    other = jnp.where(low, pltpu.roll(x, PAIR - half, 1), pltpu.roll(x, half, 1))
    return x * cos + other * (sin * sign)


def attn_bwd_kernel(len_ref, q_ref, k_ref, v_ref, o_ref, do_ref, p_ref, cos_ref, sin_ref, dq_ref, dk_ref, dv_ref,
                    doh_ref, qh_ref, kt_ref, d_ref, ds_ref, dqt_ref):
    lane = lane_iota(1)
    for h in range(2):
        own = ((lane // HEAD_DIM) == h).astype(jnp.float32).astype(jnp.bfloat16)
        doh_ref[h] = do_ref[...] * own
        qh_ref[h] = q_ref[...] * own
    kt_ref[...] = k_ref[...].T
    prod = (do_ref[...].astype(jnp.float32) * o_ref[...].astype(jnp.float32)).T
    for h in range(2):
        d_ref[h:h + 1] = jnp.sum(prod[h * HEAD_DIM:(h + 1) * HEAD_DIM], axis=0, keepdims=True)
    for h in range(2):
        for t in range(SEQ // QT):
            cols = slice(t * QT, (t + 1) * QT)
            dp = dot(v_ref[...], doh_ref[h, cols], NT)
            ds_ref[h, :, cols] = (p_ref[h, :, cols].astype(jnp.float32) * (dp - d_ref[h:h + 1, cols])).astype(jnp.bfloat16)
    dv_ref[...] = (dot(p_ref[0], doh_ref[0], NN) + dot(p_ref[1], doh_ref[1], NN)).astype(jnp.bfloat16)
    for h in range(2):
        dqt_ref[h * HEAD_DIM:(h + 1) * HEAD_DIM] = dot(kt_ref[h * HEAD_DIM:(h + 1) * HEAD_DIM], ds_ref[h], NN)
    dk = dot(ds_ref[0], qh_ref[0], NN) + dot(ds_ref[1], qh_ref[1], NN)
    dk_ref[...] = spin(dk, cos_ref[...], sin_ref[...], -1.0).astype(jnp.bfloat16)
    dq_ref[...] = (spin(dqt_ref[...].T, cos_ref[...], sin_ref[...], -1.0) * (HEAD_DIM ** -0.5)).astype(jnp.bfloat16)


def attn_bwd(lengths, q, k, v, ctx, d_ctx, probs, cos_tab, sin_tab):
    tokens, width = q.shape
    seqs, pairs = tokens // SEQ, width // PAIR
    spec = pl.BlockSpec((SEQ, PAIR), lambda b, h, n: (b, h))
    table = pl.BlockSpec((SEQ, PAIR), lambda b, h, n: (0, 0))
    return pl.pallas_call(
        attn_bwd_kernel,
        grid_spec=pltpu.PrefetchScalarGridSpec(
            num_scalar_prefetch=1, grid=(seqs, pairs),
            in_specs=[spec] * 5 + [pl.BlockSpec((None, 2, SEQ, SEQ), lambda b, h, n: (b, h, 0, 0)), table, table],
            out_specs=[spec] * 3,
            scratch_shapes=[pltpu.VMEM((2, SEQ, PAIR), jnp.bfloat16), pltpu.VMEM((2, SEQ, PAIR), jnp.bfloat16),
                            pltpu.VMEM((PAIR, SEQ), jnp.bfloat16), pltpu.VMEM((8, SEQ), jnp.float32),
                            pltpu.VMEM((2, SEQ, SEQ), jnp.bfloat16), pltpu.VMEM((PAIR, SEQ), jnp.float32)]),
        out_shape=[jax.ShapeDtypeStruct((tokens, width), jnp.bfloat16)] * 3,
        compiler_params=pltpu.CompilerParams(dimension_semantics=("arbitrary", "arbitrary"), vmem_limit_bytes=56 << 20),
        cost_estimate=pl.CostEstimate(flops=8 * tokens * SEQ * width * 4, bytes_accessed=100 << 20, transcendentals=0),
        name='attn_bwd',
    )(lengths, q, k, v, ctx, d_ctx, probs, cos_tab, sin_tab)


EPS = 1e-5
THETA = 10000.0
HIGH = 60 << 20


def whole(shape):
    return pl.BlockSpec(shape, lambda *i: (0,) * len(shape), pipeline_mode=pl.Buffered(1))


def partial(shape):
    return pl.BlockSpec(shape, lambda *i: (0,) * len(shape))


def rows_of(block, width):
    return pl.BlockSpec((block, width), lambda i: (i, 0))


def params(*semantics):
    return pltpu.CompilerParams(dimension_semantics=semantics or ('arbitrary',), vmem_limit_bytes=HIGH)


def cost(flops, moved):
    return pl.CostEstimate(flops=flops, bytes_accessed=moved, transcendentals=0)


def normal(x):
    mean = jnp.mean(x, axis=-1, keepdims=True)
    centered = x - mean
    inv = lax.rsqrt(jnp.mean(centered * centered, axis=-1, keepdims=True) + EPS)
    return centered * inv, inv


def norm_back(x, gain, grad):
    unit, inv = normal(x)
    scaled = grad * gain
    inner = scaled - jnp.mean(scaled, axis=-1, keepdims=True) - unit * jnp.mean(scaled * unit, axis=-1, keepdims=True)
    return inv * inner, unit


def eights(x):
    return jnp.sum(x.reshape(x.shape[0] // 8, 8, x.shape[1]), axis=0)


def add_up(ref, value):
    first = pl.program_id(0) == 0

    @pl.when(first)
    def _():
        ref[...] = value

    @pl.when(jnp.logical_not(first))
    def _():
        ref[...] += value


def qkv_kernel(x_ref, w_ref, b_ref, ln_ref, cos_ref, sin_ref, h_ref, q_ref, k_ref, v_ref):
    unit, _ = normal(x_ref[...].astype(jnp.float32))
    h_ref[...] = (unit * ln_ref[0:1] + ln_ref[1:2]).astype(jnp.bfloat16)
    for j, out_ref in enumerate((q_ref, k_ref, v_ref)):
        full = dot(h_ref[...], w_ref[j], NN) + b_ref[j:j + 1]
        if j == 2:
            out_ref[...] = full.astype(jnp.bfloat16)
            continue
        if j == 0:
            full = full * (HEAD_DIM ** -0.5)
        for c in range(0, full.shape[1], PAIR):
            out_ref[:, c:c + PAIR] = spin(full[:, c:c + PAIR], cos_ref[...], sin_ref[...], 1.0).astype(jnp.bfloat16)


def qkv(x, w, b, ln, cos, sin):
    tokens, width = x.shape
    block = 512
    row = rows_of(block, width)
    table = pl.BlockSpec((block, PAIR), lambda i: (i % (SEQ // block), 0))
    return pl.pallas_call(
        qkv_kernel, grid=(tokens // block,),
        in_specs=[row, whole(w.shape), whole(b.shape), whole(ln.shape), table, table],
        out_specs=[row] * 4,
        out_shape=[jax.ShapeDtypeStruct(x.shape, jnp.bfloat16)] * 4,
        compiler_params=params(), cost_estimate=cost(6 * tokens * width * width, 26 << 20), name='qkv',
    )(x, w, b, ln, cos, sin)


def out_kernel(ctx_ref, x_ref, w_ref, b_ref, ln_ref, mid_ref, h_ref):
    mid = (x_ref[...].astype(jnp.float32) + dot(ctx_ref[...], w_ref[...], NN) + b_ref[...]).astype(jnp.bfloat16)
    mid_ref[...] = mid
    unit, _ = normal(mid.astype(jnp.float32))
    h_ref[...] = (unit * ln_ref[2:3] + ln_ref[3:4]).astype(jnp.bfloat16)


def out_proj(ctx, x, w, b, ln):
    tokens, width = x.shape
    block = 512
    row = rows_of(block, width)
    return pl.pallas_call(
        out_kernel, grid=(tokens // block,),
        in_specs=[row, row, whole(w.shape), whole(b.shape), whole(ln.shape)], out_specs=[row] * 2,
        out_shape=[jax.ShapeDtypeStruct(x.shape, jnp.bfloat16)] * 2,
        compiler_params=params(), cost_estimate=cost(2 * tokens * width * width, 18 << 20), name='out_proj',
    )(ctx, x, w, b, ln)


def mlp_kernel(h_ref, mid_ref, wu_ref, bu_ref, wd_ref, bd_ref, act_ref, slope_ref, y_ref):
    total = mid_ref[...].astype(jnp.float32) + bd_ref[...]
    wide = wu_ref.shape[1]
    for c in range(0, wide, 1024):
        cols = slice(c, c + 1024)
        pre = dot(h_ref[...], wu_ref[:, cols], NN) + bu_ref[:, cols]
        cdf = 0.5 + 0.5 * lax.erf(pre * (1.0 / math.sqrt(2.0)))
        act_ref[:, cols] = (pre * cdf).astype(jnp.bfloat16)
        slope_ref[:, cols] = cdf + pre * (jnp.exp(-0.5 * pre * pre) * (1.0 / math.sqrt(2.0 * math.pi)))
        total = total + dot(act_ref[:, cols], wd_ref[cols], NN)
    y_ref[...] = total.astype(jnp.bfloat16)


def mlp(h, mid, wu, bu, wd, bd):
    tokens, width = h.shape
    wide = wu.shape[1]
    block = 256
    row, long = rows_of(block, width), rows_of(block, wide)
    return pl.pallas_call(
        mlp_kernel, grid=(tokens // block,),
        in_specs=[row, row, whole(wu.shape), whole(bu.shape), whole(wd.shape), whole(bd.shape)],
        out_specs=[long, long, row],
        out_shape=[jax.ShapeDtypeStruct((tokens, wide), jnp.bfloat16), jax.ShapeDtypeStruct((tokens, wide), jnp.float32),
                   jax.ShapeDtypeStruct(h.shape, jnp.bfloat16)],
        compiler_params=params(), cost_estimate=cost(4 * tokens * width * wide, 80 << 20), name='mlp',
    )(h, mid, wu, bu, wd, bd)


def mlp_back_kernel(dy_ref, slope_ref, wd_ref, wu_ref, mid_ref, ln_ref, wo_ref,
                    dpre_ref, dmid_ref, dctx_ref, gbu_ref, gln_ref):
    dy = dy_ref[...]
    grad = None
    wide = wu_ref.shape[1]
    first = pl.program_id(0) == 0

    @pl.when(first)
    def _():
        gbu_ref[...] = jnp.zeros_like(gbu_ref)
        gln_ref[...] = jnp.zeros_like(gln_ref)

    for c in range(0, wide, 1024):
        cols = slice(c, c + 1024)
        dpre = dot(dy, wd_ref[cols], NT) * slope_ref[:, cols]
        gbu_ref[:, cols] += eights(dpre)
        dpre_ref[:, cols] = dpre.astype(jnp.bfloat16)
        part = dot(dpre_ref[:, cols], wu_ref[:, cols], NT)
        grad = part if grad is None else grad + part
    dy = dy.astype(jnp.float32)
    back, unit = norm_back(mid_ref[...].astype(jnp.float32), ln_ref[2:3], grad)
    dmid = (dy + back).astype(jnp.bfloat16)
    dmid_ref[...] = dmid
    gln_ref[0:8] += eights(grad * unit)
    gln_ref[8:16] += eights(grad)
    gln_ref[16:24] += eights(dmid.astype(jnp.float32))
    gln_ref[24:32] += eights(dy)
    dctx_ref[...] = dot(dmid, wo_ref[...], NT).astype(jnp.bfloat16)


def mlp_back(dy, slope, wd, wu, mid, ln, wo):
    tokens, width = dy.shape
    wide = wu.shape[1]
    block = 256
    row, long = rows_of(block, width), rows_of(block, wide)
    half = jax.ShapeDtypeStruct(dy.shape, jnp.bfloat16)
    return pl.pallas_call(
        mlp_back_kernel, grid=(tokens // block,),
        in_specs=[row, long, whole(wd.shape), whole(wu.shape), row, whole(ln.shape), whole(wo.shape)],
        out_specs=[long, row, row, partial((8, wide)), partial((32, width))],
        out_shape=[jax.ShapeDtypeStruct((tokens, wide), jnp.bfloat16), half, half,
                   jax.ShapeDtypeStruct((8, wide), jnp.float32), jax.ShapeDtypeStruct((32, width), jnp.float32)],
        compiler_params=params(), cost_estimate=cost(2 * tokens * width * (2 * wide + width), 90 << 20), name='mlp_back',
    )(dy, slope, wd, wu, mid, ln, wo)


def in_back_kernel(dq_ref, dk_ref, dv_ref, w_ref, x_ref, ln_ref, dmid_ref, dx_ref, gln_ref):
    @pl.when(pl.program_id(0) == 0)
    def _():
        gln_ref[...] = jnp.zeros_like(gln_ref)

    grad = dot(dq_ref[...], w_ref[0], NT) + dot(dk_ref[...], w_ref[1], NT) + dot(dv_ref[...], w_ref[2], NT)
    back, unit = norm_back(x_ref[...].astype(jnp.float32), ln_ref[0:1], grad)
    dx_ref[...] = (dmid_ref[...].astype(jnp.float32) + back).astype(jnp.bfloat16)
    gln_ref[0:8] += eights(grad * unit)
    gln_ref[8:16] += eights(grad)


def in_back(dq, dk, dv, w, x, ln, dmid):
    tokens, width = x.shape
    block = 512
    row = rows_of(block, width)
    return pl.pallas_call(
        in_back_kernel, grid=(tokens // block,),
        in_specs=[row, row, row, whole(w.shape), row, whole(ln.shape), row],
        out_specs=[row, partial((16, width))],
        out_shape=[jax.ShapeDtypeStruct(x.shape, jnp.bfloat16), jax.ShapeDtypeStruct((16, width), jnp.float32)],
        compiler_params=params(), cost_estimate=cost(6 * tokens * width * width, 34 << 20), name='in_back',
    )(dq, dk, dv, w, x, ln, dmid)


def grad_kernel(a_ref, b_ref, g_ref):
    g_ref[...] = dot(a_ref[...], b_ref[...], TN).astype(jnp.bfloat16)


def weight_grad(a, b, name, tall):
    tokens, m = a.shape
    n = b.shape[1]
    block = 512
    if tall:
        grid, a_spec, b_spec = (m // block,), pl.BlockSpec((tokens, block), lambda i: (0, i)), whole(b.shape)
        out = pl.BlockSpec((block, n), lambda i: (i, 0))
    else:
        grid, a_spec, b_spec = (n // block,), whole(a.shape), pl.BlockSpec((tokens, block), lambda i: (0, i))
        out = pl.BlockSpec((m, block), lambda i: (0, i))
    return pl.pallas_call(
        grad_kernel, grid=grid, in_specs=[a_spec, b_spec], out_specs=out,
        out_shape=jax.ShapeDtypeStruct((m, n), jnp.bfloat16),
        compiler_params=params(), cost_estimate=cost(2 * tokens * m * n, 2 * (tokens * (m + n) + m * n)), name=name,
    )(a, b)


def qkv_grad_kernel(h_ref, dq_ref, dk_ref, dv_ref, g_ref, gb_ref):
    for j, d_ref in enumerate((dq_ref, dk_ref, dv_ref)):
        g_ref[j] = dot(h_ref[...], d_ref[...], TN).astype(jnp.bfloat16)
        gb_ref[8 * j:8 * j + 8] = eights(d_ref[...].astype(jnp.float32))


def qkv_grad(h, dq, dk, dv):
    tokens, width = h.shape
    block = 256
    cols = pl.BlockSpec((tokens, block), lambda i: (0, i))
    return pl.pallas_call(
        qkv_grad_kernel, grid=(width // block,),
        in_specs=[whole(h.shape), cols, cols, cols],
        out_specs=[pl.BlockSpec((3, width, block), lambda i: (0, 0, i)), pl.BlockSpec((24, block), lambda i: (0, i))],
        out_shape=[jax.ShapeDtypeStruct((3, width, width), jnp.bfloat16), jax.ShapeDtypeStruct((24, width), jnp.float32)],
        compiler_params=params(), cost_estimate=cost(6 * tokens * width * width, 24 << 20), name='qkv_grad',
    )(h, dq, dk, dv)


def rotary_tables():
    half = HEAD_DIM // 2
    inv_freq = 1.0 / (THETA ** (jnp.arange(half, dtype=jnp.float32) * (2.0 / HEAD_DIM)))
    angles = jnp.arange(SEQ, dtype=jnp.float32)[:, None] * inv_freq[None, :]
    cos, sin = jnp.cos(angles), jnp.sin(angles)
    return jnp.concatenate([cos] * 4, axis=1), jnp.concatenate([-sin, sin, -sin, sin], axis=1)


BITS = {'c': 1, 'x': 2, 'y': 4, 'z': 8}


def swap(value, axis_name, dim):
    return lax.ppermute(value, axis_name, [(i, i ^ BITS[dim]) for i in range(16)])


def bit_of(axis_name, dim):
    return (lax.axis_index(axis_name) // BITS[dim]) % 2


def gather_packed(packed, axis_name):
    held = packed[None]
    for dim in ('c', 'x', 'y', 'z'):
        got = swap(held, axis_name, dim)
        mine = bit_of(axis_name, dim)
        held = jnp.where(mine == 0, jnp.concatenate([held, got]), jnp.concatenate([got, held]))
    return held


def scatter_packed(full, axis_name):
    cur = full
    for dim in ('z', 'y', 'x', 'c'):
        mine = bit_of(axis_name, dim)
        half = cur.shape[0] // 2
        low, high = cur[:half], cur[half:]
        give = jnp.where(mine == 0, high, low)
        keep = jnp.where(mine == 0, low, high)
        cur = keep + swap(give, axis_name, dim)
    return cur[0]


def pack_params(b_attn, ln_par, b_up, b_down):
    layers = b_attn.shape[0]
    flat = jnp.concatenate([b_attn.reshape(layers, -1), ln_par.reshape(layers, -1), b_up, b_down], axis=1)
    return flat


def unpack_params(full, layer, n, nu):
    part = full[:, layer].astype(jnp.float32)
    b_attn = part[:, :4 * n].reshape(16, 4, n).transpose(1, 0, 2).reshape(4, 16 * n)
    ln = part[:, 4 * n:8 * n].reshape(16, 4, n).transpose(1, 0, 2).reshape(4, 16 * n)
    b_up = part[:, 8 * n:8 * n + nu].reshape(1, 16 * nu)
    b_down = part[:, 8 * n + nu:].reshape(1, 16 * n)
    return b_attn, ln, b_up, b_down


def solution(mesh):
    axis_name = mesh.axis_names[0]
    batch_spec = P(axis_name)
    weight_specs = (P(None, None, axis_name, None), P(None, None, axis_name), P(None, None, axis_name),
                    P(None, axis_name, None), P(None, axis_name), P(None, axis_name, None), P(None, axis_name))

    def device_step(x, lengths, d_y, w_attn, b_attn, ln_par, w_up, b_up, w_down, b_down):
        layers = w_attn.shape[0]
        seqs, seq_len, width = x.shape
        tokens = seqs * seq_len
        n, nu = b_attn.shape[2], b_up.shape[1]
        cos, sin = rotary_tables()
        gather = functools.partial(lax.all_gather, axis_name=axis_name, tiled=True)
        scatter = functools.partial(lax.psum_scatter, axis_name=axis_name, tiled=True)
        small = gather_packed(pack_params(b_attn, ln_par, b_up, b_down), axis_name)
        hidden = x.reshape(tokens, width)
        saved = []
        for l in range(layers):
            ba, ln, bu, bd = unpack_params(small, l, n, nu)
            wqkv = gather(w_attn[l, :3], axis=1)
            wo = gather(w_attn[l, 3], axis=0)
            wu = gather(w_up[l], axis=0)
            wd = gather(w_down[l], axis=0)
            h_one, q, k, v = qkv(hidden, wqkv, ba[:3], ln, cos, sin)
            ctx, probs = attn_fwd(lengths, q, k, v)
            mid, h_two = out_proj(ctx, hidden, wo, ba[3:4], ln)
            act, slope, out = mlp(h_two, mid, wu, bu, wd, bd)
            saved.append((hidden, h_one, q, k, v, ctx, probs, mid, h_two, act, slope, wqkv, wo, wu, wd, ln))
            hidden = out
        grad = d_y.reshape(tokens, width)
        grads = [None] * layers
        for l in reversed(range(layers)):
            x_in, h_one, q, k, v, ctx, probs, mid, h_two, act, slope, wqkv, wo, wu, wd, ln = saved[l]
            after = lax.optimization_barrier
            gw_down, grad = after((weight_grad(act, grad, 'down_grad', True), grad))
            g_down = scatter(gw_down, scatter_dimension=0)
            d_pre, d_mid, d_ctx, gb_up, gln_two = mlp_back(grad, slope, wd, wu, mid, ln, wo)
            if l + 1 < layers:
                above, h_two = after((grads[l + 1][0], h_two))
                grads[l + 1] = (above,) + grads[l + 1][1:]
            gw_up, gw_out, d_ctx = after((weight_grad(h_two, d_pre, 'up_grad', False), weight_grad(ctx, d_mid, 'out_grad', False), d_ctx))
            g_up = scatter(gw_up, scatter_dimension=0)
            g_out = scatter(gw_out, scatter_dimension=0)
            dq, dk, dv = attn_bwd(lengths, q, k, v, ctx, d_ctx, probs, cos, sin)
            g_down, dq = after((g_down, dq))
            gw, gb_qkv = qkv_grad(h_one, dq, dk, dv)
            gw, dq, g_up = after((gw, dq, g_up))
            g_qkv = scatter(gw, scatter_dimension=1)
            grad, gln_one = in_back(dq, dk, dv, wqkv, x_in, ln, d_mid)
            g_out, grad = after((g_out, grad))
            sums_two = jnp.sum(gln_two.reshape(4, 8, width), axis=1)
            sums_one = jnp.sum(gln_one.reshape(2, 8, width), axis=1)
            gb_three = jnp.sum(gb_qkv.reshape(3, 8, width), axis=1)
            gb_wide = jnp.sum(gb_up, axis=0)
            by_dev = lambda s: s.reshape(-1, 16, n).transpose(1, 0, 2).reshape(16, -1)
            packed = jnp.concatenate([by_dev(gb_three), by_dev(sums_two[2:3]), by_dev(sums_one), by_dev(sums_two[:2]),
                                      gb_wide.reshape(16, nu), by_dev(sums_two[3:4])], axis=1)
            grads[l] = ((g_qkv, g_out), g_up, g_down, packed)
        got = scatter_packed(jnp.stack([g[3] for g in grads], axis=1), axis_name)
        f32 = lambda g: g.astype(jnp.float32)
        g_attn = jnp.stack([jnp.concatenate([f32(g[0][0]), f32(g[0][1])[None]]) for g in grads])
        g_up = jnp.stack([f32(g[1]) for g in grads])
        g_down = jnp.stack([f32(g[2]) for g in grads])
        return (grad.reshape(x.shape), g_attn, got[:, :4 * n].reshape(layers, 4, n), got[:, 4 * n:8 * n].reshape(layers, 4, n),
                g_up, got[:, 8 * n:8 * n + nu], g_down, got[:, 8 * n + nu:])

    return jax.shard_map(device_step, mesh=mesh,
                         in_specs=(batch_spec, batch_spec, batch_spec) + weight_specs,
                         out_specs=(batch_spec,) + weight_specs,
                         check_vma=False)
```

time: 3130 us -> 1100 us (0.35)
  matrix products: 1080 us -> 0 us
  Pallas kernels: 0 us -> 807 us
  waiting for transfers between devices: 931 us -> 231 us
  other arithmetic: 649 us -> 11.2 us
  local copies, waits for them, and re-layouts: 271 us -> 18.5 us
  blocking collectives: 172 us -> 0 us
    dot_general x33 -> x0, matrix products: 968 us -> none  [the longest x2 143 us: layer_backward(): jnp.einsum('bqhd,bkhd->bhqk', d_context, values, preferred_element_type=j...]
    pallas_call x0 -> x22, Pallas kernels: none -> 807 us  [the longest x2 165 us: attn_bwd(): pl.pallas_call(attn_bwd_kernel, grid_spec=pltpu.PrefetchScalarGridSpec(nu...]
    reduce_scatter x4 -> x8, waiting for transfers between devices: 704 us -> 162 us  [the longest x2 70.1 us: device_step(): g_qkv = scatter(gw, scatter_dimension=1)]
    convert_element_type x20 -> x1, other arithmetic: 494 us -> 0.08 us  [unpack_params(): part = full[:, layer].astype(jnp.float32)]
    unnamed x29 -> x16, waiting for transfers between devices: 185 us -> 3.83 us
    sub x2 -> x0, matrix products: 107 us -> none  [layer_forward(): jax.nn.softmax(jnp.where(key_valid, scores, NEG_BIG), axis=-1)]
    all_gather x8 -> x0, blocking collectives: 106 us -> none  [the longest x4 50.9 us: gather_layer(): lax.all_gather(ln_par, axis_name, axis=1, tiled=True)]
    unnamed x256 -> x41, local copies, waits for them, and re-layouts: 95.8 us -> 1.32 us
  transfers between devices with their start and end apart: 22 -> 24, of which waited for: 7 -> 13; matrix products, arithmetic and copies ran while one was open for 51% -> 2% of each run, Pallas kernels for 0% -> 67%
where the time goes in v2:
time: 1100 us; the launch traced here: 1090 us
  Pallas kernels  807 us (73%)
  waiting for transfers between devices  231 us (21%)
  local copies, waits for them, and re-layouts  18.5 us (2%)
  between operations  15 us (1%)
  other arithmetic  11.2 us (1%)
    pallas_call x2, Pallas kernels, attn_bwd(): pl.pallas_call(attn_bwd_kernel, grid_spec=pltpu.PrefetchScalarGridSpec(nu...  165 us
    pallas_call x2, Pallas kernels, attn_fwd(): pl.pallas_call(attn_fwd_kernel, grid_spec=pltpu.PrefetchScalarGridSpec(nu...  152 us
    pallas_call x2, Pallas kernels, mlp(): pl.pallas_call(mlp_kernel, grid=(tokens // block,), in_specs=[row, row, w...  116 us
    pallas_call x2, Pallas kernels, mlp_back(): pl.pallas_call(mlp_back_kernel, grid=(tokens // block,), in_specs=[row, l...  113 us
    pallas_call x6, Pallas kernels, weight_grad(): pl.pallas_call(grad_kernel, grid=grid, in_specs=[a_spec, b_spec], out_spe...  109 us
    reduce_scatter x2, waiting for transfers between devices, device_step(): g_qkv = scatter(gw, scatter_dimension=1)  70.1 us
    pallas_call x2, Pallas kernels, in_back(): pl.pallas_call(in_back_kernel, grid=(tokens // block,), in_specs=[row, ro...  48.4 us
    reduce_scatter x2, waiting for transfers between devices, device_step(): g_up = scatter(gw_up, scatter_dimension=0)  46.1 us
  transfers between devices with their start and end apart: 24, of which 13 were waited for; matrix products, arithmetic and copies ran while one was open for 2% of the time, Pallas kernels for 67%

profile of v2, /device:TPU:0, one launch (start us, length us, event | category | flops | bytes accessed | tf_op | source)
XLA Modules:
  0.0 1092.3 jit_solution(1190644427831614627)
XLA Ops:
  39.8 16.1 %all-gather.17.cloned.1.call-done = bf16[1,3,1024,1024]{3,2,1,0:T(8,128)(2,1)} async-done(((bf16[1,3,64,1024]{3,2,1,0:T(8,128)(2,1)}), bf16[1,3,1024,1024]{3,2,1,0:T(8,128)(2,1)}) %all-gather.17.cloned.1.call-update) | async-done | bytes 6291472 | tf_op jit(solution)/shard_map/all_gather | solution.py:474
  55.9 20.3 %qkv.2 = (bf16[2048,1024]{1,0:T(8,128)(2,1)}, bf16[2048,1024]{1,0:T(8,128)(2,1)}, bf16[2048,1024]{1,0:T(8,128)(2,1)}, bf16[2048,1024]{1,0:T(8,128)(2,1)}) custom-call(bf16[2048,1024]{1,0:T(8,128)(2,1)} %bitcast.105, bf16[3,1024,1024]{2,1,0:T(8,128)(2,1)} %bitcast.99, f32[3,1024]{1,0:T(4,128)} %slice.136.b_ref, f32[4,1024]{1,0:T(4,128)} %reshape.148.ln_ref, ...), custom_call_target="tpu_custom_call" | custom-call | flops 12884901888 | bytes 27262976 | tf_op jit(solution)/shard_map/qkv/pallas_call | solution.py:233
  76.1 76.2 %attn_fwd.2 = (bf16[2048,1024]{1,0:T(8,128)(2,1)}, bf16[2,16,1024,1024]{3,2,1,0:T(8,128)(2,1)}) custom-call(s32[2]{0:T(128)} %len_ref.7, bf16[2048,1024]{1,0:T(8,128)(2,1)} %get-tuple-element.80.q_ref, bf16[2048,1024]{1,0:T(8,128)(2,1)} %get-tuple-element.81.k_ref, bf16[2048,1024]{1,0:T(8,128)(2,1)} %get-tuple-element.82.v_ref), custom_call_target="tpu_custom_call" | custom-call | flops 34359738368 | bytes 94371840 | tf_op jit(solution)/shard_map/attn_fwd/pallas_call | solution.py:90
  163.6 25.1 %all-gather.23.cloned.1.call-done = bf16[1,4096,1024]{2,1,0:T(8,128)(2,1)} async-done(((bf16[1,256,1024]{2,1,0:T(8,128)(2,1)}), bf16[1,4096,1024]{2,1,0:T(8,128)(2,1)}) %all-gather.23.cloned.1.call-update) | async-done | bytes 8388624 | tf_op jit(solution)/shard_map/all_gather | solution.py:477
  188.7 58.0 %mlp.2 = (bf16[2048,4096]{1,0:T(8,128)(2,1)}, f32[2048,4096]{1,0:T(8,128)}, bf16[2048,1024]{1,0:T(8,128)(2,1)}) custom-call(bf16[2048,1024]{1,0:T(8,128)(2,1)} %get-tuple-element.114.h_ref.a_ref, bf16[2048,1024]{1,0:T(8,128)(2,1)} %get-tuple-element.85.mid_ref, bf16[1024,4096]{1,0:T(8,128)(2,1)} %bitcast.91, f32[1,4096]{1,0:T(1,128)} %bitcast.90, ...), custom_call_target="tpu_custom_call" | custom-call | flops 34359738368 | bytes 83886080 | tf_op jit(solution)/shard_map/mlp/pallas_call | solution.py:279
  246.7 20.2 %qkv.3 = (bf16[2048,1024]{1,0:T(8,128)(2,1)}, bf16[2048,1024]{1,0:T(8,128)(2,1)}, bf16[2048,1024]{1,0:T(8,128)(2,1)}, bf16[2048,1024]{1,0:T(8,128)(2,1)}) custom-call(bf16[2048,1024]{1,0:T(8,128)(2,1)} %get-tuple-element.86.x_ref, bf16[3,1024,1024]{2,1,0:T(8,128)(2,1)} %bitcast.101, f32[3,1024]{1,0:T(4,128)} %slice.149.b_ref, f32[4,1024]{1,0:T(4,128)} %reshape.153.ln_ref, ...), custom_call_target="tpu_custom_call" | custom-call | flops 12884901888 | bytes 27262976 | tf_op jit(solution)/shard_map/qkv/pallas_call | solution.py:233
  266.9 76.3 %attn_fwd.3 = (bf16[2048,1024]{1,0:T(8,128)(2,1)}, bf16[2,16,1024,1024]{3,2,1,0:T(8,128)(2,1)}) custom-call(s32[2]{0:T(128)} %len_ref.7, bf16[2048,1024]{1,0:T(8,128)(2,1)} %get-tuple-element.88.q_ref, bf16[2048,1024]{1,0:T(8,128)(2,1)} %get-tuple-element.89.k_ref, bf16[2048,1024]{1,0:T(8,128)(2,1)} %get-tuple-element.90.v_ref), custom_call_target="tpu_custom_call" | custom-call | flops 34359738368 | bytes 94371840 | tf_op jit(solution)/shard_map/attn_fwd/pallas_call | solution.py:90
  365.5 57.6 %mlp.3 = (bf16[2048,4096]{1,0:T(8,128)(2,1)}, f32[2048,4096]{1,0:T(8,128)}, bf16[2048,1024]{1,0:T(8,128)(2,1)}) custom-call(bf16[2048,1024]{1,0:T(8,128)(2,1)} %get-tuple-element.92.h_ref.a_ref, bf16[2048,1024]{1,0:T(8,128)(2,1)} %get-tuple-element.93.mid_ref, bf16[1024,4096]{1,0:T(8,128)(2,1)} %bitcast.95, f32[1,4096]{1,0:T(1,128)} %bitcast.89, ...), custom_call_target="tpu_custom_call" | custom-call | flops 34359738368 | bytes 83886080 | tf_op jit(solution)/shard_map/mlp/pallas_call | solution.py:279
  423.2 22.9 %down_grad.2 = bf16[4096,1024]{1,0:T(8,128)(2,1)} custom-call(bf16[2048,4096]{1,0:T(8,128)(2,1)} %get-tuple-element.94.a_ref, bf16[2048,1024]{1,0:T(8,128)(2,1)} %bitcast.103), custom_call_target="tpu_custom_call" | custom-call | flops 17179869184 | bytes 29360128 | tf_op jit(solution)/shard_map/down_grad/pallas_call | solution.py:374
  446.1 56.7 %mlp_back.2 = (bf16[2048,4096]{1,0:T(8,128)(2,1)}, bf16[2048,1024]{1,0:T(8,128)(2,1)}, bf16[2048,1024]{1,0:T(8,128)(2,1)}, f32[8,4096]{1,0:T(8,128)}, f32[32,1024]{1,0:T(8,128)}) custom-call(bf16[2048,1024]{1,0:T(8,128)(2,1)} %bitcast.104, f32[2048,4096]{1,0:T(8,128)} %get-tuple-element.97.slope_ref, bf16[4096,1024]{1,0:T(8,128)(2,1)} %bitcast.98, ...), custom_call_target="tpu_custom_call" | custom-call | flops 38654705664 | bytes 94371840 | tf_op jit(solution)/shard_map/mlp_back/pallas_call | solution.py:325
  511.3 23.0 %up_grad.2 = bf16[1024,4096]{1,0:T(8,128)(2,1)} custom-call(bf16[2048,1024]{1,0:T(8,128)(2,1)} %get-tuple-element.92.h_ref.a_ref, bf16[2048,4096]{1,0:T(8,128)(2,1)} %get-tuple-element.98.b_ref), custom_call_target="tpu_custom_call" | custom-call | flops 17179869184 | bytes 29360128 | tf_op jit(solution)/shard_map/up_grad/pallas_call | solution.py:374
  535.1 82.7 %attn_bwd.2 = (bf16[2048,1024]{1,0:T(8,128)(2,1)}, bf16[2048,1024]{1,0:T(8,128)(2,1)}, bf16[2048,1024]{1,0:T(8,128)(2,1)}) custom-call(s32[2]{0:T(128)} %len_ref.7, bf16[2048,1024]{1,0:T(8,128)(2,1)} %get-tuple-element.88.q_ref, bf16[2048,1024]{1,0:T(8,128)(2,1)} %get-tuple-element.89.k_ref, bf16[2048,1024]{1,0:T(8,128)(2,1)} %get-tuple-element.90.v_ref, ...), custom_call_target="tpu_custom_call" | custom-call | flops 68719476736 | bytes 104857600 | tf_op jit(solution)/shard_map/attn_bwd/pallas_call | solution.py:143
  617.9 20.1 %qkv_grad.2 = (bf16[3,1024,1024]{2,1,0:T(8,128)(2,1)}, f32[24,1024]{1,0:T(8,128)}) custom-call(bf16[2048,1024]{1,0:T(8,128)(2,1)} %get-tuple-element.87.h_ref, bf16[2048,1024]{1,0:T(8,128)(2,1)} %get-tuple-element.111.dq_ref, bf16[2048,1024]{1,0:T(8,128)(2,1)} %get-tuple-element.105.dk_ref, bf16[2048,1024]{1,0:T(8,128)(2,1)} %get-tuple-element.106.dv_ref), custom_call_target="tpu_custom_call" | custom-call | flops 12884901888 | bytes 25165824 | tf_op jit(solution)/shard_map/qkv_grad/pallas_call | solution.py:391
  638.0 24.1 %in_back.2 = (bf16[2048,1024]{1,0:T(8,128)(2,1)}, f32[16,1024]{1,0:T(8,128)}) custom-call(bf16[2048,1024]{1,0:T(8,128)(2,1)} %get-tuple-element.111.dq_ref, bf16[2048,1024]{1,0:T(8,128)(2,1)} %get-tuple-element.105.dk_ref, bf16[2048,1024]{1,0:T(8,128)(2,1)} %get-tuple-element.106.dv_ref, bf16[3,1024,1024]{2,1,0:T(8,128)(2,1)} %bitcast.102, ...), custom_call_target="tpu_custom_call" | custom-call | flops 12884901888 | bytes 35651584 | tf_op jit(solution)/shard_map/in_back/pallas_call | solution.py:351
  662.1 28.6 %reduce-scatter.15.cloned.1.call-done = bf16[64,1024]{1,0:T(8,128)(2,1)} async-done(((bf16[1024,1024]{1,0:T(8,128)(2,1)}), bf16[64,1024]{1,0:T(8,128)(2,1)}) %reduce-scatter.15.cloned.1.call-update) | async-done | bytes 131088 | tf_op jit(solution)/shard_map/reduce_scatter | solution.py:497
  690.7 22.8 %down_grad.3 = bf16[4096,1024]{1,0:T(8,128)(2,1)} custom-call(bf16[2048,4096]{1,0:T(8,128)(2,1)} %get-tuple-element.115.a_ref, bf16[2048,1024]{1,0:T(8,128)(2,1)} %get-tuple-element.117.b_ref.dy_ref), custom_call_target="tpu_custom_call" | custom-call | flops 17179869184 | bytes 29360128 | tf_op jit(solution)/shard_map/down_grad/pallas_call | solution.py:374
  713.6 56.6 %mlp_back.3 = (bf16[2048,4096]{1,0:T(8,128)(2,1)}, bf16[2048,1024]{1,0:T(8,128)(2,1)}, bf16[2048,1024]{1,0:T(8,128)(2,1)}, f32[8,4096]{1,0:T(8,128)}, f32[32,1024]{1,0:T(8,128)}) custom-call(bf16[2048,1024]{1,0:T(8,128)(2,1)} %get-tuple-element.117.b_ref.dy_ref, f32[2048,4096]{1,0:T(8,128)} %get-tuple-element.118.slope_ref, bf16[4096,1024]{1,0:T(8,128)(2,1)} %bitcast.94, ...), custom_call_target="tpu_custom_call" | custom-call | flops 38654705664 | bytes 94371840 | tf_op jit(solution)/shard_map/mlp_back/pallas_call | solution.py:325
  778.8 22.9 %up_grad.3 = bf16[1024,4096]{1,0:T(8,128)(2,1)} custom-call(bf16[2048,1024]{1,0:T(8,128)(2,1)} %get-tuple-element.114.h_ref.a_ref, bf16[2048,4096]{1,0:T(8,128)(2,1)} %get-tuple-element.119.b_ref), custom_call_target="tpu_custom_call" | custom-call | flops 17179869184 | bytes 29360128 | tf_op jit(solution)/shard_map/up_grad/pallas_call | solution.py:374
  802.4 82.5 %attn_bwd.3 = (bf16[2048,1024]{1,0:T(8,128)(2,1)}, bf16[2048,1024]{1,0:T(8,128)(2,1)}, bf16[2048,1024]{1,0:T(8,128)(2,1)}) custom-call(s32[2]{0:T(128)} %len_ref.7, bf16[2048,1024]{1,0:T(8,128)(2,1)} %get-tuple-element.80.q_ref, bf16[2048,1024]{1,0:T(8,128)(2,1)} %get-tuple-element.81.k_ref, bf16[2048,1024]{1,0:T(8,128)(2,1)} %get-tuple-element.82.v_ref, ...), custom_call_target="tpu_custom_call" | custom-call | flops 68719476736 | bytes 104857600 | tf_op jit(solution)/shard_map/attn_bwd/pallas_call | solution.py:143
  884.9 20.1 %qkv_grad.3 = (bf16[3,1024,1024]{2,1,0:T(8,128)(2,1)}, f32[24,1024]{1,0:T(8,128)}) custom-call(bf16[2048,1024]{1,0:T(8,128)(2,1)} %get-tuple-element.123.h_ref, bf16[2048,1024]{1,0:T(8,128)(2,1)} %get-tuple-element.133.dq_ref, bf16[2048,1024]{1,0:T(8,128)(2,1)} %get-tuple-element.129.dk_ref, bf16[2048,1024]{1,0:T(8,128)(2,1)} %get-tuple-element.130.dv_ref), custom_call_target="tpu_custom_call" | custom-call | flops 12884901888 | bytes 25165824 | tf_op jit(solution)/shard_map/qkv_grad/pallas_call | solution.py:391
  905.0 46.1 %reduce-scatter.21.cloned.1.call-done = bf16[64,4096]{1,0:T(8,128)(2,1)} async-done(((bf16[1024,4096]{1,0:T(8,128)(2,1)}), bf16[64,4096]{1,0:T(8,128)(2,1)}) %reduce-scatter.21.cloned.1.call-update) | async-done | bytes 524304 | tf_op jit(solution)/shard_map/reduce_scatter | solution.py:496
  952.9 24.3 %in_back.3 = (bf16[2048,1024]{1,0:T(8,128)(2,1)}, f32[16,1024]{1,0:T(8,128)}) custom-call(bf16[2048,1024]{1,0:T(8,128)(2,1)} %get-tuple-element.133.dq_ref, bf16[2048,1024]{1,0:T(8,128)(2,1)} %get-tuple-element.129.dk_ref, bf16[2048,1024]{1,0:T(8,128)(2,1)} %get-tuple-element.130.dv_ref, bf16[3,1024,1024]{2,1,0:T(8,128)(2,1)} %bitcast.100, ...), custom_call_target="tpu_custom_call" | custom-call | flops 12884901888 | bytes 35651584 | tf_op jit(solution)/shard_map/in_back/pallas_call | solution.py:351
  992.8 17.2 %reduce-scatter.17.cloned.1.call-done = bf16[64,1024]{1,0:T(8,128)(2,1)} async-done(((bf16[1024,1024]{1,0:T(8,128)(2,1)}), bf16[64,1024]{1,0:T(8,128)(2,1)}) %reduce-scatter.17.cloned.1.call-update) | async-done | bytes 131088 | tf_op jit(solution)/shard_map/reduce_scatter | solution.py:497
  1012.5 70.1 %reduce-scatter.23.cloned.1.call-done = bf16[3,64,1024]{2,1,0:T(8,128)(2,1)} async-done(((bf16[3,1024,1024]{2,1,0:T(8,128)(2,1)}), bf16[3,64,1024]{2,1,0:T(8,128)(2,1)}) %reduce-scatter.23.cloned.1.call-update) | async-done | bytes 393232 | tf_op jit(solution)/shard_map/reduce_scatter | solution.py:502
  (197 shorter events, 106.8 us)
Async XLA Ops:
  7.2 48.7 %all-gather.17.cloned.1.call-start = ((), (), s32[]{:S(2)}) async-start(), calls=%async_computation.16 | async-start | bytes 6684672 | tf_op jit(solution)/shard_map/all_gather | solution.py:474
  9.4 142.9 %all-gather.19.cloned.1.call-start = ((), (), s32[]{:S(2)}) async-start(), calls=%async_computation.17 | async-start | bytes 2228224 | tf_op jit(solution)/shard_map/all_gather | solution.py:475
  11.2 152.5 %all-gather.21.cloned.1.call-start = ((), (), s32[]{:S(2)}) async-start(), calls=%async_computation.18 | async-start | bytes 8912896 | tf_op jit(solution)/shard_map/all_gather | solution.py:476
  13.5 175.2 %all-gather.23.cloned.1.call-start = ((), (), s32[]{:S(2)}) async-start(), calls=%async_computation.19 | async-start | bytes 8912896 | tf_op jit(solution)/shard_map/all_gather | solution.py:477
  14.6 232.0 %all-gather.25.cloned.1.call-start = ((), (), s32[]{:S(2)}) async-start(), calls=%async_computation.20 | async-start | bytes 6684672 | tf_op jit(solution)/shard_map/all_gather | solution.py:474
  15.2 327.9 %all-gather.27.cloned.1.call-start = ((), (), s32[]{:S(2)}) async-start(), calls=%async_computation.21 | async-start | bytes 2228224 | tf_op jit(solution)/shard_map/all_gather | solution.py:475
  15.8 338.9 %all-gather.29.cloned.1.call-start = ((), (), s32[]{:S(2)}) async-start(), calls=%async_computation.22 | async-start | bytes 8912896 | tf_op jit(solution)/shard_map/all_gather | solution.py:476
  16.5 349.0 %all-gather.31.cloned.1.call-start = ((), (), s32[]{:S(2)}) async-start(), calls=%async_computation.23 | async-start | bytes 8912896 | tf_op jit(solution)/shard_map/all_gather | solution.py:477
  17.3 600.6 %reduce-scatter.9.cloned.1.call-start = ((), (), s32[]{:S(2)}) async-start(), calls=%async_computation.8 | async-start | bytes 8912896 | tf_op jit(solution)/shard_map/reduce_scatter | solution.py:490
  17.5 1.6 collective-permute-start
  19.2 4.6 collective-permute-start.1
  23.8 4.1 collective-permute-start.2
  28.0 4.5 collective-permute-start.3
  446.1 191.9 %reduce-scatter.11.cloned.1.call-start = ((), (), s32[]{:S(2)}) async-start(), calls=%async_computation.9 | async-start | bytes 8912896 | tf_op jit(solution)/shard_map/reduce_scatter | solution.py:496
  534.3 156.4 %reduce-scatter.15.cloned.1.call-start = ((), (), s32[]{:S(2)}) async-start(), calls=%async_computation.11 | async-start | bytes 2228224 | tf_op jit(solution)/shard_map/reduce_scatter | solution.py:497
  535.1 243.7 %reduce-scatter.13.cloned.1.call-start = ((), (), s32[]{:S(2)}) async-start(), calls=%async_computation.10 | async-start | bytes 6684672 | tf_op jit(solution)/shard_map/reduce_scatter | solution.py:502
  638.0 246.9 %reduce-scatter.19.cloned.1.call-start = ((), (), s32[]{:S(2)}) async-start(), calls=%async_computation.13 | async-start | bytes 8912896 | tf_op jit(solution)/shard_map/reduce_scatter | solution.py:490
  713.6 237.6 %reduce-scatter.21.cloned.1.call-start = ((), (), s32[]{:S(2)}) async-start(), calls=%async_computation.14 | async-start | bytes 8912896 | tf_op jit(solution)/shard_map/reduce_scatter | solution.py:496
  801.7 208.3 %reduce-scatter.17.cloned.1.call-start = ((), (), s32[]{:S(2)}) async-start(), calls=%async_computation.12 | async-start | bytes 2228224 | tf_op jit(solution)/shard_map/reduce_scatter | solution.py:497
  802.3 280.3 %reduce-scatter.23.cloned.1.call-start = ((), (), s32[]{:S(2)}) async-start(), calls=%async_computation.15 | async-start | bytes 6684672 | tf_op jit(solution)/shard_map/reduce_scatter | solution.py:502
  978.7 4.6 collective-permute-start.4
  983.4 4.1 collective-permute-start.5
  987.5 3.8 collective-permute-start.6
  991.3 18.8 %collective-permute-start.7 = (f32[1,2,832]{2,1,0:T(2,128)S(1)}, f32[1,2,832]{2,1,0:T(2,128)S(1)}, u32[]{:S(2)}, u32[]{:S(2)}) collective-permute-start(f32[1,2,832]{2,1,0:T(2,128)S(1)} %broadcast_select_fusion.7), channel_id=1, source_target_pairs={{0,1},{1,0},{2,3},{3,2},{4,5},{5,4},{6,7},{7,6},{8,9},{9,8},{10,11... | collective-permute-start | bytes 19976 | tf_op jit(solution)/shard_map/ppermute | solution.py:412
  (18 other events, 525.7 us)
Sparse Core Ops, SparseCore 0:
  10.8 44.9 all-gather.16
  58.1 28.2 all-gather.18
  89.2 48.6 all-gather.20
  140.0 48.6 all-gather.22
  190.8 41.8 all-gather.24
  234.8 28.2 all-gather.26
  265.9 48.6 all-gather.28
  316.9 48.6 all-gather.30
  446.2 92.7 reduce-scatter.8
  541.1 90.9 reduce-scatter.10
  634.9 55.7 reduce-scatter.14
  692.9 70.8 reduce-scatter.12
  766.0 91.9 reduce-scatter.18
  860.2 90.9 reduce-scatter.20
  953.8 56.1 reduce-scatter.16
  1012.2 70.4 reduce-scatter.22

commit v3 on v2

--- a/solution.py
+++ b/solution.py
@@ -38,6 +38,7 @@
         ka_ref[h] = jnp.where(hidden_key, jnp.broadcast_to(bar, (SEQ, PAIR)), k_ref[...] * own)
         qa_ref[h] = q_ref[...] * own + one
     vt_ref[...] = v_ref[...].T
+
     def at(t):
         return pl.ds(pl.multiple_of(t * QT, QT), QT)
 
@@ -165,6 +166,10 @@
     return pl.BlockSpec(shape, lambda *i: (0,) * len(shape), pipeline_mode=pl.Buffered(1))
 
 
+def part_of(shape, *at):
+    return pl.BlockSpec(shape, lambda *i: at, pipeline_mode=pl.Buffered(1))
+
+
 def partial(shape):
     return pl.BlockSpec(shape, lambda *i: (0,) * len(shape))
 
@@ -197,18 +202,6 @@
 
 def eights(x):
     return jnp.sum(x.reshape(x.shape[0] // 8, 8, x.shape[1]), axis=0)
-
-
-def add_up(ref, value):
-    first = pl.program_id(0) == 0
-
-    @pl.when(first)
-    def _():
-        ref[...] = value
-
-    @pl.when(jnp.logical_not(first))
-    def _():
-        ref[...] += value
 
 
 def qkv_kernel(x_ref, w_ref, b_ref, ln_ref, cos_ref, sin_ref, h_ref, q_ref, k_ref, v_ref):
@@ -232,7 +225,7 @@
     table = pl.BlockSpec((block, PAIR), lambda i: (i % (SEQ // block), 0))
     return pl.pallas_call(
         qkv_kernel, grid=(tokens // block,),
-        in_specs=[row, whole(w.shape), whole(b.shape), whole(ln.shape), table, table],
+        in_specs=[row, part_of((3, width, width), 0, 0, 0), whole(b.shape), whole(ln.shape), table, table],
         out_specs=[row] * 4,
         out_shape=[jax.ShapeDtypeStruct(x.shape, jnp.bfloat16)] * 4,
         compiler_params=params(), cost_estimate=cost(6 * tokens * width * width, 26 << 20), name='qkv',
@@ -240,7 +233,7 @@
 
 
 def out_kernel(ctx_ref, x_ref, w_ref, b_ref, ln_ref, mid_ref, h_ref):
-    mid = (x_ref[...].astype(jnp.float32) + dot(ctx_ref[...], w_ref[...], NN) + b_ref[...]).astype(jnp.bfloat16)
+    mid = (x_ref[...].astype(jnp.float32) + dot(ctx_ref[...], w_ref[...], NN) + b_ref[3:4]).astype(jnp.bfloat16)
     mid_ref[...] = mid
     unit, _ = normal(mid.astype(jnp.float32))
     h_ref[...] = (unit * ln_ref[2:3] + ln_ref[3:4]).astype(jnp.bfloat16)
@@ -252,7 +245,7 @@
     row = rows_of(block, width)
     return pl.pallas_call(
         out_kernel, grid=(tokens // block,),
-        in_specs=[row, row, whole(w.shape), whole(b.shape), whole(ln.shape)], out_specs=[row] * 2,
+        in_specs=[row, row, part_of((None, width, width), 3, 0, 0), whole(b.shape), whole(ln.shape)], out_specs=[row] * 2,
         out_shape=[jax.ShapeDtypeStruct(x.shape, jnp.bfloat16)] * 2,
         compiler_params=params(), cost_estimate=cost(2 * tokens * width * width, 18 << 20), name='out_proj',
     )(ctx, x, w, b, ln)
@@ -311,8 +304,7 @@
     dmid_ref[...] = dmid
     gln_ref[0:8] += eights(grad * unit)
     gln_ref[8:16] += eights(grad)
-    gln_ref[16:24] += eights(dmid.astype(jnp.float32))
-    gln_ref[24:32] += eights(dy)
+    gln_ref[16:24] += eights(dy)
     dctx_ref[...] = dot(dmid, wo_ref[...], NT).astype(jnp.bfloat16)
 
 
@@ -324,10 +316,10 @@
     half = jax.ShapeDtypeStruct(dy.shape, jnp.bfloat16)
     return pl.pallas_call(
         mlp_back_kernel, grid=(tokens // block,),
-        in_specs=[row, long, whole(wd.shape), whole(wu.shape), row, whole(ln.shape), whole(wo.shape)],
-        out_specs=[long, row, row, partial((8, wide)), partial((32, width))],
+        in_specs=[row, long, whole(wd.shape), whole(wu.shape), row, whole(ln.shape), part_of((None, width, width), 3, 0, 0)],
+        out_specs=[long, row, row, partial((8, wide)), partial((24, width))],
         out_shape=[jax.ShapeDtypeStruct((tokens, wide), jnp.bfloat16), half, half,
-                   jax.ShapeDtypeStruct((8, wide), jnp.float32), jax.ShapeDtypeStruct((32, width), jnp.float32)],
+                   jax.ShapeDtypeStruct((8, wide), jnp.float32), jax.ShapeDtypeStruct((24, width), jnp.float32)],
         compiler_params=params(), cost_estimate=cost(2 * tokens * width * (2 * wide + width), 90 << 20), name='mlp_back',
     )(dy, slope, wd, wu, mid, ln, wo)
 
@@ -350,51 +342,89 @@
     row = rows_of(block, width)
     return pl.pallas_call(
         in_back_kernel, grid=(tokens // block,),
-        in_specs=[row, row, row, whole(w.shape), row, whole(ln.shape), row],
+        in_specs=[row, row, row, part_of((3, width, width), 0, 0, 0), row, whole(ln.shape), row],
         out_specs=[row, partial((16, width))],
         out_shape=[jax.ShapeDtypeStruct(x.shape, jnp.bfloat16), jax.ShapeDtypeStruct((16, width), jnp.float32)],
         compiler_params=params(), cost_estimate=cost(6 * tokens * width * width, 34 << 20), name='in_back',
     )(dq, dk, dv, w, x, ln, dmid)
 
 
-def grad_kernel(a_ref, b_ref, g_ref):
-    g_ref[...] = dot(a_ref[...], b_ref[...], TN).astype(jnp.bfloat16)
-
-
-def weight_grad(a, b, name, tall):
+def share(grad, side, keep_ref, give_ref, at):
+    low, high = grad
+    keep_ref[at] = jnp.where(side == 0, low, high).astype(jnp.bfloat16)
+    give_ref[at] = jnp.where(side == 0, high, low).astype(jnp.bfloat16)
+
+
+def down_grad_kernel(side_ref, a_ref, b_ref, keep_ref, give_ref):
+    grad = dot(a_ref[...], b_ref[...], TN)
+    half = grad.shape[0] // 2
+    share((grad[:half], grad[half:]), side_ref[0], keep_ref, give_ref, ...)
+
+
+def down_grad(side, a, b):
     tokens, m = a.shape
     n = b.shape[1]
-    block = 512
-    if tall:
-        grid, a_spec, b_spec = (m // block,), pl.BlockSpec((tokens, block), lambda i: (0, i)), whole(b.shape)
-        out = pl.BlockSpec((block, n), lambda i: (i, 0))
-    else:
-        grid, a_spec, b_spec = (n // block,), whole(a.shape), pl.BlockSpec((tokens, block), lambda i: (0, i))
-        out = pl.BlockSpec((m, block), lambda i: (0, i))
-    return pl.pallas_call(
-        grad_kernel, grid=grid, in_specs=[a_spec, b_spec], out_specs=out,
-        out_shape=jax.ShapeDtypeStruct((m, n), jnp.bfloat16),
-        compiler_params=params(), cost_estimate=cost(2 * tokens * m * n, 2 * (tokens * (m + n) + m * n)), name=name,
-    )(a, b)
-
-
-def qkv_grad_kernel(h_ref, dq_ref, dk_ref, dv_ref, g_ref, gb_ref):
-    for j, d_ref in enumerate((dq_ref, dk_ref, dv_ref)):
-        g_ref[j] = dot(h_ref[...], d_ref[...], TN).astype(jnp.bfloat16)
+    chips = 8
+    block = m // chips
+    out = pl.BlockSpec((None, block // 2, n), lambda i, s: (i, 0, 0))
+    return pl.pallas_call(
+        down_grad_kernel,
+        grid_spec=pltpu.PrefetchScalarGridSpec(
+            num_scalar_prefetch=1, grid=(chips,),
+            in_specs=[pl.BlockSpec((tokens, block), lambda i, s: (0, i)), whole(b.shape)], out_specs=[out, out]),
+        out_shape=[jax.ShapeDtypeStruct((chips, block // 2, n), jnp.bfloat16)] * 2,
+        compiler_params=params(), cost_estimate=cost(2 * tokens * m * n, 2 * (tokens * (m + n) + m * n)), name='down_grad',
+    )(side, a, b)
+
+
+def up_grad_kernel(side_ref, a_ref, b_ref, keep_ref, give_ref):
+    grad = dot(a_ref[...], b_ref[...], TN)
+    chips, half = keep_ref.shape[0], keep_ref.shape[1]
+    for i in range(chips):
+        r = 2 * i * half
+        share((grad[r:r + half], grad[r + half:r + 2 * half]), side_ref[0], keep_ref, give_ref, i)
+
+
+def up_grad(side, a, b):
+    tokens, m = a.shape
+    n = b.shape[1]
+    chips, block = 8, 512
+    out = pl.BlockSpec((chips, m // chips // 2, block), lambda i, s: (0, 0, i))
+    return pl.pallas_call(
+        up_grad_kernel,
+        grid_spec=pltpu.PrefetchScalarGridSpec(
+            num_scalar_prefetch=1, grid=(n // block,),
+            in_specs=[whole(a.shape), pl.BlockSpec((tokens, block), lambda i, s: (0, i))], out_specs=[out, out]),
+        out_shape=[jax.ShapeDtypeStruct((chips, m // chips // 2, n), jnp.bfloat16)] * 2,
+        compiler_params=params(), cost_estimate=cost(2 * tokens * m * n, 2 * (tokens * (m + n) + m * n)), name='up_grad',
+    )(side, a, b)
+
+
+def attn_grad_kernel(side_ref, h_ref, ctx_ref, dq_ref, dk_ref, dv_ref, dmid_ref, keep_ref, give_ref, gb_ref):
+    chips, half = keep_ref.shape[0], keep_ref.shape[2]
+    for j, d_ref in enumerate((dq_ref, dk_ref, dv_ref, dmid_ref)):
+        grad = dot((h_ref if j < 3 else ctx_ref)[...], d_ref[...], TN)
+        for i in range(chips):
+            r = 2 * i * half
+            share((grad[r:r + half], grad[r + half:r + 2 * half]), side_ref[0], keep_ref, give_ref, (i, j))
         gb_ref[8 * j:8 * j + 8] = eights(d_ref[...].astype(jnp.float32))
 
 
-def qkv_grad(h, dq, dk, dv):
+def attn_grad(side, h, ctx, dq, dk, dv, dmid):
     tokens, width = h.shape
-    block = 256
-    cols = pl.BlockSpec((tokens, block), lambda i: (0, i))
-    return pl.pallas_call(
-        qkv_grad_kernel, grid=(width // block,),
-        in_specs=[whole(h.shape), cols, cols, cols],
-        out_specs=[pl.BlockSpec((3, width, block), lambda i: (0, 0, i)), pl.BlockSpec((24, block), lambda i: (0, i))],
-        out_shape=[jax.ShapeDtypeStruct((3, width, width), jnp.bfloat16), jax.ShapeDtypeStruct((24, width), jnp.float32)],
-        compiler_params=params(), cost_estimate=cost(6 * tokens * width * width, 24 << 20), name='qkv_grad',
-    )(h, dq, dk, dv)
+    chips, block = 8, 256
+    cols = pl.BlockSpec((tokens, block), lambda i, s: (0, i))
+    out = pl.BlockSpec((chips, 4, width // chips // 2, block), lambda i, s: (0, 0, 0, i))
+    return pl.pallas_call(
+        attn_grad_kernel,
+        grid_spec=pltpu.PrefetchScalarGridSpec(
+            num_scalar_prefetch=1, grid=(width // block,),
+            in_specs=[whole(h.shape), whole(ctx.shape), cols, cols, cols, cols],
+            out_specs=[out, out, pl.BlockSpec((32, block), lambda i, s: (0, i))]),
+        out_shape=[jax.ShapeDtypeStruct((chips, 4, width // chips // 2, width), jnp.bfloat16)] * 2
+        + [jax.ShapeDtypeStruct((32, width), jnp.float32)],
+        compiler_params=params(), cost_estimate=cost(8 * tokens * width * width, 32 << 20), name='attn_grad',
+    )(side, h, ctx, dq, dk, dv, dmid)
 
 
 def rotary_tables():
@@ -465,56 +495,82 @@
         n, nu = b_attn.shape[2], b_up.shape[1]
         cos, sin = rotary_tables()
         gather = functools.partial(lax.all_gather, axis_name=axis_name, tiled=True)
-        scatter = functools.partial(lax.psum_scatter, axis_name=axis_name, tiled=True)
+        side = bit_of(axis_name, 'c').reshape(1)
+        after = lax.optimization_barrier
+
+        def join(keep, got):
+            return (keep.astype(jnp.float32) + got.astype(jnp.float32)).astype(jnp.bfloat16)
+
+        def spread_out(pair):
+            groups = [[2 * i + c for i in range(8)] for c in range(2)]
+            return lax.all_to_all(pair, axis_name, split_axis=0, concat_axis=0, axis_index_groups=groups, tiled=True)
+
+        def total(parts):
+            return jnp.sum(parts.astype(jnp.float32), axis=0)
+
         small = gather_packed(pack_params(b_attn, ln_par, b_up, b_down), axis_name)
         hidden = x.reshape(tokens, width)
         saved = []
         for l in range(layers):
             ba, ln, bu, bd = unpack_params(small, l, n, nu)
-            wqkv = gather(w_attn[l, :3], axis=1)
-            wo = gather(w_attn[l, 3], axis=0)
+            wa = gather(w_attn[l], axis=1)
             wu = gather(w_up[l], axis=0)
             wd = gather(w_down[l], axis=0)
-            h_one, q, k, v = qkv(hidden, wqkv, ba[:3], ln, cos, sin)
+            h_one, q, k, v = qkv(hidden, wa, ba, ln, cos, sin)
             ctx, probs = attn_fwd(lengths, q, k, v)
-            mid, h_two = out_proj(ctx, hidden, wo, ba[3:4], ln)
+            mid, h_two = out_proj(ctx, hidden, wa, ba, ln)
             act, slope, out = mlp(h_two, mid, wu, bu, wd, bd)
-            saved.append((hidden, h_one, q, k, v, ctx, probs, mid, h_two, act, slope, wqkv, wo, wu, wd, ln))
+            saved.append((hidden, h_one, q, k, v, ctx, probs, mid, h_two, act, slope, wa, wu, wd, ln))
             hidden = out
         grad = d_y.reshape(tokens, width)
         grads = [None] * layers
         for l in reversed(range(layers)):
-            x_in, h_one, q, k, v, ctx, probs, mid, h_two, act, slope, wqkv, wo, wu, wd, ln = saved[l]
-            after = lax.optimization_barrier
-            gw_down, grad = after((weight_grad(act, grad, 'down_grad', True), grad))
-            g_down = scatter(gw_down, scatter_dimension=0)
-            d_pre, d_mid, d_ctx, gb_up, gln_two = mlp_back(grad, slope, wd, wu, mid, ln, wo)
             if l + 1 < layers:
-                above, h_two = after((grads[l + 1][0], h_two))
-                grads[l + 1] = (above,) + grads[l + 1][1:]
-            gw_up, gw_out, d_ctx = after((weight_grad(h_two, d_pre, 'up_grad', False), weight_grad(ctx, d_mid, 'out_grad', False), d_ctx))
-            g_up = scatter(gw_up, scatter_dimension=0)
-            g_out = scatter(gw_out, scatter_dimension=0)
+                flying = spread_out(pair)
+            x_in, h_one, q, k, v, ctx, probs, mid, h_two, act, slope, wa, wu, wd, ln = saved[l]
+            keep, give = down_grad(side, act, grad)
+            give, grad = after((give, grad))
+            got = swap(give, axis_name, 'c')
+            d_pre, d_mid, d_ctx, gb_up, gln_two = mlp_back(grad, slope, wd, wu, mid, ln, wa)
+            got, d_pre = after((got, d_pre))
+            if l + 1 < layers:
+                flying, d_pre = after((flying, d_pre))
+                grads[l + 1][0] = total(flying)
+            pair, d_pre = after((join(keep, got), d_pre))
+            flying = spread_out(pair)
+            keep, give = up_grad(side, h_two, d_pre)
+            give, d_ctx = after((give, d_ctx))
+            got = swap(give, axis_name, 'c')
             dq, dk, dv = attn_bwd(lengths, q, k, v, ctx, d_ctx, probs, cos, sin)
-            g_down, dq = after((g_down, dq))
-            gw, gb_qkv = qkv_grad(h_one, dq, dk, dv)
-            gw, dq, g_up = after((gw, dq, g_up))
-            g_qkv = scatter(gw, scatter_dimension=1)
-            grad, gln_one = in_back(dq, dk, dv, wqkv, x_in, ln, d_mid)
-            g_out, grad = after((g_out, grad))
-            sums_two = jnp.sum(gln_two.reshape(4, 8, width), axis=1)
+            flying, got, dq = after((flying, got, dq))
+            g_down = total(flying)
+            pair, dq = after((join(keep, got), dq))
+            flying = spread_out(pair)
+            keep, give, gb_attn = attn_grad(side, h_one, ctx, dq, dk, dv, d_mid)
+            give, dq = after((give, dq))
+            got = swap(give, axis_name, 'c')
+            if l > 0:
+                grad, gln_one = in_back(dq, dk, dv, wa, x_in, ln, d_mid)
+                flying, got, grad = after((flying, got, grad))
+                g_up = total(flying)
+                pair, grad = after((join(keep, got), grad))
+            else:
+                flying, got, dq = after((flying, got, dq))
+                g_up = total(flying)
+                pair, dq = after((join(keep, got), dq))
+                flying = spread_out(pair)
+                grad, gln_one = in_back(dq, dk, dv, wa, x_in, ln, d_mid)
+            sums_two = jnp.sum(gln_two.reshape(3, 8, width), axis=1)
             sums_one = jnp.sum(gln_one.reshape(2, 8, width), axis=1)
-            gb_three = jnp.sum(gb_qkv.reshape(3, 8, width), axis=1)
+            gb_four = jnp.sum(gb_attn.reshape(4, 8, width), axis=1)
             gb_wide = jnp.sum(gb_up, axis=0)
             by_dev = lambda s: s.reshape(-1, 16, n).transpose(1, 0, 2).reshape(16, -1)
-            packed = jnp.concatenate([by_dev(gb_three), by_dev(sums_two[2:3]), by_dev(sums_one), by_dev(sums_two[:2]),
-                                      gb_wide.reshape(16, nu), by_dev(sums_two[3:4])], axis=1)
-            grads[l] = ((g_qkv, g_out), g_up, g_down, packed)
+            packed = jnp.concatenate([by_dev(gb_four), by_dev(sums_one), by_dev(sums_two[:2]),
+                                      gb_wide.reshape(16, nu), by_dev(sums_two[2:3])], axis=1)
+            grads[l] = [None, g_up, g_down, packed]
         got = scatter_packed(jnp.stack([g[3] for g in grads], axis=1), axis_name)
-        f32 = lambda g: g.astype(jnp.float32)
-        g_attn = jnp.stack([jnp.concatenate([f32(g[0][0]), f32(g[0][1])[None]]) for g in grads])
-        g_up = jnp.stack([f32(g[1]) for g in grads])
-        g_down = jnp.stack([f32(g[2]) for g in grads])
+        grads[0][0] = total(flying)
+        g_attn, g_up, g_down = (jnp.stack([g[i] for g in grads]) for i in range(3))
         return (grad.reshape(x.shape), g_attn, got[:, :4 * n].reshape(layers, 4, n), got[:, 4 * n:8 * n].reshape(layers, 4, n),
                 g_up, got[:, 8 * n:8 * n + nu], g_down, got[:, 8 * n + nu:])
 

time: 1100 us -> 1120 us (1.018)
  waiting for transfers between devices: 231 us -> 134 us
  other arithmetic: 11.2 us -> 74.1 us
  starting transfers between devices: 8.91 us -> 66.6 us
    reduce_scatter x8 -> x0, waiting for transfers between devices: 162 us -> none  [the longest x2 70.1 us: device_step(): g_qkv = scatter(gw, scatter_dimension=1)]
    all_to_all x0 -> x6, waiting for transfers between devices: none -> 71.1 us  [spread_out(): lax.all_to_all(pair, axis_name, split_axis=0, concat_axis=0, axis_index_g...]
    convert_element_type x0 -> x6, other arithmetic: none -> 45.5 us  [join(): (keep.astype(jnp.float32) + got.astype(jnp.float32)).astype(jnp.bfloat16)]
    all_to_all x0 -> x6, starting transfers between devices: none -> 36.4 us  [spread_out(): lax.all_to_all(pair, axis_name, split_axis=0, concat_axis=0, axis_index_g...]
    all_gather x2, waiting for transfers between devices: 35.9 us -> 0.02 us  [device_step(): wd = gather(w_down[l], axis=0)]
    ppermute x8 -> x14, starting transfers between devices: 8.27 us -> 29.9 us  [swap(): lax.ppermute(value, axis_name, [(i, i ^ BITS[dim]) for i in range(16)])]
    ppermute x8 -> x14, waiting for transfers between devices: 13.5 us -> 33.4 us  [swap(): lax.ppermute(value, axis_name, [(i, i ^ BITS[dim]) for i in range(16)])]
    reduce_sum x4 -> x10, other arithmetic: 0.17 us -> 18.8 us  [the longest x6 18.6 us: total(): return jnp.sum(parts.astype(jnp.float32), axis=0)]
  transfers between devices with their start and end apart: 24 -> 26, of which waited for: 13 -> 8; matrix products, arithmetic and copies ran while one was open for 2% -> 3% of each run, Pallas kernels for 67% -> 52%
where the time goes in v3:
time: 1120 us; the launch traced here: 1110 us
  Pallas kernels  802 us (72%)
  waiting for transfers between devices  134 us (12%)
  other arithmetic  74.1 us (7%)
  starting transfers between devices  66.6 us (6%)
  local copies, waits for them, and re-layouts  15.4 us (1%)
  between operations  15.2 us (1%)
    pallas_call x2, Pallas kernels, attn_bwd(): pl.pallas_call(attn_bwd_kernel, grid_spec=pltpu.PrefetchScalarGridSpec(nu...  165 us
    pallas_call x2, Pallas kernels, attn_fwd(): pl.pallas_call(attn_fwd_kernel, grid_spec=pltpu.PrefetchScalarGridSpec(nu...  153 us
    pallas_call x2, Pallas kernels, mlp(): pl.pallas_call(mlp_kernel, grid=(tokens // block,), in_specs=[row, row, w...  116 us
    pallas_call x2, Pallas kernels, mlp_back(): pl.pallas_call(mlp_back_kernel, grid=(tokens // block,), in_specs=[row, l...  112 us
    all_to_all x6, waiting for transfers between devices, spread_out(): lax.all_to_all(pair, axis_name, split_axis=0, concat_axis=0, axis_index_g...  71.1 us
    pallas_call x2, Pallas kernels, attn_grad(): pl.pallas_call(attn_grad_kernel, grid_spec=pltpu.PrefetchScalarGridSpec(n...  53.7 us
    pallas_call x2, Pallas kernels, in_back(): pl.pallas_call(in_back_kernel, grid=(tokens // block,), in_specs=[row, ro...  47.8 us
    pallas_call x2, Pallas kernels, up_grad(): pl.pallas_call(up_grad_kernel, grid_spec=pltpu.PrefetchScalarGridSpec(num...  45.8 us
  transfers between devices with their start and end apart: 26, of which 8 were waited for; matrix products, arithmetic and copies ran while one was open for 3% of the time, Pallas kernels for 52%

profile of v3, /device:TPU:0, one launch (start us, length us, event | category | flops | bytes accessed | tf_op | source)
XLA Modules:
  0.0 1107.1 jit_solution(7787506596487061625)
XLA Ops:
  35.4 27.6 %all-gather.13.cloned.1.call-done = bf16[1,4,1024,1024]{3,2,1,0:T(8,128)(2,1)} async-done(((bf16[1,4,64,1024]{3,2,1,0:T(8,128)(2,1)}), bf16[1,4,1024,1024]{3,2,1,0:T(8,128)(2,1)}) %all-gather.13.cloned.1.call-update) | async-done | bytes 8388624 | tf_op jit(solution)/shard_map/all_gather | solution.py:516
  63.0 20.3 %qkv.2 = (bf16[2048,1024]{1,0:T(8,128)(2,1)}, bf16[2048,1024]{1,0:T(8,128)(2,1)}, bf16[2048,1024]{1,0:T(8,128)(2,1)}, bf16[2048,1024]{1,0:T(8,128)(2,1)}) custom-call(bf16[2048,1024]{1,0:T(8,128)(2,1)} %bitcast.83, bf16[4,1024,1024]{2,1,0:T(8,128)(2,1)} %bitcast.69, f32[4,1024]{1,0:T(4,128)} %reshape.151.b_ref, f32[4,1024]{1,0:T(4,128)} %reshape.153.ln_ref, ...), custom_call_target="tpu_custom_call" | custom-call | flops 12884901888 | bytes 27262976 | tf_op jit(solution)/shard_map/qkv/pallas_call | solution.py:226
  83.2 76.3 %attn_fwd.2 = (bf16[2048,1024]{1,0:T(8,128)(2,1)}, bf16[2,16,1024,1024]{3,2,1,0:T(8,128)(2,1)}) custom-call(s32[2]{0:T(128)} %len_ref.7, bf16[2048,1024]{1,0:T(8,128)(2,1)} %get-tuple-element.106.q_ref, bf16[2048,1024]{1,0:T(8,128)(2,1)} %get-tuple-element.107.k_ref, bf16[2048,1024]{1,0:T(8,128)(2,1)} %get-tuple-element.108.v_ref), custom_call_target="tpu_custom_call" | custom-call | flops 34359738368 | bytes 94371840 | tf_op jit(solution)/shard_map/attn_fwd/pallas_call | solution.py:91
  170.9 58.5 %mlp.2 = (bf16[2048,4096]{1,0:T(8,128)(2,1)}, f32[2048,4096]{1,0:T(8,128)}, bf16[2048,1024]{1,0:T(8,128)(2,1)}) custom-call(bf16[2048,1024]{1,0:T(8,128)(2,1)} %get-tuple-element.110.h_ref.a_ref, bf16[2048,1024]{1,0:T(8,128)(2,1)} %get-tuple-element.111.mid_ref, bf16[1024,4096]{1,0:T(8,128)(2,1)} %bitcast.104, f32[1,4096]{1,0:T(1,128)} %bitcast.103, ...), custom_call_target="tpu_custom_call" | custom-call | flops 34359738368 | bytes 83886080 | tf_op jit(solution)/shard_map/mlp/pallas_call | solution.py:272
  229.4 20.3 %qkv.3 = (bf16[2048,1024]{1,0:T(8,128)(2,1)}, bf16[2048,1024]{1,0:T(8,128)(2,1)}, bf16[2048,1024]{1,0:T(8,128)(2,1)}, bf16[2048,1024]{1,0:T(8,128)(2,1)}) custom-call(bf16[2048,1024]{1,0:T(8,128)(2,1)} %get-tuple-element.113.x_ref, bf16[4,1024,1024]{2,1,0:T(8,128)(2,1)} %bitcast.73, f32[4,1024]{1,0:T(4,128)} %reshape.157.b_ref, f32[4,1024]{1,0:T(4,128)} %reshape.159.ln_ref, ...), custom_call_target="tpu_custom_call" | custom-call | flops 12884901888 | bytes 27262976 | tf_op jit(solution)/shard_map/qkv/pallas_call | solution.py:226
  249.7 76.3 %attn_fwd.3 = (bf16[2048,1024]{1,0:T(8,128)(2,1)}, bf16[2,16,1024,1024]{3,2,1,0:T(8,128)(2,1)}) custom-call(s32[2]{0:T(128)} %len_ref.7, bf16[2048,1024]{1,0:T(8,128)(2,1)} %get-tuple-element.115.q_ref, bf16[2048,1024]{1,0:T(8,128)(2,1)} %get-tuple-element.116.k_ref, bf16[2048,1024]{1,0:T(8,128)(2,1)} %get-tuple-element.117.v_ref), custom_call_target="tpu_custom_call" | custom-call | flops 34359738368 | bytes 94371840 | tf_op jit(solution)/shard_map/attn_fwd/pallas_call | solution.py:91
  326.0 11.7 %out_proj.3 = (bf16[2048,1024]{1,0:T(8,128)(2,1)}, bf16[2048,1024]{1,0:T(8,128)(2,1)}) custom-call(bf16[2048,1024]{1,0:T(8,128)(2,1)} %get-tuple-element.118.ctx_ref.o_ref, bf16[2048,1024]{1,0:T(8,128)(2,1)} %get-tuple-element.113.x_ref, bf16[4,1024,1024]{2,1,0:T(8,128)(2,1)} %bitcast.74, f32[4,1024]{1,0:T(4,128)} %reshape.157.b_ref, f32[4,1024]{1,0:T(4,128)} %reshape.159.ln_ref), custom_call_target="tpu_custom_call" | custom-call | flops 4294967296 | bytes 18874368 | tf_op jit(solution)/shard_map/out_proj/pallas_call | solution.py:246
  337.6 57.7 %mlp.3 = (bf16[2048,4096]{1,0:T(8,128)(2,1)}, f32[2048,4096]{1,0:T(8,128)}, bf16[2048,1024]{1,0:T(8,128)(2,1)}) custom-call(bf16[2048,1024]{1,0:T(8,128)(2,1)} %get-tuple-element.119.h_ref.a_ref, bf16[2048,1024]{1,0:T(8,128)(2,1)} %get-tuple-element.120.mid_ref, bf16[1024,4096]{1,0:T(8,128)(2,1)} %bitcast.108, f32[1,4096]{1,0:T(1,128)} %bitcast.102, ...), custom_call_target="tpu_custom_call" | custom-call | flops 34359738368 | bytes 83886080 | tf_op jit(solution)/shard_map/mlp/pallas_call | solution.py:272
  395.4 22.9 %down_grad.2 = (bf16[8,256,1024]{2,1,0:T(8,128)(2,1)}, bf16[8,256,1024]{2,1,0:T(8,128)(2,1)}) custom-call(s32[1]{0:T(128)} %bitcast.side_ref, bf16[2048,4096]{1,0:T(8,128)(2,1)} %get-tuple-element.121.a_ref, bf16[2048,1024]{1,0:T(8,128)(2,1)} %bitcast.112), custom_call_target="tpu_custom_call" | custom-call | flops 17179869184 | bytes 29360128 | tf_op jit(solution)/shard_map/down_grad/pallas_call | solution.py:370
  418.5 56.2 %mlp_back.2 = (bf16[2048,4096]{1,0:T(8,128)(2,1)}, bf16[2048,1024]{1,0:T(8,128)(2,1)}, bf16[2048,1024]{1,0:T(8,128)(2,1)}, f32[8,4096]{1,0:T(8,128)}, f32[24,1024]{1,0:T(8,128)}) custom-call(bf16[2048,1024]{1,0:T(8,128)(2,1)} %bitcast.113, f32[2048,4096]{1,0:T(8,128)} %get-tuple-element.126.slope_ref, bf16[4096,1024]{1,0:T(8,128)(2,1)} %bitcast.111, ...), custom_call_target="tpu_custom_call" | custom-call | flops 38654705664 | bytes 94371840 | tf_op jit(solution)/shard_map/mlp_back/pallas_call | solution.py:317
  482.4 22.9 %up_grad.2 = (bf16[8,64,4096]{2,1,0:T(8,128)(2,1)}, bf16[8,64,4096]{2,1,0:T(8,128)(2,1)}) custom-call(s32[1]{0:T(128)} %bitcast.side_ref, bf16[2048,1024]{1,0:T(8,128)(2,1)} %get-tuple-element.119.h_ref.a_ref, bf16[2048,4096]{1,0:T(8,128)(2,1)} %get-tuple-element.130.b_ref), custom_call_target="tpu_custom_call" | custom-call | flops 17179869184 | bytes 29360128 | tf_op jit(solution)/shard_map/up_grad/pallas_call | solution.py:393
  510.4 82.2 %attn_bwd.2 = (bf16[2048,1024]{1,0:T(8,128)(2,1)}, bf16[2048,1024]{1,0:T(8,128)(2,1)}, bf16[2048,1024]{1,0:T(8,128)(2,1)}) custom-call(s32[2]{0:T(128)} %len_ref.7, bf16[2048,1024]{1,0:T(8,128)(2,1)} %get-tuple-element.115.q_ref, bf16[2048,1024]{1,0:T(8,128)(2,1)} %get-tuple-element.116.k_ref, bf16[2048,1024]{1,0:T(8,128)(2,1)} %get-tuple-element.117.v_ref, ...), custom_call_target="tpu_custom_call" | custom-call | flops 68719476736 | bytes 104857600 | tf_op jit(solution)/shard_map/attn_bwd/pallas_call | solution.py:144
  599.9 26.8 %attn_grad.2 = (bf16[8,4,64,1024]{3,2,1,0:T(8,128)(2,1)}, bf16[8,4,64,1024]{3,2,1,0:T(8,128)(2,1)}, f32[32,1024]{1,0:T(8,128)}) custom-call(s32[1]{0:T(128)} %bitcast.side_ref, bf16[2048,1024]{1,0:T(8,128)(2,1)} %get-tuple-element.114.h_ref, bf16[2048,1024]{1,0:T(8,128)(2,1)} %get-tuple-element.118.ctx_ref.o_ref, ...), custom_call_target="tpu_custom_call" | custom-call | flops 17179869184 | bytes 33554432 | tf_op jit(solution)/shard_map/attn_grad/pallas_call | solution.py:418
  632.5 23.9 %in_back.2 = (bf16[2048,1024]{1,0:T(8,128)(2,1)}, f32[16,1024]{1,0:T(8,128)}) custom-call(bf16[2048,1024]{1,0:T(8,128)(2,1)} %get-tuple-element.149.dq_ref, bf16[2048,1024]{1,0:T(8,128)(2,1)} %get-tuple-element.142.dk_ref, bf16[2048,1024]{1,0:T(8,128)(2,1)} %get-tuple-element.143.dv_ref, bf16[4,1024,1024]{2,1,0:T(8,128)(2,1)} %bitcast.76, ...), custom_call_target="tpu_custom_call" | custom-call | flops 12884901888 | bytes 35651584 | tf_op jit(solution)/shard_map/in_back/pallas_call | solution.py:343
  656.4 28.9 %all-to-all-done.1 = bf16[8,64,4096]{2,1,0:T(8,128)(2,1)} async-done(((bf16[8,64,4096]{2,1,0:T(8,128)(2,1)}), bf16[8,64,4096]{2,1,0:T(8,128)(2,1)}, u32[]{:S(2)}, u32[]{:S(2)}) %all-to-all-start.1) | async-done | bytes 4194336 | tf_op jit(solution)/shard_map/all_to_all | solution.py:506
  693.1 22.8 %down_grad.3 = (bf16[8,256,1024]{2,1,0:T(8,128)(2,1)}, bf16[8,256,1024]{2,1,0:T(8,128)(2,1)}) custom-call(s32[1]{0:T(128)} %bitcast.side_ref, bf16[2048,4096]{1,0:T(8,128)(2,1)} %get-tuple-element.112.a_ref, bf16[2048,1024]{1,0:T(8,128)(2,1)} %get-tuple-element.157.b_ref.dy_ref), custom_call_target="tpu_custom_call" | custom-call | flops 17179869184 | bytes 29360128 | tf_op jit(solution)/shard_map/down_grad/pallas_call | solution.py:370
  723.6 56.0 %mlp_back.3 = (bf16[2048,4096]{1,0:T(8,128)(2,1)}, bf16[2048,1024]{1,0:T(8,128)(2,1)}, bf16[2048,1024]{1,0:T(8,128)(2,1)}, f32[8,4096]{1,0:T(8,128)}, f32[24,1024]{1,0:T(8,128)}) custom-call(bf16[2048,1024]{1,0:T(8,128)(2,1)} %get-tuple-element.157.b_ref.dy_ref, f32[2048,4096]{1,0:T(8,128)} %get-tuple-element.158.slope_ref, bf16[4096,1024]{1,0:T(8,128)(2,1)} %bitcast.107, ...), custom_call_target="tpu_custom_call" | custom-call | flops 38654705664 | bytes 94371840 | tf_op jit(solution)/shard_map/mlp_back/pallas_call | solution.py:317
  787.3 22.9 %up_grad.3 = (bf16[8,64,4096]{2,1,0:T(8,128)(2,1)}, bf16[8,64,4096]{2,1,0:T(8,128)(2,1)}) custom-call(s32[1]{0:T(128)} %bitcast.side_ref, bf16[2048,1024]{1,0:T(8,128)(2,1)} %get-tuple-element.110.h_ref.a_ref, bf16[2048,4096]{1,0:T(8,128)(2,1)} %get-tuple-element.164.b_ref), custom_call_target="tpu_custom_call" | custom-call | flops 17179869184 | bytes 29360128 | tf_op jit(solution)/shard_map/up_grad/pallas_call | solution.py:393
  815.7 82.3 %attn_bwd.3 = (bf16[2048,1024]{1,0:T(8,128)(2,1)}, bf16[2048,1024]{1,0:T(8,128)(2,1)}, bf16[2048,1024]{1,0:T(8,128)(2,1)}) custom-call(s32[2]{0:T(128)} %len_ref.7, bf16[2048,1024]{1,0:T(8,128)(2,1)} %get-tuple-element.106.q_ref, bf16[2048,1024]{1,0:T(8,128)(2,1)} %get-tuple-element.107.k_ref, bf16[2048,1024]{1,0:T(8,128)(2,1)} %get-tuple-element.108.v_ref, ...), custom_call_target="tpu_custom_call" | custom-call | flops 68719476736 | bytes 104857600 | tf_op jit(solution)/shard_map/attn_bwd/pallas_call | solution.py:144
  905.2 26.9 %attn_grad.3 = (bf16[8,4,64,1024]{3,2,1,0:T(8,128)(2,1)}, bf16[8,4,64,1024]{3,2,1,0:T(8,128)(2,1)}, f32[32,1024]{1,0:T(8,128)}) custom-call(s32[1]{0:T(128)} %bitcast.side_ref, bf16[2048,1024]{1,0:T(8,128)(2,1)} %get-tuple-element.105.h_ref, bf16[2048,1024]{1,0:T(8,128)(2,1)} %get-tuple-element.109.ctx_ref.o_ref, ...), custom_call_target="tpu_custom_call" | custom-call | flops 17179869184 | bytes 33554432 | tf_op jit(solution)/shard_map/attn_grad/pallas_call | solution.py:418
  948.9 42.2 %all-to-all-done.4 = bf16[8,64,4096]{2,1,0:T(8,128)(2,1)} async-done(((bf16[8,64,4096]{2,1,0:T(8,128)(2,1)}), bf16[8,64,4096]{2,1,0:T(8,128)(2,1)}, u32[]{:S(2)}, u32[]{:S(2)}) %all-to-all-start.4) | async-done | bytes 4194336 | tf_op jit(solution)/shard_map/all_to_all | solution.py:506
  999.0 23.9 %in_back.3 = (bf16[2048,1024]{1,0:T(8,128)(2,1)}, f32[16,1024]{1,0:T(8,128)}) custom-call(bf16[2048,1024]{1,0:T(8,128)(2,1)} %get-tuple-element.186.dq_ref, bf16[2048,1024]{1,0:T(8,128)(2,1)} %get-tuple-element.176.dk_ref, bf16[2048,1024]{1,0:T(8,128)(2,1)} %get-tuple-element.177.dv_ref, bf16[4,1024,1024]{2,1,0:T(8,128)(2,1)} %bitcast.72, ...), custom_call_target="tpu_custom_call" | custom-call | flops 12884901888 | bytes 35651584 | tf_op jit(solution)/shard_map/in_back/pallas_call | solution.py:343
  1036.9 28.8 %collective-permute-done.10 = f32[8,2,832]{2,0,1:T(8,128)S(1)} collective-permute-done((f32[8,2,832]{2,0,1:T(8,128)S(1)}, f32[8,2,832]{2,0,1:T(8,128)S(1)}, u32[]{:S(2)}, u32[]{:S(2)}) %collective-permute-start.10) | collective-permute-done | bytes 53280 | tf_op jit(solution)/shard_map/ppermute | solution.py:442
  1065.7 16.1 %collective-permute-start.11 = (f32[4,2,832]{2,0,1:T(4,128)S(1)}, f32[4,2,832]{2,0,1:T(4,128)S(1)}, u32[]{:S(2)}, u32[]{:S(2)}) collective-permute-start(f32[4,2,832]{2,0,1:T(4,128)S(1)} %slice_select_fusion), channel_id=1, source_target_pairs={{0,4},{1,5},{2,6},{3,7},{4,0},{5,1},{6,2},{7,3},{8,12},{9,13},{10,... | collective-permute-start | bytes 79880 | tf_op jit(solution)/shard_map/ppermute | solution.py:442
  (185 shorter events, 157.6 us)
Async XLA Ops:
  7.2 55.8 %all-gather.13.cloned.1.call-start = ((), (), s32[]{:S(2)}) async-start(), calls=%async_computation.6 | async-start | bytes 8912896 | tf_op jit(solution)/shard_map/all_gather | solution.py:516
  9.6 161.3 %all-gather.15.cloned.1.call-start = ((), (), s32[]{:S(2)}) async-start(), calls=%async_computation.7 | async-start | bytes 8912896 | tf_op jit(solution)/shard_map/all_gather | solution.py:517
  12.0 158.9 %all-gather.17.cloned.1.call-start = ((), (), s32[]{:S(2)}) async-start(), calls=%async_computation.8 | async-start | bytes 8912896 | tf_op jit(solution)/shard_map/all_gather | solution.py:518
  13.1 216.3 %all-gather.19.cloned.1.call-start = ((), (), s32[]{:S(2)}) async-start(), calls=%async_computation.9 | async-start | bytes 8912896 | tf_op jit(solution)/shard_map/all_gather | solution.py:516
  13.7 323.9 %all-gather.21.cloned.1.call-start = ((), (), s32[]{:S(2)}) async-start(), calls=%async_computation.10 | async-start | bytes 8912896 | tf_op jit(solution)/shard_map/all_gather | solution.py:517
  14.3 323.4 %all-gather.23.cloned.1.call-start = ((), (), s32[]{:S(2)}) async-start(), calls=%async_computation.11 | async-start | bytes 8912896 | tf_op jit(solution)/shard_map/all_gather | solution.py:518
  16.7 4.5 collective-permute-start.1
  21.2 4.2 collective-permute-start.2
  25.4 4.0 collective-permute-start.3
  418.2 56.4 %collective-permute-start.4 = (bf16[8,256,1024]{2,1,0:T(8,128)(2,1)}, bf16[8,256,1024]{2,1,0:T(8,128)(2,1)}, u32[]{:S(2)}, u32[]{:S(2)}) collective-permute-start(bf16[8,256,1024]{2,1,0:T(8,128)(2,1)} %get-tuple-element.124), channel_id=1, source_target_pairs={{0,1},{1,0},{2,3},{3,2},{4,5},{5,4},{6,7},{7,6},{8,9},{9,8},{10,11... | collective-permute-start | bytes 12582920 | tf_op jit(solution)/shard_map/ppermute | solution.py:442
  505.3 87.4 %all-to-all-start = ((bf16[8,256,1024]{2,1,0:T(8,128)(2,1)}), bf16[8,256,1024]{2,1,0:T(8,128)(2,1)}, u32[]{:S(2)}, u32[]{:S(2)}) async-start(bf16[8,256,1024]{2,1,0:T(8,128)(2,1)} %add_convert_fusion.5), calls=%async_computation | async-start | bytes 8388608 | tf_op jit(solution)/shard_map/all_to_all | solution.py:506
  510.1 82.6 %collective-permute-start.5 = (bf16[8,64,4096]{2,1,0:T(8,128)(2,1)}, bf16[8,64,4096]{2,1,0:T(8,128)(2,1)}, u32[]{:S(2)}, u32[]{:S(2)}) collective-permute-start(bf16[8,64,4096]{2,1,0:T(8,128)(2,1)} %get-tuple-element.135), channel_id=1, source_target_pairs={{0,1},{1,0},{2,3},{3,2},{4,5},{5,4},{6,7},{7,6},{8,9},{9,8},{10,11... | collective-permute-start | bytes 12582920 | tf_op jit(solution)/shard_map/ppermute | solution.py:442
  626.7 58.6 %collective-permute-start.6 = (bf16[8,4,64,1024]{3,2,1,0:T(8,128)(2,1)}, bf16[8,4,64,1024]{3,2,1,0:T(8,128)(2,1)}, u32[]{:S(2)}, u32[]{:S(2)}) collective-permute-start(bf16[8,4,64,1024]{3,2,1,0:T(8,128)(2,1)} %get-tuple-element.148), channel_id=1, source_target_pairs={{0,1},{1,0},{2,3},{3,2},{4,5},{5,4},{6,7},{7,6},{8,9},{9,8},{10,11... | collective-permute-start | bytes 12582920 | tf_op jit(solution)/shard_map/ppermute | solution.py:442
  626.9 58.4 %all-to-all-start.1 = ((bf16[8,64,4096]{2,1,0:T(8,128)(2,1)}), bf16[8,64,4096]{2,1,0:T(8,128)(2,1)}, u32[]{:S(2)}, u32[]{:S(2)}) async-start(bf16[8,64,4096]{2,1,0:T(8,128)(2,1)} %add_convert_fusion.4), calls=%async_computation.1 | async-start | bytes 8388608 | tf_op jit(solution)/shard_map/all_to_all | solution.py:506
  716.0 63.6 %collective-permute-start.7 = (bf16[8,256,1024]{2,1,0:T(8,128)(2,1)}, bf16[8,256,1024]{2,1,0:T(8,128)(2,1)}, u32[]{:S(2)}, u32[]{:S(2)}) collective-permute-start(bf16[8,256,1024]{2,1,0:T(8,128)(2,1)} %get-tuple-element.156), channel_id=1, source_target_pairs={{0,1},{1,0},{2,3},{3,2},{4,5},{5,4},{6,7},{7,6},{8,9},{9,8},{10,11... | collective-permute-start | bytes 12582920 | tf_op jit(solution)/shard_map/ppermute | solution.py:442
  716.0 63.6 %all-to-all-start.2 = ((bf16[8,4,64,1024]{3,2,1,0:T(8,128)(2,1)}), bf16[8,4,64,1024]{3,2,1,0:T(8,128)(2,1)}, u32[]{:S(2)}, u32[]{:S(2)}) async-start(bf16[8,4,64,1024]{3,2,1,0:T(8,128)(2,1)} %add_convert_fusion.3), calls=%async_computation.2 | async-start | bytes 8388608 | tf_op jit(solution)/shard_map/all_to_all | solution.py:506
  810.2 87.7 %all-to-all-start.3 = ((bf16[8,256,1024]{2,1,0:T(8,128)(2,1)}), bf16[8,256,1024]{2,1,0:T(8,128)(2,1)}, u32[]{:S(2)}, u32[]{:S(2)}) async-start(bf16[8,256,1024]{2,1,0:T(8,128)(2,1)} %add_convert_fusion.2), calls=%async_computation.3 | async-start | bytes 8388608 | tf_op jit(solution)/shard_map/all_to_all | solution.py:506
  815.6 82.3 %collective-permute-start.8 = (bf16[8,64,4096]{2,1,0:T(8,128)(2,1)}, bf16[8,64,4096]{2,1,0:T(8,128)(2,1)}, u32[]{:S(2)}, u32[]{:S(2)}) collective-permute-start(bf16[8,64,4096]{2,1,0:T(8,128)(2,1)} %get-tuple-element.169), channel_id=1, source_target_pairs={{0,1},{1,0},{2,3},{3,2},{4,5},{5,4},{6,7},{7,6},{8,9},{9,8},{10,11... | collective-permute-start | bytes 12582920 | tf_op jit(solution)/shard_map/ppermute | solution.py:442
  932.1 59.0 %collective-permute-start.9 = (bf16[8,4,64,1024]{3,2,1,0:T(8,128)(2,1)}, bf16[8,4,64,1024]{3,2,1,0:T(8,128)(2,1)}, u32[]{:S(2)}, u32[]{:S(2)}) collective-permute-start(bf16[8,4,64,1024]{3,2,1,0:T(8,128)(2,1)} %get-tuple-element.182), channel_id=1, source_target_pairs={{0,1},{1,0},{2,3},{3,2},{4,5},{5,4},{6,7},{7,6},{8,9},{9,8},{10,11... | collective-permute-start | bytes 12582920 | tf_op jit(solution)/shard_map/ppermute | solution.py:442
  932.6 58.5 %all-to-all-start.4 = ((bf16[8,64,4096]{2,1,0:T(8,128)(2,1)}), bf16[8,64,4096]{2,1,0:T(8,128)(2,1)}, u32[]{:S(2)}, u32[]{:S(2)}) async-start(bf16[8,64,4096]{2,1,0:T(8,128)(2,1)} %add_convert_fusion.1), calls=%async_computation.4 | async-start | bytes 8388608 | tf_op jit(solution)/shard_map/all_to_all | solution.py:506
  1023.9 71.1 %all-to-all-start.5 = ((bf16[8,4,64,1024]{3,2,1,0:T(8,128)(2,1)}), bf16[8,4,64,1024]{3,2,1,0:T(8,128)(2,1)}, u32[]{:S(2)}, u32[]{:S(2)}) async-start(bf16[8,4,64,1024]{3,2,1,0:T(8,128)(2,1)} %add_convert_fusion), calls=%async_computation.5 | async-start | bytes 8388608 | tf_op jit(solution)/shard_map/all_to_all | solution.py:506
  1031.7 34.0 %collective-permute-start.10 = (f32[8,2,832]{2,0,1:T(8,128)S(1)}, f32[8,2,832]{2,0,1:T(8,128)S(1)}, u32[]{:S(2)}, u32[]{:S(2)}) collective-permute-start(f32[8,2,832]{2,0,1:T(8,128)S(1)} %broadcast_select_fusion.2), channel_id=1, source_target_pairs={{0,8},{1,9},{2,10},{3,11},{4,12},{5,13},{6,14},{7,15},{8,0},{9,1},... | collective-permute-start | bytes 159752 | tf_op jit(solution)/shard_map/ppermute | solution.py:442
  1065.7 19.6 %collective-permute-start.11 = (f32[4,2,832]{2,0,1:T(4,128)S(1)}, f32[4,2,832]{2,0,1:T(4,128)S(1)}, u32[]{:S(2)}, u32[]{:S(2)}) collective-permute-start(f32[4,2,832]{2,0,1:T(4,128)S(1)} %slice_select_fusion), channel_id=1, source_target_pairs={{0,4},{1,5},{2,6},{3,7},{4,0},{5,1},{6,2},{7,3},{8,12},{9,13},{10,... | collective-permute-start | bytes 79880 | tf_op jit(solution)/shard_map/ppermute | solution.py:442
  1085.4 5.6 collective-permute-start.12
  (14 other events, 69.6 us)
Sparse Core Ops, SparseCore 0:
  10.8 52.0 all-gather.12
  65.2 48.9 all-gather.14
  116.5 48.9 all-gather.16
  168.3 49.0 all-gather.18
  219.5 49.0 all-gather.20
  270.6 48.9 all-gather.22

commit v4 on v3

--- a/solution.py
+++ b/solution.py
@@ -112,8 +112,10 @@
     return x * cos + other * (sin * sign)
 
 
-def attn_bwd_kernel(len_ref, q_ref, k_ref, v_ref, o_ref, do_ref, p_ref, cos_ref, sin_ref, dq_ref, dk_ref, dv_ref,
-                    doh_ref, qh_ref, kt_ref, d_ref, ds_ref, dqt_ref):
+def attn_bwd_kernel(axis, units, last, q_ref, k_ref, v_ref, o_ref, do_ref, p_ref, cos_ref, sin_ref, *refs):
+    pairs, (dq_ref, dk_ref, dv_ref), lands = refs[:units], refs[units:units + 3], refs[units + 3:2 * units + 3]
+    doh_ref, qh_ref, kt_ref, d_ref, ds_ref, dqt_ref, *sems = refs[2 * units + 3:]
+    ride(axis, last, pl.program_id(0) * pl.num_programs(1) + pl.program_id(1), pairs, lands, *sems)
     lane = lane_iota(1)
     for h in range(2):
         own = ((lane // HEAD_DIM) == h).astype(jnp.float32).astype(jnp.bfloat16)
@@ -136,25 +138,23 @@
     dq_ref[...] = (spin(dqt_ref[...].T, cos_ref[...], sin_ref[...], -1.0) * (HEAD_DIM ** -0.5)).astype(jnp.bfloat16)
 
 
-def attn_bwd(lengths, q, k, v, ctx, d_ctx, probs, cos_tab, sin_tab):
+def attn_bwd(axis, number, units, q, k, v, ctx, d_ctx, probs, cos_tab, sin_tab):
     tokens, width = q.shape
     seqs, pairs = tokens // SEQ, width // PAIR
-    spec = pl.BlockSpec((SEQ, PAIR), lambda b, h, n: (b, h))
-    table = pl.BlockSpec((SEQ, PAIR), lambda b, h, n: (0, 0))
-    return pl.pallas_call(
-        attn_bwd_kernel,
-        grid_spec=pltpu.PrefetchScalarGridSpec(
-            num_scalar_prefetch=1, grid=(seqs, pairs),
-            in_specs=[spec] * 5 + [pl.BlockSpec((None, 2, SEQ, SEQ), lambda b, h, n: (b, h, 0, 0)), table, table],
-            out_specs=[spec] * 3,
-            scratch_shapes=[pltpu.VMEM((2, SEQ, PAIR), jnp.bfloat16), pltpu.VMEM((2, SEQ, PAIR), jnp.bfloat16),
-                            pltpu.VMEM((PAIR, SEQ), jnp.bfloat16), pltpu.VMEM((8, SEQ), jnp.float32),
-                            pltpu.VMEM((2, SEQ, SEQ), jnp.bfloat16), pltpu.VMEM((PAIR, SEQ), jnp.float32)]),
-        out_shape=[jax.ShapeDtypeStruct((tokens, width), jnp.bfloat16)] * 3,
-        compiler_params=pltpu.CompilerParams(dimension_semantics=("arbitrary", "arbitrary"), vmem_limit_bytes=56 << 20),
+    spec = pl.BlockSpec((SEQ, PAIR), lambda b, h: (b, h))
+    table = pl.BlockSpec((SEQ, PAIR), lambda b, h: (0, 0))
+    return pl.pallas_call(
+        functools.partial(attn_bwd_kernel, axis, len(units), seqs * pairs - 1), grid=(seqs, pairs),
+        in_specs=[spec] * 5 + [pl.BlockSpec((None, 2, SEQ, SEQ), lambda b, h: (b, h, 0, 0)), table, table] + ride_specs(units),
+        out_specs=[spec] * 3 + ride_specs(units),
+        scratch_shapes=[pltpu.VMEM((2, SEQ, PAIR), jnp.bfloat16), pltpu.VMEM((2, SEQ, PAIR), jnp.bfloat16),
+                        pltpu.VMEM((PAIR, SEQ), jnp.bfloat16), pltpu.VMEM((8, SEQ), jnp.float32),
+                        pltpu.VMEM((2, SEQ, SEQ), jnp.bfloat16), pltpu.VMEM((PAIR, SEQ), jnp.float32)] + ride_scratch(len(units)),
+        out_shape=[jax.ShapeDtypeStruct((tokens, width), jnp.bfloat16)] * 3 + same(units),
+        compiler_params=ride_params(number, 'arbitrary', 'arbitrary'),
         cost_estimate=pl.CostEstimate(flops=8 * tokens * SEQ * width * 4, bytes_accessed=100 << 20, transcendentals=0),
         name='attn_bwd',
-    )(lengths, q, k, v, ctx, d_ctx, probs, cos_tab, sin_tab)
+    )(q, k, v, ctx, d_ctx, probs, cos_tab, sin_tab, *units)
 
 
 EPS = 1e-5
@@ -202,6 +202,61 @@
 
 def eights(x):
     return jnp.sum(x.reshape(x.shape[0] // 8, 8, x.shape[1]), axis=0)
+
+
+def ride(axis, last, step, pairs, lands, send_sem, recv_sem, own_sem):
+    me = lax.axis_index(axis)
+    side, chip = me % 2, me // 2
+    chips = pairs[0].shape[0]
+
+    def peer(j):
+        return ((chip + j) % chips) * 2 + side
+
+    def copies():
+        made = []
+        for u, (pair, land) in enumerate(zip(pairs, lands)):
+            for j in range(1, chips):
+                made.append(pltpu.make_async_remote_copy(
+                    src_ref=pair.at[(chip + j) % chips], dst_ref=land.at[chip], send_sem=send_sem.at[u, j], recv_sem=recv_sem.at[u, j],
+                    device_id=(peer(j),), device_id_type=MESH))
+            made.append(pltpu.make_async_copy(pair.at[chip], land.at[chip], own_sem.at[u]))
+        return made
+
+    @pl.when(step == 0)
+    def _():
+        barrier = pltpu.get_barrier_semaphore()
+        for j in range(1, chips):
+            pl.semaphore_signal(barrier, inc=1, device_id=(peer(j),), device_id_type=MESH)
+
+    @pl.when(step == 1)
+    def _():
+        pl.semaphore_wait(pltpu.get_barrier_semaphore(), chips - 1)
+        for c in copies():
+            c.start()
+
+    @pl.when(step == last)
+    def _():
+        for c in copies():
+            c.wait()
+
+
+MESH = pl.DeviceIdType.MESH
+
+
+def ride_scratch(units):
+    return [pltpu.SemaphoreType.DMA((units, 8)), pltpu.SemaphoreType.DMA((units, 8)), pltpu.SemaphoreType.DMA((units,))]
+
+
+def ride_specs(pairs):
+    return [pl.BlockSpec(memory_space=pl.ANY)] * len(pairs)
+
+
+def same(pairs):
+    return [jax.ShapeDtypeStruct(p.shape, p.dtype) for p in pairs]
+
+
+def ride_params(number, *semantics):
+    return pltpu.CompilerParams(dimension_semantics=semantics or ('arbitrary',), vmem_limit_bytes=HIGH, collective_id=number, has_side_effects=True)
 
 
 def qkv_kernel(x_ref, w_ref, b_ref, ln_ref, cos_ref, sin_ref, h_ref, q_ref, k_ref, v_ref):
@@ -279,8 +334,9 @@
     )(h, mid, wu, bu, wd, bd)
 
 
-def mlp_back_kernel(dy_ref, slope_ref, wd_ref, wu_ref, mid_ref, ln_ref, wo_ref,
-                    dpre_ref, dmid_ref, dctx_ref, gbu_ref, gln_ref):
+def mlp_back_kernel(axis, units, last, dy_ref, slope_ref, wd_ref, wu_ref, mid_ref, ln_ref, wo_ref, *refs):
+    pairs, (dpre_ref, dmid_ref, dctx_ref, gbu_ref, gln_ref), lands, sems = refs[:units], refs[units:units + 5], refs[units + 5:2 * units + 5], refs[2 * units + 5:]
+    ride(axis, last, pl.program_id(0), pairs, lands, *sems)
     dy = dy_ref[...]
     grad = None
     wide = wu_ref.shape[1]
@@ -308,23 +364,28 @@
     dctx_ref[...] = dot(dmid, wo_ref[...], NT).astype(jnp.bfloat16)
 
 
-def mlp_back(dy, slope, wd, wu, mid, ln, wo):
+def mlp_back(axis, number, pairs, dy, slope, wd, wu, mid, ln, wo):
     tokens, width = dy.shape
     wide = wu.shape[1]
     block = 256
     row, long = rows_of(block, width), rows_of(block, wide)
     half = jax.ShapeDtypeStruct(dy.shape, jnp.bfloat16)
     return pl.pallas_call(
-        mlp_back_kernel, grid=(tokens // block,),
-        in_specs=[row, long, whole(wd.shape), whole(wu.shape), row, whole(ln.shape), part_of((None, width, width), 3, 0, 0)],
-        out_specs=[long, row, row, partial((8, wide)), partial((24, width))],
+        functools.partial(mlp_back_kernel, axis, len(pairs), tokens // block - 1), grid=(tokens // block,),
+        in_specs=[row, long, whole(wd.shape), whole(wu.shape), row, whole(ln.shape), part_of((None, width, width), 3, 0, 0)] + ride_specs(pairs),
+        out_specs=[long, row, row, partial((8, wide)), partial((24, width))] + ride_specs(pairs),
         out_shape=[jax.ShapeDtypeStruct((tokens, wide), jnp.bfloat16), half, half,
-                   jax.ShapeDtypeStruct((8, wide), jnp.float32), jax.ShapeDtypeStruct((24, width), jnp.float32)],
-        compiler_params=params(), cost_estimate=cost(2 * tokens * width * (2 * wide + width), 90 << 20), name='mlp_back',
-    )(dy, slope, wd, wu, mid, ln, wo)
-
-
-def in_back_kernel(dq_ref, dk_ref, dv_ref, w_ref, x_ref, ln_ref, dmid_ref, dx_ref, gln_ref):
+                   jax.ShapeDtypeStruct((8, wide), jnp.float32), jax.ShapeDtypeStruct((24, width), jnp.float32)] + same(pairs),
+        scratch_shapes=ride_scratch(len(pairs)),
+        compiler_params=ride_params(number), cost_estimate=cost(2 * tokens * width * (2 * wide + width), 90 << 20), name='mlp_back',
+    )(dy, slope, wd, wu, mid, ln, wo, *pairs)
+
+
+def in_back_kernel(axis, units, last, dq_ref, dk_ref, dv_ref, w_ref, x_ref, ln_ref, dmid_ref, *refs):
+    pairs, (dx_ref, gln_ref), lands, sems = refs[:units], refs[units:units + 2], refs[units + 2:2 * units + 2], refs[2 * units + 2:]
+    if units:
+        ride(axis, last, pl.program_id(0), pairs, lands, *sems)
+
     @pl.when(pl.program_id(0) == 0)
     def _():
         gln_ref[...] = jnp.zeros_like(gln_ref)
@@ -336,95 +397,154 @@
     gln_ref[8:16] += eights(grad)
 
 
-def in_back(dq, dk, dv, w, x, ln, dmid):
+def in_back(axis, number, pairs, dq, dk, dv, w, x, ln, dmid):
     tokens, width = x.shape
     block = 512
     row = rows_of(block, width)
     return pl.pallas_call(
-        in_back_kernel, grid=(tokens // block,),
-        in_specs=[row, row, row, part_of((3, width, width), 0, 0, 0), row, whole(ln.shape), row],
-        out_specs=[row, partial((16, width))],
-        out_shape=[jax.ShapeDtypeStruct(x.shape, jnp.bfloat16), jax.ShapeDtypeStruct((16, width), jnp.float32)],
-        compiler_params=params(), cost_estimate=cost(6 * tokens * width * width, 34 << 20), name='in_back',
-    )(dq, dk, dv, w, x, ln, dmid)
-
-
-def share(grad, side, keep_ref, give_ref, at):
-    low, high = grad
-    keep_ref[at] = jnp.where(side == 0, low, high).astype(jnp.bfloat16)
-    give_ref[at] = jnp.where(side == 0, high, low).astype(jnp.bfloat16)
-
-
-def down_grad_kernel(side_ref, a_ref, b_ref, keep_ref, give_ref):
-    grad = dot(a_ref[...], b_ref[...], TN)
-    half = grad.shape[0] // 2
-    share((grad[:half], grad[half:]), side_ref[0], keep_ref, give_ref, ...)
-
-
-def down_grad(side, a, b):
+        functools.partial(in_back_kernel, axis, len(pairs), tokens // block - 1), grid=(tokens // block,),
+        in_specs=[row, row, row, part_of((3, width, width), 0, 0, 0), row, whole(ln.shape), row] + ride_specs(pairs),
+        out_specs=[row, partial((16, width))] + ride_specs(pairs),
+        out_shape=[jax.ShapeDtypeStruct(x.shape, jnp.bfloat16), jax.ShapeDtypeStruct((16, width), jnp.float32)] + same(pairs),
+        scratch_shapes=ride_scratch(len(pairs)) if pairs else [],
+        compiler_params=ride_params(number) if pairs else params(), cost_estimate=cost(6 * tokens * width * width, 34 << 20), name='in_back',
+    )(dq, dk, dv, w, x, ln, dmid, *pairs)
+
+
+def swap_step(axis, steps, make, keep_ref, send_ref, recv_ref, send_sem, recv_sem, out_ref):
+    i = pl.program_id(0)
+    me = lax.axis_index(axis)
+    side = me % 2
+    other = me + 1 - 2 * side
+
+    def copy(j):
+        return pltpu.make_async_remote_copy(
+            src_ref=send_ref.at[j], dst_ref=recv_ref.at[j], send_sem=send_sem.at[j], recv_sem=recv_sem.at[j],
+            device_id=(other,), device_id_type=MESH)
+
+    def put(at, low, high):
+        keep_ref[(i % 3,) + at] = jnp.where(side == 0, low, high)
+        send_ref[(i,) + at] = jnp.where(side == 0, high, low).astype(jnp.bfloat16)
+
+    def finish():
+        out_ref[...] = (keep_ref[(i + 1) % 3] + recv_ref[i - 2].astype(jnp.float32)).astype(jnp.bfloat16)
+
+    @pl.when(i == 0)
+    def _():
+        barrier = pltpu.get_barrier_semaphore()
+        pl.semaphore_signal(barrier, inc=1, device_id=(other,), device_id_type=MESH)
+        pl.semaphore_wait(barrier, 1)
+
+    @pl.when((i >= 1) & (i <= steps))
+    def _():
+        copy(i - 1).start()
+
+    @pl.when(i >= 2)
+    def _():
+        copy(i - 2).wait()
+
+    @pl.when(i < 2)
+    def _():
+        make(put)
+
+    @pl.when((i >= 2) & (i < steps))
+    def _():
+        make(put)
+        finish()
+
+    @pl.when(i >= steps)
+    def _():
+        finish()
+
+
+def swap_scratch(steps, block):
+    return [pltpu.VMEM((3,) + block, jnp.float32), pltpu.VMEM((steps,) + block, jnp.bfloat16), pltpu.VMEM((steps,) + block, jnp.bfloat16),
+            pltpu.SemaphoreType.DMA((steps,)), pltpu.SemaphoreType.DMA((steps,))]
+
+
+def swap_params(number):
+    return pltpu.CompilerParams(dimension_semantics=('arbitrary',), vmem_limit_bytes=HIGH, collective_id=number, has_side_effects=True)
+
+
+def down_grad_kernel(axis, steps, a_ref, b_ref, out_ref, *scratch):
+    def make(put):
+        grad = dot(a_ref[...], b_ref[...], TN)
+        half = grad.shape[0] // 2
+        put((), grad[:half], grad[half:])
+
+    swap_step(axis, steps, make, *scratch, out_ref)
+
+
+def down_grad(axis, number, a, b):
     tokens, m = a.shape
     n = b.shape[1]
     chips = 8
     block = m // chips
-    out = pl.BlockSpec((None, block // 2, n), lambda i, s: (i, 0, 0))
-    return pl.pallas_call(
-        down_grad_kernel,
-        grid_spec=pltpu.PrefetchScalarGridSpec(
-            num_scalar_prefetch=1, grid=(chips,),
-            in_specs=[pl.BlockSpec((tokens, block), lambda i, s: (0, i)), whole(b.shape)], out_specs=[out, out]),
-        out_shape=[jax.ShapeDtypeStruct((chips, block // 2, n), jnp.bfloat16)] * 2,
-        compiler_params=params(), cost_estimate=cost(2 * tokens * m * n, 2 * (tokens * (m + n) + m * n)), name='down_grad',
-    )(side, a, b)
-
-
-def up_grad_kernel(side_ref, a_ref, b_ref, keep_ref, give_ref):
-    grad = dot(a_ref[...], b_ref[...], TN)
-    chips, half = keep_ref.shape[0], keep_ref.shape[1]
-    for i in range(chips):
-        r = 2 * i * half
-        share((grad[r:r + half], grad[r + half:r + 2 * half]), side_ref[0], keep_ref, give_ref, i)
-
-
-def up_grad(side, a, b):
+    return pl.pallas_call(
+        functools.partial(down_grad_kernel, axis, chips), grid=(chips + 2,),
+        in_specs=[pl.BlockSpec((tokens, block), lambda i: (0, jnp.minimum(i, chips - 1))), whole(b.shape)],
+        out_specs=pl.BlockSpec((None, block // 2, n), lambda i: (jnp.maximum(i - 2, 0), 0, 0)),
+        out_shape=jax.ShapeDtypeStruct((chips, block // 2, n), jnp.bfloat16),
+        scratch_shapes=swap_scratch(chips, (block // 2, n)),
+        compiler_params=swap_params(number), cost_estimate=cost(2 * tokens * m * n, 2 * (tokens * (m + n) + m * n)), name='down_grad',
+    )(a, b)
+
+
+def up_grad_kernel(axis, steps, a_ref, b_ref, out_ref, *scratch):
+    def make(put):
+        grad = dot(a_ref[...], b_ref[...], TN)
+        chips, half = out_ref.shape[0], out_ref.shape[1]
+        for c in range(chips):
+            r = 2 * c * half
+            put((c,), grad[r:r + half], grad[r + half:r + 2 * half])
+
+    swap_step(axis, steps, make, *scratch, out_ref)
+
+
+def up_grad(axis, number, a, b):
     tokens, m = a.shape
     n = b.shape[1]
     chips, block = 8, 512
-    out = pl.BlockSpec((chips, m // chips // 2, block), lambda i, s: (0, 0, i))
-    return pl.pallas_call(
-        up_grad_kernel,
-        grid_spec=pltpu.PrefetchScalarGridSpec(
-            num_scalar_prefetch=1, grid=(n // block,),
-            in_specs=[whole(a.shape), pl.BlockSpec((tokens, block), lambda i, s: (0, i))], out_specs=[out, out]),
-        out_shape=[jax.ShapeDtypeStruct((chips, m // chips // 2, n), jnp.bfloat16)] * 2,
-        compiler_params=params(), cost_estimate=cost(2 * tokens * m * n, 2 * (tokens * (m + n) + m * n)), name='up_grad',
-    )(side, a, b)
-
-
-def attn_grad_kernel(side_ref, h_ref, ctx_ref, dq_ref, dk_ref, dv_ref, dmid_ref, keep_ref, give_ref, gb_ref):
-    chips, half = keep_ref.shape[0], keep_ref.shape[2]
-    for j, d_ref in enumerate((dq_ref, dk_ref, dv_ref, dmid_ref)):
-        grad = dot((h_ref if j < 3 else ctx_ref)[...], d_ref[...], TN)
-        for i in range(chips):
-            r = 2 * i * half
-            share((grad[r:r + half], grad[r + half:r + 2 * half]), side_ref[0], keep_ref, give_ref, (i, j))
-        gb_ref[8 * j:8 * j + 8] = eights(d_ref[...].astype(jnp.float32))
-
-
-def attn_grad(side, h, ctx, dq, dk, dv, dmid):
+    steps = n // block
+    half = m // chips // 2
+    return pl.pallas_call(
+        functools.partial(up_grad_kernel, axis, steps), grid=(steps + 2,),
+        in_specs=[whole(a.shape), pl.BlockSpec((tokens, block), lambda i: (0, jnp.minimum(i, steps - 1)))],
+        out_specs=pl.BlockSpec((chips, half, block), lambda i: (0, 0, jnp.maximum(i - 2, 0))),
+        out_shape=jax.ShapeDtypeStruct((chips, half, n), jnp.bfloat16),
+        scratch_shapes=swap_scratch(steps, (chips, half, block)),
+        compiler_params=swap_params(number), cost_estimate=cost(2 * tokens * m * n, 2 * (tokens * (m + n) + m * n)), name='up_grad',
+    )(a, b)
+
+
+def attn_grad_kernel(axis, steps, h_ref, ctx_ref, dq_ref, dk_ref, dv_ref, dmid_ref, out_ref, gb_ref, *scratch):
+    def make(put):
+        chips, half = out_ref.shape[0], out_ref.shape[2]
+        for j, d_ref in enumerate((dq_ref, dk_ref, dv_ref, dmid_ref)):
+            grad = dot((h_ref if j < 3 else ctx_ref)[...], d_ref[...], TN)
+            for c in range(chips):
+                r = 2 * c * half
+                put((c, j), grad[r:r + half], grad[r + half:r + 2 * half])
+            gb_ref[8 * j:8 * j + 8] = eights(d_ref[...].astype(jnp.float32))
+
+    swap_step(axis, steps, make, *scratch, out_ref)
+
+
+def attn_grad(axis, number, h, ctx, dq, dk, dv, dmid):
     tokens, width = h.shape
     chips, block = 8, 256
-    cols = pl.BlockSpec((tokens, block), lambda i, s: (0, i))
-    out = pl.BlockSpec((chips, 4, width // chips // 2, block), lambda i, s: (0, 0, 0, i))
-    return pl.pallas_call(
-        attn_grad_kernel,
-        grid_spec=pltpu.PrefetchScalarGridSpec(
-            num_scalar_prefetch=1, grid=(width // block,),
-            in_specs=[whole(h.shape), whole(ctx.shape), cols, cols, cols, cols],
-            out_specs=[out, out, pl.BlockSpec((32, block), lambda i, s: (0, i))]),
-        out_shape=[jax.ShapeDtypeStruct((chips, 4, width // chips // 2, width), jnp.bfloat16)] * 2
-        + [jax.ShapeDtypeStruct((32, width), jnp.float32)],
-        compiler_params=params(), cost_estimate=cost(8 * tokens * width * width, 32 << 20), name='attn_grad',
-    )(side, h, ctx, dq, dk, dv, dmid)
+    steps = width // block
+    half = width // chips // 2
+    cols = pl.BlockSpec((tokens, block), lambda i: (0, jnp.minimum(i, steps - 1)))
+    return pl.pallas_call(
+        functools.partial(attn_grad_kernel, axis, steps), grid=(steps + 2,),
+        in_specs=[whole(h.shape), whole(ctx.shape), cols, cols, cols, cols],
+        out_specs=[pl.BlockSpec((chips, 4, half, block), lambda i: (0, 0, 0, jnp.maximum(i - 2, 0))),
+                   pl.BlockSpec((32, block), lambda i: (0, jnp.minimum(i, steps - 1)))],
+        out_shape=[jax.ShapeDtypeStruct((chips, 4, half, width), jnp.bfloat16), jax.ShapeDtypeStruct((32, width), jnp.float32)],
+        scratch_shapes=swap_scratch(steps, (chips, 4, half, block)),
+        compiler_params=swap_params(number), cost_estimate=cost(8 * tokens * width * width, 32 << 20), name='attn_grad',
+    )(h, ctx, dq, dk, dv, dmid)
 
 
 def rotary_tables():
@@ -495,15 +615,7 @@
         n, nu = b_attn.shape[2], b_up.shape[1]
         cos, sin = rotary_tables()
         gather = functools.partial(lax.all_gather, axis_name=axis_name, tiled=True)
-        side = bit_of(axis_name, 'c').reshape(1)
         after = lax.optimization_barrier
-
-        def join(keep, got):
-            return (keep.astype(jnp.float32) + got.astype(jnp.float32)).astype(jnp.bfloat16)
-
-        def spread_out(pair):
-            groups = [[2 * i + c for i in range(8)] for c in range(2)]
-            return lax.all_to_all(pair, axis_name, split_axis=0, concat_axis=0, axis_index_groups=groups, tiled=True)
 
         def total(parts):
             return jnp.sum(parts.astype(jnp.float32), axis=0)
@@ -524,42 +636,28 @@
             hidden = out
         grad = d_y.reshape(tokens, width)
         grads = [None] * layers
+        number = 0
+        waiting = None
         for l in reversed(range(layers)):
-            if l + 1 < layers:
-                flying = spread_out(pair)
             x_in, h_one, q, k, v, ctx, probs, mid, h_two, act, slope, wa, wu, wd, ln = saved[l]
-            keep, give = down_grad(side, act, grad)
-            give, grad = after((give, grad))
-            got = swap(give, axis_name, 'c')
-            d_pre, d_mid, d_ctx, gb_up, gln_two = mlp_back(grad, slope, wd, wu, mid, ln, wa)
-            got, d_pre = after((got, d_pre))
-            if l + 1 < layers:
-                flying, d_pre = after((flying, d_pre))
-                grads[l + 1][0] = total(flying)
-            pair, d_pre = after((join(keep, got), d_pre))
-            flying = spread_out(pair)
-            keep, give = up_grad(side, h_two, d_pre)
-            give, d_ctx = after((give, d_ctx))
-            got = swap(give, axis_name, 'c')
-            dq, dk, dv = attn_bwd(lengths, q, k, v, ctx, d_ctx, probs, cos, sin)
-            flying, got, dq = after((flying, got, dq))
-            g_down = total(flying)
-            pair, dq = after((join(keep, got), dq))
-            flying = spread_out(pair)
-            keep, give, gb_attn = attn_grad(side, h_one, ctx, dq, dk, dv, d_mid)
-            give, dq = after((give, dq))
-            got = swap(give, axis_name, 'c')
-            if l > 0:
-                grad, gln_one = in_back(dq, dk, dv, wa, x_in, ln, d_mid)
-                flying, got, grad = after((flying, got, grad))
-                g_up = total(flying)
-                pair, grad = after((join(keep, got), grad))
+            pair_down, grad = after((down_grad(axis_name, number, act, grad), grad))
+            carried = [pair_down] if l + 1 == layers else [waiting]
+            d_pre, d_mid, d_ctx, gb_up, gln_two, landed = mlp_back(axis_name, number + 1, carried, grad, slope, wd, wu, mid, ln, wa)
+            if l + 1 == layers:
+                g_down, carried = total(landed), []
             else:
-                flying, got, dq = after((flying, got, dq))
-                g_up = total(flying)
-                pair, dq = after((join(keep, got), dq))
-                flying = spread_out(pair)
-                grad, gln_one = in_back(dq, dk, dv, wa, x_in, ln, d_mid)
+                grads[l + 1][0], carried = total(landed), [pair_down]
+            pair_up, d_ctx = after((up_grad(axis_name, number + 2, h_two, d_pre), d_ctx))
+            dq, dk, dv, landed, *rest = attn_bwd(axis_name, number + 3, [pair_up] + carried, q, k, v, ctx, d_ctx, probs, cos, sin)
+            g_up = total(landed)
+            if rest:
+                g_down = total(rest[0])
+            waiting, gb_attn = attn_grad(axis_name, number + 4, h_one, ctx, dq, dk, dv, d_mid)
+            waiting, dq = after((waiting, dq))
+            carried = [waiting] if l == 0 else []
+            grad, gln_one, *rest = in_back(axis_name, number + 5, carried, dq, dk, dv, wa, x_in, ln, d_mid)
+            g_attn = total(rest[0]) if rest else None
+            number += 6
             sums_two = jnp.sum(gln_two.reshape(3, 8, width), axis=1)
             sums_one = jnp.sum(gln_one.reshape(2, 8, width), axis=1)
             gb_four = jnp.sum(gb_attn.reshape(4, 8, width), axis=1)
@@ -567,9 +665,8 @@
             by_dev = lambda s: s.reshape(-1, 16, n).transpose(1, 0, 2).reshape(16, -1)
             packed = jnp.concatenate([by_dev(gb_four), by_dev(sums_one), by_dev(sums_two[:2]),
                                       gb_wide.reshape(16, nu), by_dev(sums_two[2:3])], axis=1)
-            grads[l] = [None, g_up, g_down, packed]
+            grads[l] = [g_attn, g_up, g_down, packed]
         got = scatter_packed(jnp.stack([g[3] for g in grads], axis=1), axis_name)
-        grads[0][0] = total(flying)
         g_attn, g_up, g_down = (jnp.stack([g[i] for g in grads]) for i in range(3))
         return (grad.reshape(x.shape), g_attn, got[:, :4 * n].reshape(layers, 4, n), got[:, 4 * n:8 * n].reshape(layers, 4, n),
                 g_up, got[:, 8 * n:8 * n + nu], g_down, got[:, 8 * n + nu:])

time: 1120 us -> 1070 us (0.955)
  Pallas kernels: 802 us -> 957 us
  waiting for transfers between devices: 134 us -> 34.6 us
  starting transfers between devices: 66.6 us -> 9.9 us
  other arithmetic: 74.1 us -> 22.8 us
    pallas_call x12, Pallas kernels: 470 us -> 625 us  [the longest x2 205 us: attn_bwd(): pl.pallas_call(functools.partial(attn_bwd_kernel, axis, len(units), seqs...]
    all_to_all x6 -> x0, waiting for transfers between devices: 71.1 us -> none  [spread_out(): lax.all_to_all(pair, axis_name, split_axis=0, concat_axis=0, axis_index_g...]
    convert_element_type x6 -> x0, other arithmetic: 45.5 us -> none  [join(): (keep.astype(jnp.float32) + got.astype(jnp.float32)).astype(jnp.bfloat16)]
    all_to_all x6 -> x0, starting transfers between devices: 36.4 us -> none  [spread_out(): lax.all_to_all(pair, axis_name, split_axis=0, concat_axis=0, axis_index_g...]
    ppermute x14 -> x8, waiting for transfers between devices: 33.4 us -> 5.29 us  [swap(): lax.ppermute(value, axis_name, [(i, i ^ BITS[dim]) for i in range(16)])]
    ppermute x14 -> x8, starting transfers between devices: 29.9 us -> 9.66 us  [swap(): lax.ppermute(value, axis_name, [(i, i ^ BITS[dim]) for i in range(16)])]
  transfers between devices with their start and end apart: 26 -> 14, of which waited for: 8 -> 6; matrix products, arithmetic and copies ran while one was open for 3% -> 2% of each run, Pallas kernels for 52% -> 26%
where the time goes in v4:
time: 1070 us; the launch traced here: 1060 us
  Pallas kernels  957 us (89%)
  waiting for transfers between devices  34.6 us (3%)
  other arithmetic  22.8 us (2%)
  local copies, waits for them, and re-layouts  21 us (2%)
  between operations  15.2 us (1%)
    pallas_call x2, Pallas kernels, attn_bwd(): pl.pallas_call(functools.partial(attn_bwd_kernel, axis, len(units), seqs...  205 us
    pallas_call x2, Pallas kernels, mlp_back(): pl.pallas_call(functools.partial(mlp_back_kernel, axis, len(pairs), token...  156 us
    pallas_call x2, Pallas kernels, attn_fwd(): pl.pallas_call(attn_fwd_kernel, grid_spec=pltpu.PrefetchScalarGridSpec(nu...  153 us
    pallas_call x2, Pallas kernels, mlp(): pl.pallas_call(mlp_kernel, grid=(tokens // block,), in_specs=[row, row, w...  116 us
    pallas_call x2, Pallas kernels, in_back(): pl.pallas_call(functools.partial(in_back_kernel, axis, len(pairs), tokens...  98.7 us
    pallas_call x2, Pallas kernels, attn_grad(): pl.pallas_call(functools.partial(attn_grad_kernel, axis, steps), grid=(st...  60.6 us
    pallas_call x2, Pallas kernels, up_grad(): pl.pallas_call(functools.partial(up_grad_kernel, axis, steps), grid=(step...  52.9 us
    pallas_call x2, Pallas kernels, down_grad(): pl.pallas_call(functools.partial(down_grad_kernel, axis, chips), grid=(ch...  52.8 us
  transfers between devices with their start and end apart: 14, of which 6 were waited for; matrix products, arithmetic and copies ran while one was open for 2% of the time, Pallas kernels for 26%

profile of v4, /device:TPU:0, one launch (start us, length us, event | category | flops | bytes accessed | tf_op | source)
XLA Modules:
  0.0 1061.1 jit_solution(5123396925080337288)
XLA Ops:
  35.3 27.7 %all-gather.13.cloned.1.call-done = bf16[1,4,1024,1024]{3,2,1,0:T(8,128)(2,1)} async-done(((bf16[1,4,64,1024]{3,2,1,0:T(8,128)(2,1)}), bf16[1,4,1024,1024]{3,2,1,0:T(8,128)(2,1)}) %all-gather.13.cloned.1.call-update) | async-done | bytes 8388624 | tf_op jit(solution)/shard_map/all_gather | solution.py:628
  63.0 20.2 %qkv.2 = (bf16[2048,1024]{1,0:T(8,128)(2,1)}, bf16[2048,1024]{1,0:T(8,128)(2,1)}, bf16[2048,1024]{1,0:T(8,128)(2,1)}, bf16[2048,1024]{1,0:T(8,128)(2,1)}) custom-call(bf16[2048,1024]{1,0:T(8,128)(2,1)} %bitcast.83, bf16[4,1024,1024]{2,1,0:T(8,128)(2,1)} %bitcast.68, f32[4,1024]{1,0:T(4,128)} %reshape.147.b_ref, f32[4,1024]{1,0:T(4,128)} %reshape.149.ln_ref, ...), custom_call_target="tpu_custom_call" | custom-call | flops 12884901888 | bytes 27262976 | tf_op jit(solution)/shard_map/qkv/pallas_call | solution.py:281
  83.2 76.3 %attn_fwd.2 = (bf16[2048,1024]{1,0:T(8,128)(2,1)}, bf16[2,16,1024,1024]{3,2,1,0:T(8,128)(2,1)}) custom-call(s32[2]{0:T(128)} %len_ref.3, bf16[2048,1024]{1,0:T(8,128)(2,1)} %get-tuple-element.72.q_ref, bf16[2048,1024]{1,0:T(8,128)(2,1)} %get-tuple-element.73.k_ref, bf16[2048,1024]{1,0:T(8,128)(2,1)} %get-tuple-element.74.v_ref), custom_call_target="tpu_custom_call" | custom-call | flops 34359738368 | bytes 94371840 | tf_op jit(solution)/shard_map/attn_fwd/pallas_call | solution.py:91
  159.5 11.4 %out_proj.2 = (bf16[2048,1024]{1,0:T(8,128)(2,1)}, bf16[2048,1024]{1,0:T(8,128)(2,1)}) custom-call(bf16[2048,1024]{1,0:T(8,128)(2,1)} %get-tuple-element.75.ctx_ref.o_ref, bf16[2048,1024]{1,0:T(8,128)(2,1)} %bitcast.84, bf16[4,1024,1024]{2,1,0:T(8,128)(2,1)} %bitcast.69, f32[4,1024]{1,0:T(4,128)} %reshape.147.b_ref, f32[4,1024]{1,0:T(4,128)} %reshape.149.ln_ref), custom_call_target="tpu_custom_call" | custom-call | flops 4294967296 | bytes 18874368 | tf_op jit(solution)/shard_map/out_proj/pallas_call | solution.py:301
  170.9 58.4 %mlp.2 = (bf16[2048,4096]{1,0:T(8,128)(2,1)}, f32[2048,4096]{1,0:T(8,128)}, bf16[2048,1024]{1,0:T(8,128)(2,1)}) custom-call(bf16[2048,1024]{1,0:T(8,128)(2,1)} %get-tuple-element.76.h_ref.a_ref, bf16[2048,1024]{1,0:T(8,128)(2,1)} %get-tuple-element.77.mid_ref, bf16[1024,4096]{1,0:T(8,128)(2,1)} %bitcast.104, f32[1,4096]{1,0:T(1,128)} %bitcast.103, ...), custom_call_target="tpu_custom_call" | custom-call | flops 34359738368 | bytes 83886080 | tf_op jit(solution)/shard_map/mlp/pallas_call | solution.py:327
  229.4 20.3 %qkv.3 = (bf16[2048,1024]{1,0:T(8,128)(2,1)}, bf16[2048,1024]{1,0:T(8,128)(2,1)}, bf16[2048,1024]{1,0:T(8,128)(2,1)}, bf16[2048,1024]{1,0:T(8,128)(2,1)}) custom-call(bf16[2048,1024]{1,0:T(8,128)(2,1)} %get-tuple-element.79.x_ref, bf16[4,1024,1024]{2,1,0:T(8,128)(2,1)} %bitcast.72, f32[4,1024]{1,0:T(4,128)} %reshape.153.b_ref, f32[4,1024]{1,0:T(4,128)} %reshape.155.ln_ref, ...), custom_call_target="tpu_custom_call" | custom-call | flops 12884901888 | bytes 27262976 | tf_op jit(solution)/shard_map/qkv/pallas_call | solution.py:281
  249.7 76.3 %attn_fwd.3 = (bf16[2048,1024]{1,0:T(8,128)(2,1)}, bf16[2,16,1024,1024]{3,2,1,0:T(8,128)(2,1)}) custom-call(s32[2]{0:T(128)} %len_ref.3, bf16[2048,1024]{1,0:T(8,128)(2,1)} %get-tuple-element.81.q_ref, bf16[2048,1024]{1,0:T(8,128)(2,1)} %get-tuple-element.82.k_ref, bf16[2048,1024]{1,0:T(8,128)(2,1)} %get-tuple-element.83.v_ref), custom_call_target="tpu_custom_call" | custom-call | flops 34359738368 | bytes 94371840 | tf_op jit(solution)/shard_map/attn_fwd/pallas_call | solution.py:91
  326.0 11.6 %out_proj.3 = (bf16[2048,1024]{1,0:T(8,128)(2,1)}, bf16[2048,1024]{1,0:T(8,128)(2,1)}) custom-call(bf16[2048,1024]{1,0:T(8,128)(2,1)} %get-tuple-element.84.ctx_ref.o_ref, bf16[2048,1024]{1,0:T(8,128)(2,1)} %get-tuple-element.79.x_ref, bf16[4,1024,1024]{2,1,0:T(8,128)(2,1)} %bitcast.73, f32[4,1024]{1,0:T(4,128)} %reshape.153.b_ref, f32[4,1024]{1,0:T(4,128)} %reshape.155.ln_ref), custom_call_target="tpu_custom_call" | custom-call | flops 4294967296 | bytes 18874368 | tf_op jit(solution)/shard_map/out_proj/pallas_call | solution.py:301
  337.6 57.7 %mlp.3 = (bf16[2048,4096]{1,0:T(8,128)(2,1)}, f32[2048,4096]{1,0:T(8,128)}, bf16[2048,1024]{1,0:T(8,128)(2,1)}) custom-call(bf16[2048,1024]{1,0:T(8,128)(2,1)} %get-tuple-element.85.h_ref.a_ref, bf16[2048,1024]{1,0:T(8,128)(2,1)} %get-tuple-element.86.mid_ref, bf16[1024,4096]{1,0:T(8,128)(2,1)} %bitcast.108, f32[1,4096]{1,0:T(1,128)} %bitcast.102, ...), custom_call_target="tpu_custom_call" | custom-call | flops 34359738368 | bytes 83886080 | tf_op jit(solution)/shard_map/mlp/pallas_call | solution.py:327
  395.3 26.4 %down_grad.2.refs_0_ = bf16[8,256,1024]{2,1,0:T(8,128)(2,1)} custom-call(bf16[2048,4096]{1,0:T(8,128)(2,1)} %get-tuple-element.87.a_ref, bf16[2048,1024]{1,0:T(8,128)(2,1)} %bitcast.112), custom_call_target="tpu_custom_call" | custom-call | flops 17179869184 | bytes 29360128 | tf_op jit(solution)/shard_map/down_grad/pallas_call | solution.py:483
  421.7 76.4 %mlp_back.2 = (bf16[2048,4096]{1,0:T(8,128)(2,1)}, bf16[2048,1024]{1,0:T(8,128)(2,1)}, bf16[2048,1024]{1,0:T(8,128)(2,1)}, f32[8,4096]{1,0:T(8,128)}, f32[24,1024]{1,0:T(8,128)}, /*index=5*/bf16[8,256,1024]{2,1,0:T(8,128)(2,1)}) custom-call(bf16[2048,1024]{1,0:T(8,128)(2,1)} %bitcast.113, f32[2048,4096]{1,0:T(8,128)} %get-tuple-element.89.slope_ref, ...), custom_call_target="tpu_custom_call" | custom-call | flops 38654705664 | bytes 94371840 | tf_op jit(solution)/shard_map/mlp_back/pallas_call | solution.py:373
  498.1 26.4 %up_grad.2.refs_0_ = bf16[8,64,4096]{2,1,0:T(8,128)(2,1)} custom-call(bf16[2048,1024]{1,0:T(8,128)(2,1)} %get-tuple-element.85.h_ref.a_ref, bf16[2048,4096]{1,0:T(8,128)(2,1)} %get-tuple-element.91.b_ref), custom_call_target="tpu_custom_call" | custom-call | flops 17179869184 | bytes 29360128 | tf_op jit(solution)/shard_map/up_grad/pallas_call | solution.py:510
  524.5 83.9 %attn_bwd.2 = (bf16[2048,1024]{1,0:T(8,128)(2,1)}, bf16[2048,1024]{1,0:T(8,128)(2,1)}, bf16[2048,1024]{1,0:T(8,128)(2,1)}, bf16[8,64,4096]{2,1,0:T(8,128)(2,1)}) custom-call(bf16[2048,1024]{1,0:T(8,128)(2,1)} %get-tuple-element.81.q_ref, bf16[2048,1024]{1,0:T(8,128)(2,1)} %get-tuple-element.82.k_ref, bf16[2048,1024]{1,0:T(8,128)(2,1)} %get-tuple-element.83.v_ref, ...), custom_call_target="tpu_custom_call" | custom-call | flops 68719476736 | bytes 104857600 | tf_op jit(solution)/shard_map/attn_bwd/pallas_call | solution.py:146
  608.4 30.4 %attn_grad.2 = (bf16[8,4,64,1024]{3,2,1,0:T(8,128)(2,1)}, f32[32,1024]{1,0:T(8,128)}) custom-call(bf16[2048,1024]{1,0:T(8,128)(2,1)} %get-tuple-element.80.h_ref, bf16[2048,1024]{1,0:T(8,128)(2,1)} %get-tuple-element.84.ctx_ref.o_ref, bf16[2048,1024]{1,0:T(8,128)(2,1)} %get-tuple-element.101.dq_ref, bf16[2048,1024]{1,0:T(8,128)(2,1)} %get-tuple-element.97.dk_ref, ...), custom_call_target="tpu_custom_call" | custom-call | flops 17179869184 | bytes 33554432 | tf_op jit(solution)/shard_map/attn_grad/pallas_call | solution.py:539
  638.8 24.3 %in_back.2 = (bf16[2048,1024]{1,0:T(8,128)(2,1)}, f32[16,1024]{1,0:T(8,128)}) custom-call(bf16[2048,1024]{1,0:T(8,128)(2,1)} %get-tuple-element.101.dq_ref, bf16[2048,1024]{1,0:T(8,128)(2,1)} %get-tuple-element.97.dk_ref, bf16[2048,1024]{1,0:T(8,128)(2,1)} %get-tuple-element.98.dv_ref, bf16[4,1024,1024]{2,1,0:T(8,128)(2,1)} %bitcast.75, ...), custom_call_target="tpu_custom_call" | custom-call | flops 12884901888 | bytes 35651584 | tf_op jit(solution)/shard_map/in_back/pallas_call | solution.py:404
  663.1 26.4 %down_grad.3.refs_1_ = bf16[8,256,1024]{2,1,0:T(8,128)(2,1)} custom-call(bf16[2048,4096]{1,0:T(8,128)(2,1)} %get-tuple-element.78.a_ref, bf16[2048,1024]{1,0:T(8,128)(2,1)} %get-tuple-element.103.b_ref.dy_ref), custom_call_target="tpu_custom_call" | custom-call | flops 17179869184 | bytes 29360128 | tf_op jit(solution)/shard_map/down_grad/pallas_call | solution.py:483
  689.5 79.3 %mlp_back.3 = (bf16[2048,4096]{1,0:T(8,128)(2,1)}, bf16[2048,1024]{1,0:T(8,128)(2,1)}, bf16[2048,1024]{1,0:T(8,128)(2,1)}, f32[8,4096]{1,0:T(8,128)}, f32[24,102...) custom-call(bf16[2048,1024]{1,0:T(8,128)(2,1)} %get-tuple-element.103.b_ref.dy_ref, ...), custom_call_target="tpu_custom_call" | custom-call | flops 38654705664 | bytes 94371840 | tf_op jit(solution)/shard_map/mlp_back/pallas_call | solution.py:373
  770.0 3.0 convert_reduce_fusion.2
  773.0 26.4 %up_grad.3.refs_0_ = bf16[8,64,4096]{2,1,0:T(8,128)(2,1)} custom-call(bf16[2048,1024]{1,0:T(8,128)(2,1)} %get-tuple-element.76.h_ref.a_ref, bf16[2048,4096]{1,0:T(8,128)(2,1)} %get-tuple-element.106.b_ref), custom_call_target="tpu_custom_call" | custom-call | flops 17179869184 | bytes 29360128 | tf_op jit(solution)/shard_map/up_grad/pallas_call | solution.py:510
  799.5 120.6 %attn_bwd.3 = (bf16[2048,1024]{1,0:T(8,128)(2,1)}, bf16[2048,1024]{1,0:T(8,128)(2,1)}, bf16[2048,1024]{1,0:T(8,128)(2,1)}, bf16[8,64,4096]{2,1,0:T(8,128)(2,1)}, bf16[8,256,1024]{2,1,0:T(8,128)(2,1)}) custom-call(bf16[2048,1024]{1,0:T(8,128)(2,1)} %get-tuple-element.72.q_ref, bf16[2048,1024]{1,0:T(8,128)(2,1)} %get-tuple-element.73.k_ref, ...), custom_call_target="tpu_custom_call" | custom-call | flops 68719476736 | bytes 104857600 | tf_op jit(solution)/shard_map/attn_bwd/pallas_call | solution.py:146
  923.1 30.2 %attn_grad.3 = (bf16[8,4,64,1024]{3,2,1,0:T(8,128)(2,1)}, f32[32,1024]{1,0:T(8,128)}) custom-call(bf16[2048,1024]{1,0:T(8,128)(2,1)} %get-tuple-element.71.h_ref, bf16[2048,1024]{1,0:T(8,128)(2,1)} %get-tuple-element.75.ctx_ref.o_ref, bf16[2048,1024]{1,0:T(8,128)(2,1)} %get-tuple-element.117.dq_ref, bf16[2048,1024]{1,0:T(8,128)(2,1)} %get-tuple-element.113.dk_ref, ...), custom_call_target="tpu_custom_call" | custom-call | flops 17179869184 | bytes 33554432 | tf_op jit(solution)/shard_map/attn_grad/pallas_call | solution.py:539
  953.4 74.4 %in_back.3 = (bf16[2048,1024]{1,0:T(8,128)(2,1)}, f32[16,1024]{1,0:T(8,128)}, bf16[8,4,64,1024]{3,2,1,0:T(8,128)(2,1)}) custom-call(bf16[2048,1024]{1,0:T(8,128)(2,1)} %get-tuple-element.117.dq_ref, bf16[2048,1024]{1,0:T(8,128)(2,1)} %get-tuple-element.113.dk_ref, bf16[2048,1024]{1,0:T(8,128)(2,1)} %get-tuple-element.114.dv_ref, ...), custom_call_target="tpu_custom_call" | custom-call | flops 12884901888 | bytes 35651584 | tf_op jit(solution)/shard_map/in_back/pallas_call | solution.py:404
  1030.3 3.3 convert_reduce_fusion.5
  1049.2 4.6 copy.70
  (166 shorter events, 49.8 us)
Async XLA Ops:
  7.2 55.8 %all-gather.13.cloned.1.call-start = ((), (), s32[]{:S(2)}) async-start(), calls=%async_computation | async-start | bytes 8912896 | tf_op jit(solution)/shard_map/all_gather | solution.py:628
  9.5 5.4 copy-start.15
  9.6 161.3 %all-gather.15.cloned.1.call-start = ((), (), s32[]{:S(2)}) async-start(), calls=%async_computation.1 | async-start | bytes 8912896 | tf_op jit(solution)/shard_map/all_gather | solution.py:629
  11.9 159.0 %all-gather.17.cloned.1.call-start = ((), (), s32[]{:S(2)}) async-start(), calls=%async_computation.2 | async-start | bytes 8912896 | tf_op jit(solution)/shard_map/all_gather | solution.py:630
  13.0 216.4 %all-gather.19.cloned.1.call-start = ((), (), s32[]{:S(2)}) async-start(), calls=%async_computation.3 | async-start | bytes 8912896 | tf_op jit(solution)/shard_map/all_gather | solution.py:628
  13.6 324.0 %all-gather.21.cloned.1.call-start = ((), (), s32[]{:S(2)}) async-start(), calls=%async_computation.4 | async-start | bytes 8912896 | tf_op jit(solution)/shard_map/all_gather | solution.py:629
  14.2 323.4 %all-gather.23.cloned.1.call-start = ((), (), s32[]{:S(2)}) async-start(), calls=%async_computation.5 | async-start | bytes 8912896 | tf_op jit(solution)/shard_map/all_gather | solution.py:630
  15.0 1.6 collective-permute-start
  16.6 4.5 collective-permute-start.1
  21.1 4.2 collective-permute-start.2
  25.3 4.0 collective-permute-start.3
  689.5 80.3 %copy-start.8 = (f32[24,1024]{1,0:T(8,128)S(1)}, f32[24,1024]{1,0:T(8,128)}, u32[]{:S(2)}) copy-start(f32[24,1024]{1,0:T(8,128)} %get-tuple-element.128) | copy-start | bytes 294916
  769.8 29.6 %copy-start.10 = (f32[3,1024]{1,0:T(4,128)}, f32[3,1024]{1,0:T(4,128)S(1)}, u32[]{:S(2)}) copy-start(f32[3,1024]{1,0:T(4,128)S(1)} %bitcast_reduce_fusion.3) | copy-start | bytes 36868
  769.9 29.5 %copy-start.11 = (f32[3,1024]{1,0:T(4,128)}, f32[3,1024]{1,0:T(4,128)S(1)}, u32[]{:S(2)}) copy-start(f32[3,1024]{1,0:T(4,128)S(1)} %bitcast_reduce_fusion.2) | copy-start | bytes 36868
  953.3 75.8 %slice-start = ((f32[3,1024]{1,0:T(4,128)}), f32[2,1024]{1,0:T(2,128)S(1)}, s32[]{:S(2)}) async-start(f32[3,1024]{1,0:T(4,128)} %copy-done.10), calls=%async_computation.6 | async-start | bytes 16384 | tf_op jit(solution)/shard_map/slice | solution.py:666
  953.4 76.0 %slice-start.1 = ((f32[3,1024]{1,0:T(4,128)}), f32[2,1024]{1,0:T(2,128)S(1)}, s32[]{:S(2)}) async-start(f32[3,1024]{1,0:T(4,128)} %copy-done.11), calls=%async_computation.7 | async-start | bytes 16384 | tf_op jit(solution)/shard_map/slice | solution.py:666
  953.4 76.2 %copy-start.7 = (f32[32,1024]{1,0:T(8,128)S(1)}, f32[32,1024]{1,0:T(8,128)}, u32[]{:S(2)}) copy-start(f32[32,1024]{1,0:T(8,128)} %get-tuple-element.122) | copy-start | bytes 393220
  953.4 76.4 %copy-start.6 = (f32[8,4096]{1,0:T(8,128)S(1)}, f32[8,4096]{1,0:T(8,128)}, u32[]{:S(2)}) copy-start(f32[8,4096]{1,0:T(8,128)} %get-tuple-element.125) | copy-start | bytes 393220
  953.4 76.4 %copy-start.4 = (f32[8,4096]{1,0:T(8,128)S(1)}, f32[8,4096]{1,0:T(8,128)}, u32[]{:S(2)}) copy-start(f32[8,4096]{1,0:T(8,128)} %get-tuple-element.129) | copy-start | bytes 393220
  953.4 76.5 %copy-start.5 = (f32[32,1024]{1,0:T(8,128)S(1)}, f32[32,1024]{1,0:T(8,128)}, u32[]{:S(2)}) copy-start(f32[32,1024]{1,0:T(8,128)} %get-tuple-element.126) | copy-start | bytes 393220
  1030.3 7.0 collective-permute-start.4
  1037.3 3.9 collective-permute-start.5
  1041.3 3.8 collective-permute-start.6
  1045.1 1.6 collective-permute-start.7
  (8 other events, 34.6 us)
Sparse Core Ops, SparseCore 0:
  10.8 52.1 all-gather.12
  65.2 49.0 all-gather.14
  116.5 48.9 all-gather.16
  168.3 49.0 all-gather.18
  219.5 49.0 all-gather.20
  270.6 49.0 all-gather.22

commit v5 on v4

--- a/solution.py
+++ b/solution.py
@@ -112,10 +112,10 @@
     return x * cos + other * (sin * sign)
 
 
-def attn_bwd_kernel(axis, units, last, q_ref, k_ref, v_ref, o_ref, do_ref, p_ref, cos_ref, sin_ref, *refs):
+def attn_bwd_kernel(axis, units, turns, q_ref, k_ref, v_ref, o_ref, do_ref, p_ref, cos_ref, sin_ref, *refs):
     pairs, (dq_ref, dk_ref, dv_ref), lands = refs[:units], refs[units:units + 3], refs[units + 3:2 * units + 3]
     doh_ref, qh_ref, kt_ref, d_ref, ds_ref, dqt_ref, *sems = refs[2 * units + 3:]
-    ride(axis, last, pl.program_id(0) * pl.num_programs(1) + pl.program_id(1), pairs, lands, *sems)
+    ride(axis, pl.program_id(0) * pl.num_programs(1) + pl.program_id(1), turns, pairs, lands, by_unit(sems, units))
     lane = lane_iota(1)
     for h in range(2):
         own = ((lane // HEAD_DIM) == h).astype(jnp.float32).astype(jnp.bfloat16)
@@ -144,13 +144,13 @@
     spec = pl.BlockSpec((SEQ, PAIR), lambda b, h: (b, h))
     table = pl.BlockSpec((SEQ, PAIR), lambda b, h: (0, 0))
     return pl.pallas_call(
-        functools.partial(attn_bwd_kernel, axis, len(units), seqs * pairs - 1), grid=(seqs, pairs),
+        functools.partial(attn_bwd_kernel, axis, len(units), (1, 8, 12, 14) if len(units) > 1 else (1, 6, 9, 11)), grid=(seqs, pairs),
         in_specs=[spec] * 5 + [pl.BlockSpec((None, 2, SEQ, SEQ), lambda b, h: (b, h, 0, 0)), table, table] + ride_specs(units),
         out_specs=[spec] * 3 + ride_specs(units),
         scratch_shapes=[pltpu.VMEM((2, SEQ, PAIR), jnp.bfloat16), pltpu.VMEM((2, SEQ, PAIR), jnp.bfloat16),
                         pltpu.VMEM((PAIR, SEQ), jnp.bfloat16), pltpu.VMEM((8, SEQ), jnp.float32),
-                        pltpu.VMEM((2, SEQ, SEQ), jnp.bfloat16), pltpu.VMEM((PAIR, SEQ), jnp.float32)] + ride_scratch(len(units)),
-        out_shape=[jax.ShapeDtypeStruct((tokens, width), jnp.bfloat16)] * 3 + same(units),
+                        pltpu.VMEM((2, SEQ, SEQ), jnp.bfloat16), pltpu.VMEM((PAIR, SEQ), jnp.float32)] + ride_scratch(units),
+        out_shape=[jax.ShapeDtypeStruct((tokens, width), jnp.bfloat16)] * 3 + sums(units),
         compiler_params=ride_params(number, 'arbitrary', 'arbitrary'),
         cost_estimate=pl.CostEstimate(flops=8 * tokens * SEQ * width * 4, bytes_accessed=100 << 20, transcendentals=0),
         name='attn_bwd',
@@ -204,55 +204,142 @@
     return jnp.sum(x.reshape(x.shape[0] // 8, 8, x.shape[1]), axis=0)
 
 
-def ride(axis, last, step, pairs, lands, send_sem, recv_sem, own_sem):
+ORDERS = ((1, 2, 4), (2, 4, 1), (4, 1, 2))
+
+
+def thirds(width):
+    tiles = width // 128
+    cuts = [0, (tiles + 2) // 3, (2 * tiles + 2) // 3, tiles]
+    return [(128 * lo, 128 * hi) for lo, hi in zip(cuts, cuts[1:])]
+
+
+def ride(axis, step, turns, pair_refs, sum_refs, scratch):
     me = lax.axis_index(axis)
     side, chip = me % 2, me // 2
-    chips = pairs[0].shape[0]
-
-    def peer(j):
-        return ((chip + j) % chips) * 2 + side
-
-    def copies():
-        made = []
-        for u, (pair, land) in enumerate(zip(pairs, lands)):
-            for j in range(1, chips):
-                made.append(pltpu.make_async_remote_copy(
-                    src_ref=pair.at[(chip + j) % chips], dst_ref=land.at[chip], send_sem=send_sem.at[u, j], recv_sem=recv_sem.at[u, j],
-                    device_id=(peer(j),), device_id_type=MESH))
-            made.append(pltpu.make_async_copy(pair.at[chip], land.at[chip], own_sem.at[u]))
-        return made
+    units = len(pair_refs)
+
+    def bit(weight):
+        return (chip // weight) % 2
+
+    def beside(weight):
+        return (chip + weight - 2 * weight * bit(weight)) * 2 + side
+
+    def send(u, o, j, source, target, weight):
+        sems = scratch[u][-2:]
+        return pltpu.make_async_remote_copy(
+            src_ref=source, dst_ref=target, send_sem=sems[0].at[o, j], recv_sem=sems[1].at[o, j],
+            device_id=(beside(weight),), device_id_type=MESH)
+
+    def lanes(u, o):
+        lo, hi = thirds(pair_refs[u].shape[2])[o]
+        return slice(lo, hi)
+
+    def fetch(u):
+        return pltpu.make_async_copy(pair_refs[u], scratch[u][0], scratch[u][-3].at[0])
+
+    def store(u):
+        return pltpu.make_async_copy(scratch[u][7], sum_refs[u], scratch[u][-3].at[0])
+
+    def first(u, o):
+        mine, in_one = scratch[u][0], scratch[u][1]
+        w, cols = ORDERS[o], lanes(u, o)
+        return [send(u, o, 2 * i + j, mine.at[(1 - bit(w[0])) * w[0] + i * w[1] + j * w[2], :, cols], in_one.at[2 * i + j, :, cols], w[0])
+                for i in range(2) for j in range(2)]
+
+    def second(u, o):
+        w, cols = ORDERS[o], lanes(u, o)
+        return [send(u, o, 4 + j, scratch[u][5].at[j, :, cols], scratch[u][2].at[j, :, cols], w[1]) for j in range(2)]
+
+    def third(u, o):
+        w, cols = ORDERS[o], lanes(u, o)
+        return [send(u, o, 6, scratch[u][6].at[:, cols], scratch[u][3].at[:, cols], w[2])]
+
+    each = [(u, o) for u in range(units) for o in range(3)]
 
     @pl.when(step == 0)
     def _():
+        for u in range(units):
+            fetch(u).start()
         barrier = pltpu.get_barrier_semaphore()
-        for j in range(1, chips):
-            pl.semaphore_signal(barrier, inc=1, device_id=(peer(j),), device_id_type=MESH)
-
-    @pl.when(step == 1)
-    def _():
-        pl.semaphore_wait(pltpu.get_barrier_semaphore(), chips - 1)
-        for c in copies():
-            c.start()
-
-    @pl.when(step == last)
-    def _():
-        for c in copies():
-            c.wait()
+        for w in ORDERS[0]:
+            pl.semaphore_signal(barrier, inc=1, device_id=(beside(w),), device_id_type=MESH)
+
+    @pl.when(step == turns[0])
+    def _():
+        for u in range(units):
+            fetch(u).wait()
+        pl.semaphore_wait(pltpu.get_barrier_semaphore(), 3)
+        for u, o in each:
+            for c in first(u, o):
+                c.start()
+
+    @pl.when(step == turns[1])
+    def _():
+        for u, o in each:
+            mine, in_one, _, _, kept, out_two = scratch[u][:6]
+            w, cols = ORDERS[o], lanes(u, o)
+            for c in first(u, o):
+                c.wait()
+            stay = bit(w[1])
+            for j in range(2):
+                base = bit(w[0]) * w[0] + j * w[2]
+                kept[j, :, cols] = mine[base + stay * w[1], :, cols].astype(jnp.float32) + in_one[2 * stay + j, :, cols].astype(jnp.float32)
+                out_two[j, :, cols] = (mine[base + (1 - stay) * w[1], :, cols].astype(jnp.float32)
+                                       + in_one[2 * (1 - stay) + j, :, cols].astype(jnp.float32)).astype(jnp.bfloat16)
+            for c in second(u, o):
+                c.start()
+
+    @pl.when(step == turns[2])
+    def _():
+        for u, o in each:
+            _, _, in_two, _, kept, _, out_three, final = scratch[u][:8]
+            w, cols = ORDERS[o], lanes(u, o)
+            for c in second(u, o):
+                c.wait()
+            stay = bit(w[2])
+            final[:, cols] = kept[stay, :, cols] + in_two[stay, :, cols].astype(jnp.float32)
+            out_three[:, cols] = (kept[1 - stay, :, cols] + in_two[1 - stay, :, cols].astype(jnp.float32)).astype(jnp.bfloat16)
+            for c in third(u, o):
+                c.start()
+
+    @pl.when(step == turns[3])
+    def _():
+        for u, o in each:
+            in_three, final = scratch[u][3], scratch[u][7]
+            cols = lanes(u, o)
+            for c in third(u, o):
+                c.wait()
+            final[:, cols] += in_three[:, cols].astype(jnp.float32)
+        for u in range(units):
+            store(u).start()
+        for u in range(units):
+            store(u).wait()
 
 
 MESH = pl.DeviceIdType.MESH
 
 
-def ride_scratch(units):
-    return [pltpu.SemaphoreType.DMA((units, 8)), pltpu.SemaphoreType.DMA((units, 8)), pltpu.SemaphoreType.DMA((units,))]
+def ride_scratch(pairs):
+    made = []
+    for p in pairs:
+        chips, rows, width = p.shape
+        half = lambda *lead: pltpu.VMEM(lead + (rows, width), jnp.bfloat16)
+        full = lambda *lead: pltpu.VMEM(lead + (rows, width), jnp.float32)
+        made += [half(chips), half(4), half(2), half(), full(2), half(2), half(), full(),
+                 pltpu.SemaphoreType.DMA((1,)), pltpu.SemaphoreType.DMA((3, 7)), pltpu.SemaphoreType.DMA((3, 7))]
+    return made
+
+
+def by_unit(refs, units):
+    return [refs[11 * u:11 * u + 11] for u in range(units)]
 
 
 def ride_specs(pairs):
     return [pl.BlockSpec(memory_space=pl.ANY)] * len(pairs)
 
 
-def same(pairs):
-    return [jax.ShapeDtypeStruct(p.shape, p.dtype) for p in pairs]
+def sums(pairs):
+    return [jax.ShapeDtypeStruct(p.shape[1:], jnp.float32) for p in pairs]
 
 
 def ride_params(number, *semantics):
@@ -334,9 +421,9 @@
     )(h, mid, wu, bu, wd, bd)
 
 
-def mlp_back_kernel(axis, units, last, dy_ref, slope_ref, wd_ref, wu_ref, mid_ref, ln_ref, wo_ref, *refs):
+def mlp_back_kernel(axis, units, turns, dy_ref, slope_ref, wd_ref, wu_ref, mid_ref, ln_ref, wo_ref, *refs):
     pairs, (dpre_ref, dmid_ref, dctx_ref, gbu_ref, gln_ref), lands, sems = refs[:units], refs[units:units + 5], refs[units + 5:2 * units + 5], refs[2 * units + 5:]
-    ride(axis, last, pl.program_id(0), pairs, lands, *sems)
+    ride(axis, pl.program_id(0), turns, pairs, lands, by_unit(sems, units))
     dy = dy_ref[...]
     grad = None
     wide = wu_ref.shape[1]
@@ -371,20 +458,20 @@
     row, long = rows_of(block, width), rows_of(block, wide)
     half = jax.ShapeDtypeStruct(dy.shape, jnp.bfloat16)
     return pl.pallas_call(
-        functools.partial(mlp_back_kernel, axis, len(pairs), tokens // block - 1), grid=(tokens // block,),
+        functools.partial(mlp_back_kernel, axis, len(pairs), (1, 4, 6, 7)), grid=(tokens // block,),
         in_specs=[row, long, whole(wd.shape), whole(wu.shape), row, whole(ln.shape), part_of((None, width, width), 3, 0, 0)] + ride_specs(pairs),
         out_specs=[long, row, row, partial((8, wide)), partial((24, width))] + ride_specs(pairs),
         out_shape=[jax.ShapeDtypeStruct((tokens, wide), jnp.bfloat16), half, half,
-                   jax.ShapeDtypeStruct((8, wide), jnp.float32), jax.ShapeDtypeStruct((24, width), jnp.float32)] + same(pairs),
-        scratch_shapes=ride_scratch(len(pairs)),
+                   jax.ShapeDtypeStruct((8, wide), jnp.float32), jax.ShapeDtypeStruct((24, width), jnp.float32)] + sums(pairs),
+        scratch_shapes=ride_scratch(pairs),
         compiler_params=ride_params(number), cost_estimate=cost(2 * tokens * width * (2 * wide + width), 90 << 20), name='mlp_back',
     )(dy, slope, wd, wu, mid, ln, wo, *pairs)
 
 
-def in_back_kernel(axis, units, last, dq_ref, dk_ref, dv_ref, w_ref, x_ref, ln_ref, dmid_ref, *refs):
+def in_back_kernel(axis, units, turns, dq_ref, dk_ref, dv_ref, w_ref, x_ref, ln_ref, dmid_ref, *refs):
     pairs, (dx_ref, gln_ref), lands, sems = refs[:units], refs[units:units + 2], refs[units + 2:2 * units + 2], refs[2 * units + 2:]
     if units:
-        ride(axis, last, pl.program_id(0), pairs, lands, *sems)
+        ride(axis, pl.program_id(0), turns, pairs, lands, by_unit(sems, units))
 
     @pl.when(pl.program_id(0) == 0)
     def _():
@@ -399,14 +486,14 @@
 
 def in_back(axis, number, pairs, dq, dk, dv, w, x, ln, dmid):
     tokens, width = x.shape
-    block = 512
+    block = 256
     row = rows_of(block, width)
     return pl.pallas_call(
-        functools.partial(in_back_kernel, axis, len(pairs), tokens // block - 1), grid=(tokens // block,),
+        functools.partial(in_back_kernel, axis, len(pairs), (1, 6, 7, 7)), grid=(tokens // block,),
         in_specs=[row, row, row, part_of((3, width, width), 0, 0, 0), row, whole(ln.shape), row] + ride_specs(pairs),
         out_specs=[row, partial((16, width))] + ride_specs(pairs),
-        out_shape=[jax.ShapeDtypeStruct(x.shape, jnp.bfloat16), jax.ShapeDtypeStruct((16, width), jnp.float32)] + same(pairs),
-        scratch_shapes=ride_scratch(len(pairs)) if pairs else [],
+        out_shape=[jax.ShapeDtypeStruct(x.shape, jnp.bfloat16), jax.ShapeDtypeStruct((16, width), jnp.float32)] + sums(pairs),
+        scratch_shapes=ride_scratch(pairs) if pairs else [],
         compiler_params=ride_params(number) if pairs else params(), cost_estimate=cost(6 * tokens * width * width, 34 << 20), name='in_back',
     )(dq, dk, dv, w, x, ln, dmid, *pairs)
 
@@ -519,12 +606,12 @@
 
 def attn_grad_kernel(axis, steps, h_ref, ctx_ref, dq_ref, dk_ref, dv_ref, dmid_ref, out_ref, gb_ref, *scratch):
     def make(put):
-        chips, half = out_ref.shape[0], out_ref.shape[2]
+        chips, half = out_ref.shape[0], out_ref.shape[1] // 4
         for j, d_ref in enumerate((dq_ref, dk_ref, dv_ref, dmid_ref)):
             grad = dot((h_ref if j < 3 else ctx_ref)[...], d_ref[...], TN)
             for c in range(chips):
                 r = 2 * c * half
-                put((c, j), grad[r:r + half], grad[r + half:r + 2 * half])
+                put((c, slice(j * half, (j + 1) * half)), grad[r:r + half], grad[r + half:r + 2 * half])
             gb_ref[8 * j:8 * j + 8] = eights(d_ref[...].astype(jnp.float32))
 
     swap_step(axis, steps, make, *scratch, out_ref)
@@ -539,12 +626,43 @@
     return pl.pallas_call(
         functools.partial(attn_grad_kernel, axis, steps), grid=(steps + 2,),
         in_specs=[whole(h.shape), whole(ctx.shape), cols, cols, cols, cols],
-        out_specs=[pl.BlockSpec((chips, 4, half, block), lambda i: (0, 0, 0, jnp.maximum(i - 2, 0))),
+        out_specs=[pl.BlockSpec((chips, 4 * half, block), lambda i: (0, 0, jnp.maximum(i - 2, 0))),
                    pl.BlockSpec((32, block), lambda i: (0, jnp.minimum(i, steps - 1)))],
-        out_shape=[jax.ShapeDtypeStruct((chips, 4, half, width), jnp.bfloat16), jax.ShapeDtypeStruct((32, width), jnp.float32)],
-        scratch_shapes=swap_scratch(steps, (chips, 4, half, block)),
+        out_shape=[jax.ShapeDtypeStruct((chips, 4 * half, width), jnp.bfloat16), jax.ShapeDtypeStruct((32, width), jnp.float32)],
+        scratch_shapes=swap_scratch(steps, (chips, 4 * half, block)),
         compiler_params=swap_params(number), cost_estimate=cost(8 * tokens * width * width, 32 << 20), name='attn_grad',
     )(h, ctx, dq, dk, dv, dmid)
+
+
+def small_kernel(axis, in_ref, out_ref, land_ref, send_sem, recv_sem):
+    me = lax.axis_index(axis)
+    count = in_ref.shape[0]
+    barrier = pltpu.get_barrier_semaphore()
+    for j in range(1, count):
+        pl.semaphore_signal(barrier, inc=1, device_id=((me + j) % count,), device_id_type=MESH)
+    pl.semaphore_wait(barrier, count - 1)
+    copies = [pltpu.make_async_remote_copy(
+        src_ref=in_ref.at[(me + j) % count], dst_ref=land_ref.at[j], send_sem=send_sem.at[j], recv_sem=recv_sem.at[j],
+        device_id=((me + j) % count,), device_id_type=MESH) for j in range(1, count)]
+    for c in copies:
+        c.start()
+    total = in_ref[me]
+    for c in copies:
+        c.wait()
+    for j in range(1, count):
+        total = total + land_ref[j]
+    out_ref[...] = total
+
+
+def small_sums(axis, number, packed):
+    count = packed.shape[0]
+    return pl.pallas_call(
+        functools.partial(small_kernel, axis),
+        in_specs=[pl.BlockSpec(memory_space=pltpu.VMEM)], out_specs=pl.BlockSpec(memory_space=pltpu.VMEM),
+        out_shape=jax.ShapeDtypeStruct(packed.shape[1:], jnp.float32),
+        scratch_shapes=[pltpu.VMEM(packed.shape, jnp.float32), pltpu.SemaphoreType.DMA((count,)), pltpu.SemaphoreType.DMA((count,))],
+        compiler_params=pltpu.CompilerParams(collective_id=number, has_side_effects=True), name='small_sums',
+    )(packed)
 
 
 def rotary_tables():
@@ -573,18 +691,6 @@
         mine = bit_of(axis_name, dim)
         held = jnp.where(mine == 0, jnp.concatenate([held, got]), jnp.concatenate([got, held]))
     return held
-
-
-def scatter_packed(full, axis_name):
-    cur = full
-    for dim in ('z', 'y', 'x', 'c'):
-        mine = bit_of(axis_name, dim)
-        half = cur.shape[0] // 2
-        low, high = cur[:half], cur[half:]
-        give = jnp.where(mine == 0, high, low)
-        keep = jnp.where(mine == 0, low, high)
-        cur = keep + swap(give, axis_name, dim)
-    return cur[0]
 
 
 def pack_params(b_attn, ln_par, b_up, b_down):
@@ -616,9 +722,6 @@
         cos, sin = rotary_tables()
         gather = functools.partial(lax.all_gather, axis_name=axis_name, tiled=True)
         after = lax.optimization_barrier
-
-        def total(parts):
-            return jnp.sum(parts.astype(jnp.float32), axis=0)
 
         small = gather_packed(pack_params(b_attn, ln_par, b_up, b_down), axis_name)
         hidden = x.reshape(tokens, width)
@@ -644,19 +747,19 @@
             carried = [pair_down] if l + 1 == layers else [waiting]
             d_pre, d_mid, d_ctx, gb_up, gln_two, landed = mlp_back(axis_name, number + 1, carried, grad, slope, wd, wu, mid, ln, wa)
             if l + 1 == layers:
-                g_down, carried = total(landed), []
+                g_down, carried = landed, []
             else:
-                grads[l + 1][0], carried = total(landed), [pair_down]
+                grads[l + 1][0], carried = landed, [pair_down]
             pair_up, d_ctx = after((up_grad(axis_name, number + 2, h_two, d_pre), d_ctx))
             dq, dk, dv, landed, *rest = attn_bwd(axis_name, number + 3, [pair_up] + carried, q, k, v, ctx, d_ctx, probs, cos, sin)
-            g_up = total(landed)
+            g_up = landed
             if rest:
-                g_down = total(rest[0])
+                g_down = rest[0]
             waiting, gb_attn = attn_grad(axis_name, number + 4, h_one, ctx, dq, dk, dv, d_mid)
             waiting, dq = after((waiting, dq))
             carried = [waiting] if l == 0 else []
             grad, gln_one, *rest = in_back(axis_name, number + 5, carried, dq, dk, dv, wa, x_in, ln, d_mid)
-            g_attn = total(rest[0]) if rest else None
+            g_attn = rest[0] if rest else None
             number += 6
             sums_two = jnp.sum(gln_two.reshape(3, 8, width), axis=1)
             sums_one = jnp.sum(gln_one.reshape(2, 8, width), axis=1)
@@ -666,7 +769,9 @@
             packed = jnp.concatenate([by_dev(gb_four), by_dev(sums_one), by_dev(sums_two[:2]),
                                       gb_wide.reshape(16, nu), by_dev(sums_two[2:3])], axis=1)
             grads[l] = [g_attn, g_up, g_down, packed]
-        got = scatter_packed(jnp.stack([g[3] for g in grads], axis=1), axis_name)
+        got = small_sums(axis_name, number, jnp.stack([jnp.pad(g[3], ((0, 0), (0, 64))) for g in grads], axis=1))[:, :832]
+        for g in grads:
+            g[0] = g[0].reshape(4, -1, width)
         g_attn, g_up, g_down = (jnp.stack([g[i] for g in grads]) for i in range(3))
         return (grad.reshape(x.shape), g_attn, got[:, :4 * n].reshape(layers, 4, n), got[:, 4 * n:8 * n].reshape(layers, 4, n),
                 g_up, got[:, 8 * n:8 * n + nu], g_down, got[:, 8 * n + nu:])

time: 1070 us -> 990 us (0.925)
  Pallas kernels: 957 us -> 867 us
  local copies, waits for them, and re-layouts: 21 us -> 42.6 us
    pallas_call x6 -> x7, Pallas kernels: 459 us -> 369 us  [the longest x2 170 us: attn_bwd(): pl.pallas_call(functools.partial(attn_bwd_kernel, axis, len(units), (1, 8...]
    reduce_sum x6 -> x0, other arithmetic: 11.9 us -> none  [total(): return jnp.sum(parts.astype(jnp.float32), axis=0)]
  transfers between devices with their start and end apart: 14 -> 10, of which waited for: 6 -> 4; matrix products, arithmetic and copies ran while one was open for 2% -> 1% of each run, Pallas kernels for 26% -> 28%
where the time goes in v5:
time: 990 us; the launch traced here: 980 us
  Pallas kernels  867 us (88%)
  local copies, waits for them, and re-layouts  42.6 us (4%)
  waiting for transfers between devices  31.9 us (3%)
  other arithmetic  15.5 us (2%)
  between operations  14.7 us (1%)
    pallas_call x2, Pallas kernels, attn_bwd(): pl.pallas_call(functools.partial(attn_bwd_kernel, axis, len(units), (1, 8...  170 us
    pallas_call x2, Pallas kernels, attn_fwd(): pl.pallas_call(attn_fwd_kernel, grid_spec=pltpu.PrefetchScalarGridSpec(nu...  152 us
    pallas_call x2, Pallas kernels, mlp_back(): pl.pallas_call(functools.partial(mlp_back_kernel, axis, len(pairs), (1, 4...  121 us
    pallas_call x2, Pallas kernels, mlp(): pl.pallas_call(mlp_kernel, grid=(tokens // block,), in_specs=[row, row, w...  117 us
    pallas_call x2, Pallas kernels, in_back(): pl.pallas_call(functools.partial(in_back_kernel, axis, len(pairs), (1, 6,...  69.5 us
    pallas_call x2, Pallas kernels, attn_grad(): pl.pallas_call(functools.partial(attn_grad_kernel, axis, steps), grid=(st...  60.7 us
    pallas_call x2, Pallas kernels, up_grad(): pl.pallas_call(functools.partial(up_grad_kernel, axis, steps), grid=(step...  53.1 us
    pallas_call x2, Pallas kernels, down_grad(): pl.pallas_call(functools.partial(down_grad_kernel, axis, chips), grid=(ch...  52.7 us
  transfers between devices with their start and end apart: 10, of which 4 were waited for; matrix products, arithmetic and copies ran while one was open for 1% of the time, Pallas kernels for 28%

profile of v5, /device:TPU:0, one launch (start us, length us, event | category | flops | bytes accessed | tf_op | source)
XLA Modules:
  0.0 980.3 jit_solution(10581074098726336887)
XLA Ops:
  16.6 2.9 collective-permute-start.1
  35.3 27.7 %all-gather.13.cloned.1.call-done = bf16[1,4,1024,1024]{3,2,1,0:T(8,128)(2,1)} async-done(((bf16[1,4,64,1024]{3,2,1,0:T(8,128)(2,1)}), bf16[1,4,1024,1024]{3,2,1,0:T(8,128)(2,1)}) %all-gather.13.cloned.1.call-update) | async-done | bytes 8388624 | tf_op jit(solution)/shard_map/all_gather | solution.py:731
  63.0 20.2 %qkv.2 = (bf16[2048,1024]{1,0:T(8,128)(2,1)}, bf16[2048,1024]{1,0:T(8,128)(2,1)}, bf16[2048,1024]{1,0:T(8,128)(2,1)}, bf16[2048,1024]{1,0:T(8,128)(2,1)}) custom-call(bf16[2048,1024]{1,0:T(8,128)(2,1)} %bitcast.72, bf16[4,1024,1024]{2,1,0:T(8,128)(2,1)} %bitcast.63, f32[4,1024]{1,0:T(4,128)} %reshape.147.b_ref, f32[4,1024]{1,0:T(4,128)} %reshape.149.ln_ref, ...), custom_call_target="tpu_custom_call" | custom-call | flops 12884901888 | bytes 27262976 | tf_op jit(solution)/shard_map/qkv/pallas_call | solution.py:368
  83.3 76.3 %attn_fwd.2 = (bf16[2048,1024]{1,0:T(8,128)(2,1)}, bf16[2,16,1024,1024]{3,2,1,0:T(8,128)(2,1)}) custom-call(s32[2]{0:T(128)} %len_ref.3, bf16[2048,1024]{1,0:T(8,128)(2,1)} %get-tuple-element.72.q_ref, bf16[2048,1024]{1,0:T(8,128)(2,1)} %get-tuple-element.73.k_ref, bf16[2048,1024]{1,0:T(8,128)(2,1)} %get-tuple-element.74.v_ref), custom_call_target="tpu_custom_call" | custom-call | flops 34359738368 | bytes 94371840 | tf_op jit(solution)/shard_map/attn_fwd/pallas_call | solution.py:91
  159.5 11.3 %out_proj.2 = (bf16[2048,1024]{1,0:T(8,128)(2,1)}, bf16[2048,1024]{1,0:T(8,128)(2,1)}) custom-call(bf16[2048,1024]{1,0:T(8,128)(2,1)} %get-tuple-element.75.ctx_ref.o_ref, bf16[2048,1024]{1,0:T(8,128)(2,1)} %bitcast.73, bf16[4,1024,1024]{2,1,0:T(8,128)(2,1)} %bitcast.64, f32[4,1024]{1,0:T(4,128)} %reshape.147.b_ref, f32[4,1024]{1,0:T(4,128)} %reshape.149.ln_ref), custom_call_target="tpu_custom_call" | custom-call | flops 4294967296 | bytes 18874368 | tf_op jit(solution)/shard_map/out_proj/pallas_call | solution.py:388
  170.9 58.8 %mlp.2 = (bf16[2048,4096]{1,0:T(8,128)(2,1)}, f32[2048,4096]{1,0:T(8,128)}, bf16[2048,1024]{1,0:T(8,128)(2,1)}) custom-call(bf16[2048,1024]{1,0:T(8,128)(2,1)} %get-tuple-element.76.h_ref.a_ref, bf16[2048,1024]{1,0:T(8,128)(2,1)} %get-tuple-element.77.mid_ref, bf16[1024,4096]{1,0:T(8,128)(2,1)} %bitcast.93, f32[1,4096]{1,0:T(1,128)} %bitcast.92, ...), custom_call_target="tpu_custom_call" | custom-call | flops 34359738368 | bytes 83886080 | tf_op jit(solution)/shard_map/mlp/pallas_call | solution.py:414
  229.7 20.4 %qkv.3 = (bf16[2048,1024]{1,0:T(8,128)(2,1)}, bf16[2048,1024]{1,0:T(8,128)(2,1)}, bf16[2048,1024]{1,0:T(8,128)(2,1)}, bf16[2048,1024]{1,0:T(8,128)(2,1)}) custom-call(bf16[2048,1024]{1,0:T(8,128)(2,1)} %get-tuple-element.79.x_ref, bf16[4,1024,1024]{2,1,0:T(8,128)(2,1)} %bitcast.67, f32[4,1024]{1,0:T(4,128)} %reshape.153.b_ref, f32[4,1024]{1,0:T(4,128)} %reshape.155.ln_ref, ...), custom_call_target="tpu_custom_call" | custom-call | flops 12884901888 | bytes 27262976 | tf_op jit(solution)/shard_map/qkv/pallas_call | solution.py:368
  250.1 76.2 %attn_fwd.3 = (bf16[2048,1024]{1,0:T(8,128)(2,1)}, bf16[2,16,1024,1024]{3,2,1,0:T(8,128)(2,1)}) custom-call(s32[2]{0:T(128)} %len_ref.3, bf16[2048,1024]{1,0:T(8,128)(2,1)} %get-tuple-element.81.q_ref, bf16[2048,1024]{1,0:T(8,128)(2,1)} %get-tuple-element.82.k_ref, bf16[2048,1024]{1,0:T(8,128)(2,1)} %get-tuple-element.83.v_ref), custom_call_target="tpu_custom_call" | custom-call | flops 34359738368 | bytes 94371840 | tf_op jit(solution)/shard_map/attn_fwd/pallas_call | solution.py:91
  326.4 11.4 %out_proj.3 = (bf16[2048,1024]{1,0:T(8,128)(2,1)}, bf16[2048,1024]{1,0:T(8,128)(2,1)}) custom-call(bf16[2048,1024]{1,0:T(8,128)(2,1)} %get-tuple-element.84.ctx_ref.o_ref, bf16[2048,1024]{1,0:T(8,128)(2,1)} %get-tuple-element.79.x_ref, bf16[4,1024,1024]{2,1,0:T(8,128)(2,1)} %bitcast.68, f32[4,1024]{1,0:T(4,128)} %reshape.153.b_ref, f32[4,1024]{1,0:T(4,128)} %reshape.155.ln_ref), custom_call_target="tpu_custom_call" | custom-call | flops 4294967296 | bytes 18874368 | tf_op jit(solution)/shard_map/out_proj/pallas_call | solution.py:388
  337.8 57.7 %mlp.3 = (bf16[2048,4096]{1,0:T(8,128)(2,1)}, f32[2048,4096]{1,0:T(8,128)}, bf16[2048,1024]{1,0:T(8,128)(2,1)}) custom-call(bf16[2048,1024]{1,0:T(8,128)(2,1)} %get-tuple-element.85.h_ref.a_ref, bf16[2048,1024]{1,0:T(8,128)(2,1)} %get-tuple-element.86.mid_ref, bf16[1024,4096]{1,0:T(8,128)(2,1)} %bitcast.97, f32[1,4096]{1,0:T(1,128)} %bitcast.91, ...), custom_call_target="tpu_custom_call" | custom-call | flops 34359738368 | bytes 83886080 | tf_op jit(solution)/shard_map/mlp/pallas_call | solution.py:414
  395.5 26.3 %down_grad.2.refs_0_ = bf16[8,256,1024]{2,1,0:T(8,128)(2,1)} custom-call(bf16[2048,4096]{1,0:T(8,128)(2,1)} %get-tuple-element.87.a_ref, bf16[2048,1024]{1,0:T(8,128)(2,1)} %bitcast.101), custom_call_target="tpu_custom_call" | custom-call | flops 17179869184 | bytes 29360128 | tf_op jit(solution)/shard_map/down_grad/pallas_call | solution.py:570
  421.9 61.1 %mlp_back.2 = (bf16[2048,4096]{1,0:T(8,128)(2,1)}, bf16[2048,1024]{1,0:T(8,128)(2,1)}, bf16[2048,1024]{1,0:T(8,128)(2,1)}, f32[8,4096]{1,0:T(8,128)}, f32[24,1024]{1,0:T(8,128)}, /*index=5*/f32[256,1024]{1,0:T(8,128)}) custom-call(bf16[2048,1024]{1,0:T(8,128)(2,1)} %bitcast.102, f32[2048,4096]{1,0:T(8,128)} %get-tuple-element.89.slope_ref, ...), custom_call_target="tpu_custom_call" | custom-call | flops 38654705664 | bytes 94371840 | tf_op jit(solution)/shard_map/mlp_back/pallas_call | solution.py:460
  483.0 26.4 %up_grad.2.refs_0_ = bf16[8,64,4096]{2,1,0:T(8,128)(2,1)} custom-call(bf16[2048,1024]{1,0:T(8,128)(2,1)} %get-tuple-element.85.h_ref.a_ref, bf16[2048,4096]{1,0:T(8,128)(2,1)} %get-tuple-element.91.b_ref), custom_call_target="tpu_custom_call" | custom-call | flops 17179869184 | bytes 29360128 | tf_op jit(solution)/shard_map/up_grad/pallas_call | solution.py:597
  509.3 84.4 %attn_bwd.2 = (bf16[2048,1024]{1,0:T(8,128)(2,1)}, bf16[2048,1024]{1,0:T(8,128)(2,1)}, bf16[2048,1024]{1,0:T(8,128)(2,1)}, f32[64,4096]{1,0:T(8,128)}) custom-call(bf16[2048,1024]{1,0:T(8,128)(2,1)} %get-tuple-element.81.q_ref, bf16[2048,1024]{1,0:T(8,128)(2,1)} %get-tuple-element.82.k_ref, bf16[2048,1024]{1,0:T(8,128)(2,1)} %get-tuple-element.83.v_ref, ...), custom_call_target="tpu_custom_call" | custom-call | flops 68719476736 | bytes 104857600 | tf_op jit(solution)/shard_map/attn_bwd/pallas_call | solution.py:146
  593.8 30.3 %attn_grad.2 = (bf16[8,256,1024]{2,1,0:T(8,128)(2,1)}, f32[32,1024]{1,0:T(8,128)}) custom-call(bf16[2048,1024]{1,0:T(8,128)(2,1)} %get-tuple-element.80.h_ref, bf16[2048,1024]{1,0:T(8,128)(2,1)} %get-tuple-element.84.ctx_ref.o_ref, bf16[2048,1024]{1,0:T(8,128)(2,1)} %get-tuple-element.101.dq_ref, bf16[2048,1024]{1,0:T(8,128)(2,1)} %get-tuple-element.97.dk_ref, ...), custom_call_target="tpu_custom_call" | custom-call | flops 17179869184 | bytes 33554432 | tf_op jit(solution)/shard_map/attn_grad/pallas_call | solution.py:626
  624.1 23.9 %in_back.2 = (bf16[2048,1024]{1,0:T(8,128)(2,1)}, f32[16,1024]{1,0:T(8,128)}) custom-call(bf16[2048,1024]{1,0:T(8,128)(2,1)} %get-tuple-element.101.dq_ref, bf16[2048,1024]{1,0:T(8,128)(2,1)} %get-tuple-element.97.dk_ref, bf16[2048,1024]{1,0:T(8,128)(2,1)} %get-tuple-element.98.dv_ref, bf16[4,1024,1024]{2,1,0:T(8,128)(2,1)} %bitcast.70, ...), custom_call_target="tpu_custom_call" | custom-call | flops 12884901888 | bytes 35651584 | tf_op jit(solution)/shard_map/in_back/pallas_call | solution.py:491
  648.0 26.3 %down_grad.3.refs_1_ = bf16[8,256,1024]{2,1,0:T(8,128)(2,1)} custom-call(bf16[2048,4096]{1,0:T(8,128)(2,1)} %get-tuple-element.78.a_ref, bf16[2048,1024]{1,0:T(8,128)(2,1)} %get-tuple-element.103.b_ref.dy_ref), custom_call_target="tpu_custom_call" | custom-call | flops 17179869184 | bytes 29360128 | tf_op jit(solution)/shard_map/down_grad/pallas_call | solution.py:570
  674.4 60.3 %mlp_back.3 = (bf16[2048,4096]{1,0:T(8,128)(2,1)}, bf16[2048,1024]{1,0:T(8,128)(2,1)}, bf16[2048,1024]{1,0:T(8,128)(2,1)}, f32[8,4096]{1,0:T(8,128)}, f32[24,1024]{1,0:T(8,128)}, /*index=5*/f32[256,1024]{1,0:T(8,128)}) custom-call(bf16[2048,1024]{1,0:T(8,128)(2,1)} %get-tuple-element.103.b_ref.dy_ref, f32[2048,4096]{1,0:T(8,128)} %get-tuple-element.104.slope_ref, ...), custom_call_target="tpu_custom_call" | custom-call | flops 38654705664 | bytes 94371840 | tf_op jit(solution)/shard_map/mlp_back/pallas_call | solution.py:460
  738.8 26.8 %up_grad.3.refs_0_ = bf16[8,64,4096]{2,1,0:T(8,128)(2,1)} custom-call(bf16[2048,1024]{1,0:T(8,128)(2,1)} %get-tuple-element.76.h_ref.a_ref, bf16[2048,4096]{1,0:T(8,128)(2,1)} %get-tuple-element.106.b_ref), custom_call_target="tpu_custom_call" | custom-call | flops 17179869184 | bytes 29360128 | tf_op jit(solution)/shard_map/up_grad/pallas_call | solution.py:597
  765.5 85.8 %attn_bwd.3 = (bf16[2048,1024]{1,0:T(8,128)(2,1)}, bf16[2048,1024]{1,0:T(8,128)(2,1)}, bf16[2048,1024]{1,0:T(8,128)(2,1)}, f32[64,4096]{1,0:T(8,128)}, f32[256,1024]{1,0:T(8,128)}) custom-call(bf16[2048,1024]{1,0:T(8,128)(2,1)} %get-tuple-element.72.q_ref, bf16[2048,1024]{1,0:T(8,128)(2,1)} %get-tuple-element.73.k_ref, ...), custom_call_target="tpu_custom_call" | custom-call | flops 68719476736 | bytes 104857600 | tf_op jit(solution)/shard_map/attn_bwd/pallas_call | solution.py:146
  851.4 30.4 %attn_grad.3 = (bf16[8,256,1024]{2,1,0:T(8,128)(2,1)}, f32[32,1024]{1,0:T(8,128)}) custom-call(bf16[2048,1024]{1,0:T(8,128)(2,1)} %get-tuple-element.71.h_ref, bf16[2048,1024]{1,0:T(8,128)(2,1)} %get-tuple-element.75.ctx_ref.o_ref, bf16[2048,1024]{1,0:T(8,128)(2,1)} %get-tuple-element.117.dq_ref, bf16[2048,1024]{1,0:T(8,128)(2,1)} %get-tuple-element.113.dk_ref, ...), custom_call_target="tpu_custom_call" | custom-call | flops 17179869184 | bytes 33554432 | tf_op jit(solution)/shard_map/attn_grad/pallas_call | solution.py:626
  881.8 45.6 %in_back.3 = (bf16[2048,1024]{1,0:T(8,128)(2,1)}, f32[16,1024]{1,0:T(8,128)}, f32[256,1024]{1,0:T(8,128)}) custom-call(bf16[2048,1024]{1,0:T(8,128)(2,1)} %get-tuple-element.117.dq_ref, bf16[2048,1024]{1,0:T(8,128)(2,1)} %get-tuple-element.113.dk_ref, bf16[2048,1024]{1,0:T(8,128)(2,1)} %get-tuple-element.114.dv_ref, bf16[4,1024,1024]{2,1,0:T(8,128)(2,1)} %bitcast.66, ...), custom_call_target="tpu_custom_call" | custom-call | flops 12884901888 | bytes 35651584 | tf_op jit(solution)/shard_map/in_back/pallas_call | solution.py:491
  953.5 7.3 small_sums.1
  964.6 2.8 pad_maximum_fusion.1
  (147 shorter events, 64.7 us)
Async XLA Ops:
  7.2 4.8 copy-start.1
  7.2 55.8 %all-gather.13.cloned.1.call-start = ((), (), s32[]{:S(2)}) async-start(), calls=%async_computation | async-start | bytes 8912896 | tf_op jit(solution)/shard_map/all_gather | solution.py:731
  9.5 5.3 copy-start.12
  9.5 5.4 copy-start.13
  9.5 5.5 copy-start.14
  9.5 5.5 copy-start.15
  9.6 161.3 %all-gather.15.cloned.1.call-start = ((), (), s32[]{:S(2)}) async-start(), calls=%async_computation.1 | async-start | bytes 8912896 | tf_op jit(solution)/shard_map/all_gather | solution.py:732
  11.9 159.0 %all-gather.17.cloned.1.call-start = ((), (), s32[]{:S(2)}) async-start(), calls=%async_computation.2 | async-start | bytes 8912896 | tf_op jit(solution)/shard_map/all_gather | solution.py:733
  13.1 216.6 %all-gather.19.cloned.1.call-start = ((), (), s32[]{:S(2)}) async-start(), calls=%async_computation.3 | async-start | bytes 8912896 | tf_op jit(solution)/shard_map/all_gather | solution.py:731
  13.7 324.1 %all-gather.21.cloned.1.call-start = ((), (), s32[]{:S(2)}) async-start(), calls=%async_computation.4 | async-start | bytes 8912896 | tf_op jit(solution)/shard_map/all_gather | solution.py:732
  14.2 323.6 %all-gather.23.cloned.1.call-start = ((), (), s32[]{:S(2)}) async-start(), calls=%async_computation.5 | async-start | bytes 8912896 | tf_op jit(solution)/shard_map/all_gather | solution.py:733
  15.0 1.6 collective-permute-start
  16.6 4.5 collective-permute-start.1
  21.1 4.2 collective-permute-start.2
  25.4 4.0 collective-permute-start.3
  674.4 62.5 %copy-start.10 = (f32[24,1024]{1,0:T(8,128)S(1)}, f32[24,1024]{1,0:T(8,128)}, u32[]{:S(2)}) copy-start(f32[24,1024]{1,0:T(8,128)} %get-tuple-element.128) | copy-start | bytes 294916
  674.4 63.8 %copy-start.11 = (f32[16,1024]{1,0:T(8,128)S(1)}, f32[16,1024]{1,0:T(8,128)}, u32[]{:S(2)}) copy-start(f32[16,1024]{1,0:T(8,128)} %get-tuple-element.127) | copy-start | bytes 196612
  881.7 65.0 %copy-start.9 = (f32[8,4096]{1,0:T(8,128)S(1)}, f32[8,4096]{1,0:T(8,128)}, u32[]{:S(2)}) copy-start(f32[8,4096]{1,0:T(8,128)} %get-tuple-element.125) | copy-start | bytes 393220
  881.8 66.3 %copy-start.8 = (f32[32,1024]{1,0:T(8,128)S(1)}, f32[32,1024]{1,0:T(8,128)}, u32[]{:S(2)}) copy-start(f32[32,1024]{1,0:T(8,128)} %get-tuple-element.126) | copy-start | bytes 393220
  881.8 66.6 %copy-start.7 = (f32[8,4096]{1,0:T(8,128)S(1)}, f32[8,4096]{1,0:T(8,128)}, u32[]{:S(2)}) copy-start(f32[8,4096]{1,0:T(8,128)} %get-tuple-element.129) | copy-start | bytes 393220
  881.8 82.8 %copy-start.3 = (f32[64,4096]{1,0:T(8,128)S(1)}, f32[64,4096]{1,0:T(8,128)}, u32[]{:S(2)}) copy-start(f32[64,4096]{1,0:T(8,128)} %get-tuple-element.131) | copy-start | bytes 3145732
  927.4 40.1 %copy-start.2 = (f32[256,1024]{1,0:T(8,128)S(1)}, f32[256,1024]{1,0:T(8,128)}, u32[]{:S(2)}) copy-start(f32[256,1024]{1,0:T(8,128)} %get-tuple-element.133) | copy-start | bytes 3145732
  927.4 40.1 %copy-start.5 = (f32[256,1024]{1,0:T(8,128)S(1)}, f32[256,1024]{1,0:T(8,128)}, u32[]{:S(2)}) copy-start(f32[256,1024]{1,0:T(8,128)} %get-tuple-element.132) | copy-start | bytes 3145732
  964.6 4.3 copy-start.6
  (2 other events, 8.0 us)
Sparse Core Ops, SparseCore 0:
  10.8 52.1 all-gather.12
  65.2 48.9 all-gather.14
  116.5 48.9 all-gather.16
  168.3 49.0 all-gather.18
  219.5 49.0 all-gather.20
  270.6 48.9 all-gather.22
